TPU v7x, 32 devices: a 4x4x1 block of a 4x4x8 slice. The times are simulated.
32 devices in a mesh: part: 1 (over z), tpa: 4 (over y), tpb: 8 (over x, core).
Axes of the slice: x: 4, y: 4, z: 1, core: 2. Of those that a mesh axis runs over, the one named last changes fastest.
The devices are a block of a 4x4x8 slice.
Arguments:
- x: bfloat16 [64, 1024, 2048], P(('part', 'tpb'))
- lengths: int32 [64], P(('part', 'tpb'))
- k_buf: bfloat16 [64, 1024, 4, 64], P(('part', 'tpb'), None, 'tpa')
- v_buf: bfloat16 [64, 1024, 4, 64], P(('part', 'tpb'), None, 'tpa')
- w_qkv: bfloat16 [2048, 2560], P('part', ('tpa', 'tpb'))
- w_o: bfloat16 [2048, 2048], P(('part', 'tpa', 'tpb'))
- w_gate_up: bfloat16 [2048, 11264], P('part', ('tpa', 'tpb'))
- w_down: bfloat16 [5632, 2048], P(('part', 'tpa', 'tpb'))
- g_attn: bfloat16 [2048], P('part')
- g_mlp: bfloat16 [2048], P('part')
Outputs:
- output 1: bfloat16 [64, 1024, 2048], P(('part', 'tpb'))
- output 2: bfloat16 [64, 1024, 4, 64], P(('part', 'tpb'), None, 'tpa')
- output 3: bfloat16 [64, 1024, 4, 64], P(('part', 'tpb'), None, 'tpa')
- output 4: bfloat16 [2048, 2048], P('part', 'tpa')
- output 5: bfloat16 [2048, 256], P('part', 'tpa')
- output 6: bfloat16 [2048, 256], P('part', 'tpa')
- output 7: bfloat16 [2048, 2048], P(('part', 'tpa'))
- output 8: bfloat16 [2048, 5632], P('part', 'tpa')
- output 9: bfloat16 [2048, 5632], P('part', 'tpa')
- output 10: bfloat16 [5632, 2048], P(('part', 'tpa'))
All inputs are finite; a program needn't handle non-finite values.
Results may differ from a plain program's by a relative error of at most 0.0142439.
Values are sent between devices in bfloat16 or wider.
A program may use at most 768 MiB of HBM per device.

v0:
```python
import math
import jax
import jax.numpy as jnp
from jax import lax
from jax.sharding import PartitionSpec as P

ROPE_BASE = 500000.0
ROPE_FACTOR = 8.0
LOW_FREQ = 1.0
HIGH_FREQ = 4.0
ORIG_CONTEXT = 8192.0
NORM_EPS = 1e-5
MASK_VALUE = -1e30


def rms_norm(x_in, gain_vec):
    x_wide = x_in.astype(jnp.float32)
    mean_sq = jnp.mean(x_wide * x_wide, axis=-1, keepdims=True)
    return (x_wide * lax.rsqrt(mean_sq + NORM_EPS) * gain_vec.astype(jnp.float32)).astype(jnp.bfloat16)


def rope_tables(seq_len, head_dim):
    exponent = jnp.arange(head_dim // 2, dtype=jnp.float32) * (2.0 / head_dim)
    inv_freq = 1.0 / jnp.power(ROPE_BASE, exponent)
    wavelen = 2.0 * math.pi / inv_freq
    smooth = (ORIG_CONTEXT / wavelen - LOW_FREQ) / (HIGH_FREQ - LOW_FREQ)
    blended = (1.0 - smooth) * inv_freq / ROPE_FACTOR + smooth * inv_freq
    rope_freq = jnp.where(wavelen < ORIG_CONTEXT / HIGH_FREQ, inv_freq, jnp.where(wavelen > ORIG_CONTEXT / LOW_FREQ, inv_freq / ROPE_FACTOR, blended))
    angles = jnp.arange(seq_len, dtype=jnp.float32)[:, None] * rope_freq[None, :]
    return jnp.cos(angles), jnp.sin(angles)


def apply_rope(vec_in, cos_tab, sin_tab):
    half_dim = vec_in.shape[-1] // 2
    first_half = vec_in[..., :half_dim]
    second_half = vec_in[..., half_dim:]
    return jnp.concatenate([first_half * cos_tab - second_half * sin_tab, second_half * cos_tab + first_half * sin_tab], axis=-1)


def split_weights(qkv_cols, gu_cols, kv_local, head_dim, n_tpb):
    model_dim = qkv_cols.shape[0]
    group_size = qkv_cols.shape[1] // (kv_local * head_dim) - 2
    packed = qkv_cols.reshape(model_dim, kv_local, group_size + 2, head_dim)
    w_query = packed[:, :, :group_size, :].reshape(model_dim, kv_local * group_size * head_dim)
    w_key = packed[:, :, group_size, :].reshape(model_dim, kv_local * head_dim)
    w_value = packed[:, :, group_size + 1, :].reshape(model_dim, kv_local * head_dim)
    ff_block = gu_cols.shape[1] // (2 * n_tpb)
    gu_view = gu_cols.reshape(model_dim, n_tpb, 2, ff_block)
    w_gate = gu_view[:, :, 0, :].reshape(model_dim, n_tpb * ff_block)
    w_up = gu_view[:, :, 1, :].reshape(model_dim, n_tpb * ff_block)
    return w_query, w_key, w_value, w_gate, w_up


def prefill(x_loc, len_loc, k_buf, v_buf, qkv_cols, o_rows, gu_cols, down_rows, g_attn, g_mlp, n_tpb):
    batch_loc, seq_len, model_dim = x_loc.shape
    kv_local = k_buf.shape[2]
    head_dim = k_buf.shape[3]
    group_size = qkv_cols.shape[1] // (kv_local * head_dim) - 2
    x_normed = rms_norm(x_loc, g_attn)
    qkv_act = jnp.einsum('bsd,dc->bsc', x_normed, qkv_cols, preferred_element_type=jnp.float32).astype(jnp.bfloat16)
    qkv_act = qkv_act.reshape(batch_loc, seq_len, kv_local, group_size + 2, head_dim)
    cos_tab, sin_tab = rope_tables(seq_len, head_dim)
    q_rot = apply_rope(qkv_act[:, :, :, :group_size, :].astype(jnp.float32), cos_tab[:, None, None, :], sin_tab[:, None, None, :]).astype(jnp.bfloat16)
    k_rot = apply_rope(qkv_act[:, :, :, group_size, :].astype(jnp.float32), cos_tab[:, None, :], sin_tab[:, None, :]).astype(jnp.bfloat16)
    values = qkv_act[:, :, :, group_size + 1, :]
    scores = jnp.einsum('bqkgd,bskd->bkgqs', q_rot, k_rot, preferred_element_type=jnp.float32) * head_dim ** -0.5
    positions = jnp.arange(seq_len)
    allowed = (positions[None, None, :] <= positions[None, :, None]) & (positions[None, None, :] < len_loc[:, None, None])
    scores = jnp.where(allowed[:, None, None], scores, MASK_VALUE)
    attn_prob = jax.nn.softmax(scores, axis=-1).astype(jnp.bfloat16)
    attn_out = jnp.einsum('bkgqs,bskd->bqkgd', attn_prob, values, preferred_element_type=jnp.float32).astype(jnp.bfloat16)
    attn_out = attn_out.reshape(batch_loc, seq_len, kv_local * group_size * head_dim)
    attn_part = jnp.einsum('bsh,hd->bsd', attn_out, o_rows, preferred_element_type=jnp.float32).astype(jnp.bfloat16)
    attn_sum = lax.psum(attn_part, 'tpa')
    hidden = (x_loc.astype(jnp.float32) + attn_sum.astype(jnp.float32)).astype(jnp.bfloat16)
    h_normed = rms_norm(hidden, g_mlp)
    ff_block = gu_cols.shape[1] // (2 * n_tpb)
    gu_act = jnp.einsum('bsd,dc->bsc', h_normed, gu_cols, preferred_element_type=jnp.float32).astype(jnp.bfloat16)
    gu_act = gu_act.reshape(batch_loc, seq_len, n_tpb, 2, ff_block)
    mid_act = (jax.nn.silu(gu_act[..., 0, :].astype(jnp.float32)) * gu_act[..., 1, :].astype(jnp.float32)).astype(jnp.bfloat16)
    mid_act = mid_act.reshape(batch_loc, seq_len, n_tpb * ff_block)
    mlp_part = jnp.einsum('bsf,fd->bsd', mid_act, down_rows, preferred_element_type=jnp.float32).astype(jnp.bfloat16)
    mlp_sum = lax.psum(mlp_part, 'tpa')
    layer_out = (hidden.astype(jnp.float32) + mlp_sum.astype(jnp.float32)).astype(jnp.bfloat16)
    valid_pos = (positions[None, :] < len_loc[:, None])[:, :, None, None]
    k_cache = jnp.where(valid_pos, k_rot, k_buf)
    v_cache = jnp.where(valid_pos, values, v_buf)
    return layer_out, k_cache, v_cache


def solution(mesh):
    n_tpb = mesh.shape['tpb']

    def local_step(x_loc, len_loc, k_buf, v_buf, w_qkv, w_o, w_gate_up, w_down, g_attn, g_mlp):
        qkv_cols = lax.all_gather(w_qkv, 'tpb', axis=1, tiled=True)
        o_rows = lax.all_gather(w_o, 'tpb', axis=0, tiled=True)
        gu_cols = lax.all_gather(w_gate_up, 'tpb', axis=1, tiled=True)
        down_rows = lax.all_gather(w_down, 'tpb', axis=0, tiled=True)
        w_query, w_key, w_value, w_gate, w_up = split_weights(qkv_cols, gu_cols, k_buf.shape[2], k_buf.shape[3], n_tpb)
        layer_out, k_cache, v_cache = prefill(x_loc, len_loc, k_buf, v_buf, qkv_cols, o_rows, gu_cols, down_rows, g_attn, g_mlp, n_tpb)
        return (layer_out, k_cache, v_cache, w_query, w_key, w_value, o_rows, w_gate, w_up, down_rows)

    batch_spec = P(('part', 'tpb'), None, None)
    len_spec = P(('part', 'tpb'))
    cache_spec = P(('part', 'tpb'), None, 'tpa', None)
    train_cols = P('part', ('tpa', 'tpb'))
    train_rows = P(('part', 'tpa', 'tpb'), None)
    gain_spec = P('part')
    gen_cols = P('part', 'tpa')
    gen_rows = P(('part', 'tpa'), None)
    return jax.shard_map(local_step, mesh=mesh, in_specs=(batch_spec, len_spec, cache_spec, cache_spec, train_cols, train_rows, train_cols, train_rows, gain_spec, gain_spec), out_specs=(batch_spec, cache_spec, cache_spec, gen_cols, gen_cols, gen_cols, gen_rows, gen_cols, gen_cols, gen_rows), check_vma=False)
```

profile of v0, /device:TPU:97, one launch (start us, length us, event | category | flops | bytes accessed | tf_op | source)
XLA Modules:
  0.0 1910.0 jit_solution(6309711133880017136)
XLA Ops:
  7.2 0.1 all-gather.5.cloned.1.call-start
  7.3 0.7 all-gather.5.cloned.1.call-update
  8.0 0.1 all-gather.7.cloned.1.call-start
  8.1 0.7 all-gather.7.cloned.1.call-update
  8.8 0.1 all-reduce.3.cloned.1.call-start
  8.9 0.3 iota_compare_fusion
  9.2 11.3 fusion.4
  20.6 0.5 fusion.52
  21.2 0.1 iota_compare_fusion.1
  21.2 0.6 copy-done.6
  21.8 5.5 broadcast_and_fusion
  27.3 10.2 all-gather.5.cloned.1.call-done
  37.5 27.3 %fusion.36 = bf16[8,1024,640]{1,2,0:T(8,128)(2,1)S(1)} fusion(bf16[8,1024,2048]{2,1,0:T(8,128)(2,1)} %param.10, f32[2048]{0:T(1024)S(1)} %convert_element_type.106, f32[8,1024]{1,0:T(8,128)S(1)} %add_rsqrt_fusion.1, bf16[2048,640]{0,1:T(8,128)(2,1)} %all-gather.5.cloned.1.call-done), kind=kOutput, calls=%fused_computation.47 | convolution fusion | flops 21547188224 | bytes 46702592 | tf_op jit(solution)/shard_map/bsd,dc->bsc/dot_general | solution.py:60
  64.9 4.0 copy-done
  68.9 1.6 fusion.44
  70.5 11.9 slice_convert_fusion
  82.4 2.0 subtract_convert_fusion.1
  84.4 9.7 fusion.40
  94.1 88.4 %fusion.1 = (f32[8,8,1024]{2,1,0:T(8,128)S(1)}, f32[8,1024,1024,8]{2,1,3,0:T(8,128)}) fusion(pred[8,1024,1024]{1,2,0:T(8,128)(4,1)S(1)} %bitcast.112, bf16[8,1024,8,32]{1,3,2,0:T(8,128)(2,1)} %get-tuple-element.33, bf16[8,1024,8,32]{1,3,2,0:T(8,128)(2,1)} %get-tuple-element.32, bf16[8,1024,32]{1,2,0:T(8,128)(2,1)S(1)} %bitcast.124, ...), kind=kOutput, calls=%fused_computation.4 | convolution fusion | flops 8810070016 | bytes 286523392 | tf_op jit(solution)/shard_map/bqkgd,bskd->bkgqs/dot_general | solution.py:66
  182.5 83.4 %fusion = f32[8,8,1024]{2,1,0:T(8,128)S(1)} fusion(f32[8,1024,1024,8]{2,1,3,0:T(8,128)} %get-tuple-element.45, f32[8,8,1024]{2,1,0:T(8,128)S(1)} %get-tuple-element.44, pred[8,1024,1024]{1,2,0:T(8,128)(4,1)} %broadcast_and_fusion), kind=kLoop, calls=%fused_computation.3 | loop fusion | flops 268369920 | bytes 277348352 | tf_op jit(solution)/shard_map/reduce_sum | solution.py:70
  265.9 91.2 %fusion.33 = bf16[8,64,8,1024]{3,1,2,0:T(8,128)(2,1)} fusion(f32[8,8,1024]{2,1,0:T(8,128)S(1)} %fusion, f32[8,8,1024]{2,1,0:T(8,128)S(1)} %get-tuple-element.44, f32[8,1024,1024,8]{2,1,3,0:T(8,128)} %get-tuple-element.45, pred[8,1024,1024]{1,2,0:T(8,128)(4,1)} %broadcast_and_fusion, bf16[8,1024,1,10,64]{1,4,3,0,2:T(8,128)(2,1)} %bitcast.118), kind=kOutput, calls=%fused_computation.46 | convolution fusion | flops 8929673216 | bytes 286785536 | tf_op jit(solution)/shard_map/bkgqs,bskd->bqkgd/dot_general | solution.py:71
  357.1 25.5 %convolution_convert_fusion.1 = bf16[8,1024,2048]{2,1,0:T(8,128)(2,1)} fusion(bf16[8,1024,512]{1,2,0:T(8,128)(2,1)} %bitcast.125, bf16[512,2048]{1,0:T(8,128)(2,1)} %all-gather.7.cloned.1.call-done), kind=kOutput, calls=%fused_computation.36 | convolution fusion | flops 17196646400 | bytes 44040192 | tf_op jit(solution)/shard_map/bsh,hd->bsd/dot_general | solution.py:73
  382.7 0.1 all-reduce.3.cloned.1.call-update
  382.7 0.1 all-gather.9.cloned.1.call-start
  382.8 0.6 all-gather.9.cloned.1.call-update
  383.4 0.1 all-gather.11.cloned.1.call-start
  383.4 0.6 all-gather.11.cloned.1.call-update
  384.0 0.1 all-reduce.5.cloned.1.call-start
  384.1 558.7 %all-reduce.3.cloned.1.call-done = bf16[8,1024,2048]{2,1,0:T(8,128)(2,1)} async-done(((bf16[8,1024,2048]{2,1,0:T(8,128)(2,1)}), bf16[8,1024,2048]{2,1,0:T(8,128)(2,1)}) %all-reduce.3.cloned.1.call-update) | async-done | bytes 33554448 | tf_op jit(solution)/shard_map/psum | solution.py:74
  942.8 21.2 %fusion.8 = f32[8,1024]{1,0:T(8,128)S(1)} fusion(bf16[8,1024,2048]{2,1,0:T(8,128)(2,1)} %all-reduce.3.cloned.1.call-done, bf16[8,1024,2048]{2,1,0:T(8,128)(2,1)} %param.10), kind=kLoop, calls=%fused_computation.17 | loop fusion | flops 117432320 | bytes 67141632 | tf_op jit(solution)/shard_map/reduce_sum | solution.py:18
  964.0 41.2 %all-gather.9.cloned.1.call-done = bf16[2048,2816]{0,1:T(8,128)(2,1)} async-done(((bf16[2048,352]{0,1:T(8,128)(2,1)}), bf16[2048,2816]{0,1:T(8,128)(2,1)}) %all-gather.9.cloned.1.call-update) | async-done | bytes 11534352 | tf_op jit(solution)/shard_map/all_gather | solution.py:97
  1005.1 110.6 %fusion.25 = bf16[8,1024,2816]{2,1,0:T(8,128)(2,1)} fusion(f32[2048]{0:T(1024)S(1)} %convert_element_type.120, f32[8,1024]{1,0:T(8,128)S(1)} %add_rsqrt_fusion, bf16[2048,2816]{0,1:T(8,128)(2,1)} %all-gather.9.cloned.1.call-done, bf16[8,1024,2048]{2,1,0:T(8,128)(2,1)} %param.10, bf16[8,1024,2048]{2,1,0:T(8,128)(2,1)} %all-reduce.3.cloned.1.call-done), kind=kOutput, calls=%fused_computation.34 | convolution fusion | flops 94646566912 | bytes 124821504 | tf_op jit(solution)/shard_map/bsd,dc->bsc/dot_general | solution.py:78
  1115.7 56.0 %copy.32 = bf16[8,1024,2816]{1,2,0:T(8,128)(2,1)} copy(bf16[8,1024,2816]{2,1,0:T(8,128)(2,1)} %fusion.25) | data formatting | bytes 92274688 | tf_op jit(solution)/shard_map/convert_element_type | solution.py:78
  1171.7 30.3 %fusion.57 = (bf16[8,1024,8,1,176]{1,4,3,2,0:T(8,128)(2,1)}, bf16[8,1024,8,1,176]{1,4,3,2,0:T(8,128)(2,1)}) fusion(bf16[8,1024,8,2,176]{1,4,3,2,0:T(8,128)(2,1)} %bitcast.110), kind=kLoop, calls=%fused_computation.80 | loop fusion | bytes 92274688 | tf_op jit(solution)/shard_map/slice | solution.py:80
  1202.0 30.0 %fusion.16 = bf16[8,1024,1408]{1,2,0:T(8,128)(2,1)} fusion(bf16[8,1024,8,1,176]{1,4,3,2,0:T(8,128)(2,1)} %get-tuple-element.31, bf16[8,1024,8,1,176]{1,4,3,2,0:T(8,128)(2,1)} %get-tuple-element.30), kind=kLoop, calls=%fused_computation.27 | loop fusion | flops 92274688 | bytes 69206016 | tf_op jit(solution)/shard_map/convert_element_type | solution.py:80
  1232.1 59.9 %convolution_convert_fusion = bf16[8,1024,2048]{2,1,0:T(8,128)(2,1)} fusion(bf16[8,1024,1408]{1,2,0:T(8,128)(2,1)} %fusion.16, bf16[1408,2048]{1,0:T(8,128)(2,1)} %all-gather.11.cloned.1.call-done), kind=kOutput, calls=%fused_computation.35 | convolution fusion | flops 47261417472 | bytes 62390272 | tf_op jit(solution)/shard_map/bsf,fd->bsd/dot_general | solution.py:82
  1292.0 0.1 all-reduce.5.cloned.1.call-update
  1292.1 1.8 slice.65
  1293.9 2.5 copy.40
  1296.4 4.2 fusion.48
  1300.5 1.9 slice_bitcast_fusion.1
  1302.4 11.2 fusion.58
  1313.6 8.3 copy.41
  1322.0 8.3 copy.42
  1330.3 521.6 %all-reduce.5.cloned.1.call-done = bf16[8,1024,2048]{2,1,0:T(8,128)(2,1)} async-done(((bf16[8,1024,2048]{2,1,0:T(8,128)(2,1)}), bf16[8,1024,2048]{2,1,0:T(8,128)(2,1)}) %all-reduce.5.cloned.1.call-update) | async-done | bytes 33554448 | tf_op jit(solution)/shard_map/psum | solution.py:83
  1851.9 43.3 %fusion.11 = bf16[8,1024,2048]{2,1,0:T(8,128)(2,1)} fusion(bf16[8,1024,2048]{2,1,0:T(8,128)(2,1)} %all-reduce.5.cloned.1.call-done, bf16[8,1024,2048]{2,1,0:T(8,128)(2,1)} %all-reduce.3.cloned.1.call-done, bf16[8,1024,2048]{2,1,0:T(8,128)(2,1)} %param.10), kind=kLoop, calls=%fused_computation.20 | loop fusion | flops 134217728 | bytes 134217728 | tf_op jit(solution)/shard_map/convert_element_type | solution.py:84
  1895.2 1.3 copy.55
  1896.5 6.2 copy.56
  (32 shorter events, 0.1 us)
Async XLA Ops:
  7.2 13.4 copy-start.8
  7.2 14.0 copy-start.10
  7.2 30.3 %all-gather.5.cloned.1.call-start = ((), (), s32[]{:S(2)}) async-start(), calls=%async_computation | async-start | bytes 2949120 | tf_op jit(solution)/shard_map/all_gather | solution.py:95
  8.0 349.1 %all-gather.7.cloned.1.call-start = ((), (), s32[]{:S(2)}) async-start(), calls=%async_computation.1 | async-start | bytes 2359296 | tf_op jit(solution)/shard_map/all_gather | solution.py:96
  8.8 934.0 %all-reduce.3.cloned.1.call-start = ((), (), s32[]{:S(2)}) async-start(), calls=%async_computation.2 | async-start | bytes 67108864 | tf_op jit(solution)/shard_map/psum | solution.py:74
  21.2 0.6 copy-start.6
  64.9 4.0 copy-start
  70.5 23.7 %slice-start = ((s8[8388608]{0:T(1024)(128)(4,1)}), s8[4194304]{0:T(1024)(128)(4,1)S(1)}, s32[]{:S(2)}) async-start(s8[8388608]{0:T(1024)(128)(4,1)} %bitcast.111), calls=%async_computation.6 | async-start | bytes 8388608
  82.4 11.7 slice-start.1
  84.4 98.1 %copy-start.2 = (bf16[8,1024,1,32]{1,3,0,2:T(8,128)(2,1)}, bf16[8,1024,1,32]{1,3,0,2:T(8,128)(2,1)S(1)}, u32[]{:S(2)}) copy-start(bf16[8,1024,1,32]{1,3,0,2:T(8,128)(2,1)S(1)} %get-tuple-element.38) | copy-start | bytes 1572868
  84.4 98.1 %copy-start.4 = (bf16[8,1024,1,32]{1,3,0,2:T(8,128)(2,1)}, bf16[8,1024,1,32]{1,3,0,2:T(8,128)(2,1)S(1)}, u32[]{:S(2)}) copy-start(bf16[8,1024,1,32]{1,3,0,2:T(8,128)(2,1)S(1)} %get-tuple-element.39) | copy-start | bytes 1572868
  382.6 1.4 copy-start.9
  382.7 622.4 %all-gather.9.cloned.1.call-start = ((), (), s32[]{:S(2)}) async-start(), calls=%async_computation.3 | async-start | bytes 12976128 | tf_op jit(solution)/shard_map/all_gather | solution.py:97
  383.4 848.7 %all-gather.11.cloned.1.call-start = ((), (), s32[]{:S(2)}) async-start(), calls=%async_computation.4 | async-start | bytes 6488064 | tf_op jit(solution)/shard_map/all_gather | solution.py:98
  384.0 1467.9 %all-reduce.5.cloned.1.call-start = ((), (), s32[]{:S(2)}) async-start(), calls=%async_computation.5 | async-start | bytes 67108864 | tf_op jit(solution)/shard_map/psum | solution.py:83
  1292.0 4.4 copy-start.3
  1292.0 4.4 copy-start.5
  1292.0 4.4 copy-start.7
  1330.3 564.9 %copy-start.1 = (bf16[512,2048]{1,0:T(8,128)(2,1)S(1)}, bf16[512,2048]{1,0:T(8,128)(2,1)}, u32[]{:S(2)}) copy-start(bf16[512,2048]{1,0:T(8,128)(2,1)} %all-gather.7.cloned.1.call-done) | copy-start | bytes 6291460
Sparse Core Ops, SparseCore 0:
  9.6 27.8 all-gather.4
  39.2 23.0 all-gather.6
  382.8 559.8 all-reduce.2
  944.2 60.8 all-gather.8
  1006.6 36.1 all-gather.10
  1292.2 559.6 all-reduce.4
where the time goes:
time: 1920 us; the launch traced here: 1910 us
  waiting for transfers between devices  1130 us (59%)
  matrix products  403 us (21%)
  other arithmetic  225 us (12%)
  local copies, waits for them, and re-layouts  132 us (7%)
    psum x1, waiting for transfers between devices, prefill(): attn_sum = lax.psum(attn_part, 'tpa')  559 us
    psum x1, waiting for transfers between devices, prefill(): mlp_sum = lax.psum(mlp_part, 'tpa')  522 us
    dot_general x1, matrix products, prefill(): jnp.einsum('bsd,dc->bsc', h_normed, gu_cols, preferred_element_type=jnp.f...  111 us
    dot_general x1, matrix products, prefill(): jnp.einsum('bkgqs,bskd->bqkgd', attn_prob, values, preferred_element_type...  91.2 us
    dot_general x1, matrix products, prefill(): jnp.einsum('bqkgd,bskd->bkgqs', q_rot, k_rot, preferred_element_type=jnp....  88.4 us
    reduce_sum x1, other arithmetic, prefill(): attn_prob = jax.nn.softmax(scores, axis=-1).astype(jnp.bfloat16)  83.4 us
    dot_general x1, matrix products, prefill(): jnp.einsum('bsf,fd->bsd', mid_act, down_rows, preferred_element_type=jnp....  59.9 us
    convert_element_type x1, local copies, waits for them, and re-layouts, prefill(): jnp.einsum('bsd,dc->bsc', h_normed, gu_cols, preferred_element_type=jnp.f...  56 us
  transfers between devices with their start and end apart: 6, of which 4 were waited for; matrix products, arithmetic and copies ran while one was open for 32% of the time, Pallas kernels for 0%

commit v1 on v0

v1 whole, which is shorter than its diff:
```python
import functools
import math
import jax
import jax.numpy as jnp
from jax import lax
from jax.experimental import pallas as pl
from jax.experimental.pallas import tpu as pltpu
from jax.sharding import PartitionSpec as P

ROPE_BASE = 500000.0
ROPE_FACTOR = 8.0
LOW_FREQ = 1.0
HIGH_FREQ = 4.0
ORIG_CONTEXT = 8192.0
NORM_EPS = 1e-5
MASK_VALUE = -1e30
Q_TILE = 256
CHUNKS_PER_PROMPT = 2


def rms_norm(x_in, gain_vec):
    x_wide = x_in.astype(jnp.float32)
    mean_sq = jnp.mean(x_wide * x_wide, axis=-1, keepdims=True)
    return (x_wide * lax.rsqrt(mean_sq + NORM_EPS) * gain_vec.astype(jnp.float32)).astype(jnp.bfloat16)


def rope_tables(seq_len, head_dim):
    exponent = jnp.arange(head_dim // 2, dtype=jnp.float32) * (2.0 / head_dim)
    inv_freq = 1.0 / jnp.power(ROPE_BASE, exponent)
    wavelen = 2.0 * math.pi / inv_freq
    smooth = (ORIG_CONTEXT / wavelen - LOW_FREQ) / (HIGH_FREQ - LOW_FREQ)
    blended = (1.0 - smooth) * inv_freq / ROPE_FACTOR + smooth * inv_freq
    rope_freq = jnp.where(wavelen < ORIG_CONTEXT / HIGH_FREQ, inv_freq, jnp.where(wavelen > ORIG_CONTEXT / LOW_FREQ, inv_freq / ROPE_FACTOR, blended))
    angles = jnp.arange(seq_len, dtype=jnp.float32)[:, None] * rope_freq[None, :]
    return jnp.cos(angles), jnp.sin(angles)


def attention_kernel(head_dim, group_size, len_ref, qkv_ref, cos_ref, sin_ref, out_ref, k_scr, vl_scr, vr_scr):
    seq_len = qkv_ref.shape[1]
    pair = 2 * head_dim
    length = len_ref[pl.program_id(0)]
    lane = lax.broadcasted_iota(jnp.int32, (1, pair), 1)
    low_lane = lane < head_dim
    first_half = lax.rem(lane, head_dim) < head_dim // 2

    def rope(vec, rows):
        ahead = pltpu.roll(vec, pair - head_dim // 2, 1)
        behind = pltpu.roll(vec, head_dim // 2, 1)
        return vec * cos_ref[rows, :] + jnp.where(first_half, ahead, behind) * sin_ref[rows, :]

    q_cols = group_size * head_dim
    for start in range(0, seq_len, Q_TILE):
        rows = pl.ds(start, Q_TILE)
        kv = qkv_ref[0, rows, q_cols:q_cols + pair].astype(jnp.float32)
        k_rot = rope(kv, rows)
        k_scr[rows, :] = jnp.where(low_lane, k_rot, pltpu.roll(k_rot, head_dim, 1)).astype(jnp.bfloat16)
        vl_scr[rows, :] = jnp.where(low_lane, pltpu.roll(kv, head_dim, 1), 0.0).astype(jnp.bfloat16)
        vr_scr[rows, :] = jnp.where(low_lane, 0.0, kv).astype(jnp.bfloat16)

    for start in range(0, seq_len, Q_TILE):
        rows = pl.ds(start, Q_TILE)
        keys = start + Q_TILE
        row_id = start + lax.broadcasted_iota(jnp.int32, (Q_TILE, Q_TILE), 0)

        def weights(query):
            scores = lax.dot_general(query, k_scr[:keys, :], (((1,), (1,)), ((), ())), preferred_element_type=jnp.float32)
            parts = []
            for block in range(0, keys, Q_TILE):
                col_id = block + lax.broadcasted_iota(jnp.int32, (Q_TILE, Q_TILE), 1)
                allowed = col_id < length
                if block == start:
                    allowed = allowed & (col_id <= row_id)
                parts.append(jnp.where(allowed, scores[:, block:block + Q_TILE], MASK_VALUE))
            top = parts[0]
            for part in parts[1:]:
                top = jnp.maximum(top, part)
            top = jnp.max(top, axis=1, keepdims=True)
            parts = [jnp.exp(part - top) for part in parts]
            total = parts[0]
            for part in parts[1:]:
                total = total + part
            scale = 1.0 / jnp.sum(total, axis=1, keepdims=True)
            return jnp.concatenate([(part * scale).astype(jnp.bfloat16) for part in parts], axis=1)

        def head_pair(index, carry):
            cols = pl.ds(pl.multiple_of(index * pair, pair), pair)
            query = rope(qkv_ref[0, rows, cols].astype(jnp.float32), rows).astype(jnp.bfloat16).astype(jnp.float32) * head_dim ** -0.5
            left = weights(jnp.where(low_lane, query, 0.0).astype(jnp.bfloat16))
            right = weights(jnp.where(low_lane, 0.0, query).astype(jnp.bfloat16))
            acc = jnp.dot(left, vl_scr[:keys, :], preferred_element_type=jnp.float32)
            acc = acc + jnp.dot(right, vr_scr[:keys, :], preferred_element_type=jnp.float32)
            out_ref[0, rows, cols] = acc.astype(jnp.bfloat16)
            return carry

        lax.fori_loop(0, group_size // 2, head_pair, 0)


def attention(qkv_act, lengths, cos_tab, sin_tab, kv_heads, head_dim):
    batch, seq_len, qkv_cols = qkv_act.shape
    group_cols = qkv_cols // kv_heads
    group_size = group_cols // head_dim - 2
    out_cols = group_size * head_dim
    pair = 2 * head_dim
    cos_pair = jnp.tile(cos_tab, (1, 4))
    sin_pair = jnp.tile(jnp.concatenate([-sin_tab, sin_tab], axis=1), (1, 2))
    flops = 2 * 2 * batch * kv_heads * group_size * seq_len * seq_len * head_dim
    return pl.pallas_call(
        functools.partial(attention_kernel, head_dim, group_size),
        out_shape=jax.ShapeDtypeStruct((batch, seq_len, kv_heads * out_cols), jnp.bfloat16),
        grid_spec=pltpu.PrefetchScalarGridSpec(
            num_scalar_prefetch=1,
            grid=(batch, kv_heads),
            in_specs=[
                pl.BlockSpec((1, seq_len, group_cols), lambda b, g, _: (b, 0, g)),
                pl.BlockSpec((seq_len, pair), lambda b, g, _: (0, 0)),
                pl.BlockSpec((seq_len, pair), lambda b, g, _: (0, 0)),
            ],
            out_specs=pl.BlockSpec((1, seq_len, out_cols), lambda b, g, _: (b, 0, g)),
            scratch_shapes=[pltpu.VMEM((seq_len, pair), jnp.bfloat16)] * 3,
        ),
        compiler_params=pltpu.CompilerParams(dimension_semantics=('arbitrary', 'arbitrary'), vmem_limit_bytes=48 * 1024 * 1024),
        cost_estimate=pl.CostEstimate(flops=4 * flops, bytes_accessed=2 * batch * seq_len * (qkv_cols + kv_heads * out_cols), transcendentals=batch * kv_heads * group_size * seq_len * seq_len),
        name='prefill_attention',
    )(lengths, qkv_act, cos_pair, sin_pair)


def empty(shape, dtype):
    return pl.pallas_call(lambda out_ref: None, out_shape=jax.ShapeDtypeStruct(shape, dtype), out_specs=pl.BlockSpec(memory_space=pl.ANY), name='output_buffer')()


def matmul_t(lhs, rhs_t):
    return lax.dot_general(lhs, rhs_t, (((lhs.ndim - 1,), (1,)), ((), ())), preferred_element_type=jnp.float32)


def solution(mesh):
    n_tpa = mesh.shape['tpa']
    n_tpb = mesh.shape['tpb']
    up_ring = [(i, (i + 1) % n_tpa) for i in range(n_tpa)]
    down_ring = [(i, (i - 1) % n_tpa) for i in range(n_tpa)]
    both = ('tpa', 'tpb')

    def layer_step(x_loc, len_loc, k_buf, v_buf, w_qkv, w_o, w_gate_up, w_down, g_attn, g_mlp):
        row = lax.axis_index('tpa')
        batch_loc, seq_len, model_dim = x_loc.shape
        head_dim = k_buf.shape[3]
        own_batch = batch_loc // n_tpa
        ff_block = w_gate_up.shape[1] // 2
        qkv_row = w_qkv.shape[1] * n_tpb
        o_row = w_o.shape[0] * n_tpb
        ff_row = ff_block * n_tpb

        qkv_block = w_qkv.shape[1]
        qkvo = lax.all_gather(jnp.concatenate([w_qkv.T, w_o], axis=0), both, axis=0, tiled=False)
        qkv_t = qkvo[:, :qkv_block].reshape(-1, model_dim)
        o_full = qkvo[:, qkv_block:].reshape(-1, model_dim)
        gu_t = lax.all_gather(w_gate_up.T.reshape(2, ff_block, model_dim), both, axis=1, tiled=True)
        down_full = lax.all_gather(w_down, both, axis=0, tiled=True)

        cos_tab, sin_tab = rope_tables(seq_len, head_dim)
        x_own = lax.dynamic_index_in_dim(x_loc.reshape(own_batch, n_tpa, seq_len, model_dim), row, 1, keepdims=False)
        len_own = lax.dynamic_index_in_dim(len_loc.reshape(own_batch, n_tpa), row, 1, keepdims=False)

        qkv_act = matmul_t(rms_norm(x_own, g_attn), qkv_t).astype(jnp.bfloat16)
        attn_out = attention(qkv_act, len_own, cos_tab, sin_tab, n_tpa * k_buf.shape[2], head_dim)
        attn_proj = jnp.dot(attn_out, o_full, preferred_element_type=jnp.float32)
        hidden = (x_own.astype(jnp.float32) + attn_proj).astype(jnp.bfloat16)

        chunk = seq_len // CHUNKS_PER_PROMPT
        fars = []
        spots = [(slot, start) for slot in range(own_batch) for start in range(0, seq_len, chunk)]
        y_all = empty((own_batch, n_tpa, seq_len, model_dim), jnp.bfloat16)

        def put(y_buf, piece, slot, owner, start):
            return lax.dynamic_update_slice(y_buf, piece[None, None], (slot, lax.rem(owner + n_tpa, n_tpa), start, 0))

        mids = []
        ahead = 2
        for index, (slot, start) in enumerate(spots):
            h_normed = rms_norm(hidden[slot, start:start + chunk], g_mlp)
            gate_act = matmul_t(h_normed, gu_t[0]).astype(jnp.bfloat16)
            up_act = matmul_t(h_normed, gu_t[1]).astype(jnp.bfloat16)
            mids.append((jax.nn.silu(gate_act.astype(jnp.float32)) * up_act.astype(jnp.float32)).astype(jnp.bfloat16))
            if index == ahead - 1:
                down_use, *mids = lax.optimization_barrier((down_full, *mids))
        y_parts = []
        for mid_act, (slot, start) in zip(mids, spots):
            mlp_out = jnp.dot(mid_act, down_use, preferred_element_type=jnp.float32)
            y_parts.append((hidden[slot, start:start + chunk].astype(jnp.float32) + mlp_out).astype(jnp.bfloat16))
        near = []
        for part in y_parts:
            near.append((lax.ppermute(part, 'tpa', up_ring), lax.ppermute(part, 'tpa', down_ring)))
        for part, (slot, start) in zip(y_parts, spots):
            y_all = put(y_all, part, slot, row, start)

        qkv_own = lax.dynamic_slice_in_dim(qkv_t, row * qkv_row, qkv_row, 0)
        kv_cols = k_buf.shape[2] * head_dim
        q_cols = qkv_row - 2 * kv_cols
        w_query = qkv_own[:q_cols].T
        w_key = qkv_own[q_cols:q_cols + kv_cols].T
        w_value = qkv_own[q_cols + kv_cols:].T
        gu_own = lax.dynamic_slice_in_dim(gu_t, row * ff_row, ff_row, 1)
        w_gate = gu_own[0].T
        w_up = gu_own[1].T
        o_rows = lax.dynamic_slice_in_dim(o_full, row * o_row, o_row, 0)
        down_rows = lax.dynamic_slice_in_dim(down_full, row * ff_row, ff_row, 0)

        kv_new = matmul_t(rms_norm(x_loc, g_attn), qkv_own[q_cols:]).astype(jnp.bfloat16)
        half_dim = head_dim // 2
        k_first = kv_new[..., :half_dim].astype(jnp.float32)
        k_second = kv_new[..., half_dim:head_dim].astype(jnp.float32)
        k_rot = jnp.concatenate([k_first * cos_tab - k_second * sin_tab, k_second * cos_tab + k_first * sin_tab], axis=-1).astype(jnp.bfloat16)
        valid_pos = (jnp.arange(seq_len)[None, :] < len_loc[:, None])[:, :, None, None]
        k_cache = jnp.where(valid_pos, k_rot[:, :, None, :], k_buf)
        v_cache = jnp.where(valid_pos, kv_new[:, :, None, head_dim:], v_buf)
        fillers = (w_query, w_gate, w_up, down_rows, k_cache, v_cache)
        near[0], fillers, y_all = lax.optimization_barrier((near[0], fillers, y_all))
        w_query, w_gate, w_up, down_rows, k_cache, v_cache = fillers
        for index, ((from_below, from_above), (slot, start)) in enumerate(zip(near, spots)):
            if index % 2 == 0:
                far = lax.ppermute(from_below, 'tpa', up_ring)
            else:
                far = lax.ppermute(from_above, 'tpa', down_ring)
            y_all = put(y_all, from_below, slot, row - 1, start)
            y_all = put(y_all, from_above, slot, row + 1, start)
            fars.append(far)
        for far, (slot, start) in zip(fars, spots):
            y_all = put(y_all, far, slot, row - 2, start)
        layer_out = y_all.reshape(batch_loc, seq_len, model_dim)
        return (layer_out, k_cache, v_cache, w_query, w_key, w_value, o_rows, w_gate, w_up, down_rows)

    batch_spec = P(('part', 'tpb'), None, None)
    len_spec = P(('part', 'tpb'))
    cache_spec = P(('part', 'tpb'), None, 'tpa', None)
    train_cols = P('part', ('tpa', 'tpb'))
    train_rows = P(('part', 'tpa', 'tpb'), None)
    gain_spec = P('part')
    gen_cols = P('part', 'tpa')
    gen_rows = P(('part', 'tpa'), None)
    return jax.shard_map(layer_step, mesh=mesh, in_specs=(batch_spec, len_spec, cache_spec, cache_spec, train_cols, train_rows, train_cols, train_rows, gain_spec, gain_spec), out_specs=(batch_spec, cache_spec, cache_spec, gen_cols, gen_cols, gen_cols, gen_rows, gen_cols, gen_cols, gen_rows), check_vma=False)
```

time: 1920 us -> 774 us (0.40)
  waiting for transfers between devices: 1130 us -> 182 us
  other arithmetic: 225 us -> 29.9 us
  Pallas kernels: 0 us -> 130 us
  matrix products: 403 us -> 304 us
  local copies, waits for them, and re-layouts: 132 us -> 95.6 us
    psum x2 -> x0, waiting for transfers between devices: 1080 us -> none  [the longest x1 559 us: prefill(): attn_sum = lax.psum(attn_part, 'tpa')]
    pallas_call x0 -> x2, Pallas kernels: none -> 130 us  [the longest x1 130 us: attention(): pl.pallas_call(functools.partial(attention_kernel, head_dim, group_size),...]
    ppermute x0 -> x12, waiting for transfers between devices: none -> 127 us  [the longest x4 51.4 us: layer_step(): lax.ppermute(part, 'tpa', down_ring)]
    dot_general x6 -> x15, matrix products: 403 us -> 304 us  [the longest x10 205 us: matmul_t(): lax.dot_general(lhs, rhs_t, (((lhs.ndim - 1,), (1,)), ((), ())), preferre...]
    convert_element_type x4 -> x0, other arithmetic: 86.8 us -> none  [the longest x1 43.3 us: prefill(): (hidden.astype(jnp.float32) + mlp_sum.astype(jnp.float32)).astype(jnp.bfl...]
    reduce_sum x1 -> x0, other arithmetic: 83.4 us -> none  [prefill(): attn_prob = jax.nn.softmax(scores, axis=-1).astype(jnp.bfloat16)]
    convert_element_type x1 -> x0, local copies, waits for them, and re-layouts: 56 us -> none  [prefill(): jnp.einsum('bsd,dc->bsc', h_normed, gu_cols, preferred_element_type=jnp.f...]
    dynamic_update_slice x0 -> x12, local copies, waits for them, and re-layouts: none -> 29.4 us  [put(): lax.dynamic_update_slice(y_buf, piece[None, None], (slot, lax.rem(owner +...]
  transfers between devices with their start and end apart: 6 -> 15, of which waited for: 4 -> 6; matrix products, arithmetic and copies ran while one was open for 32% -> 40% of each run, Pallas kernels for 0% -> 17%
where the time goes in v1:
time: 774 us; the launch traced here: 768 us
  matrix products  304 us (39%)
  waiting for transfers between devices  182 us (24%)
  Pallas kernels  130 us (17%)
  local copies, waits for them, and re-layouts  95.6 us (12%)
  other arithmetic  29.9 us (4%)
  between operations  14.4 us (2%)
  starting transfers between devices  12.2 us (2%)
    dot_general x10, matrix products, matmul_t(): lax.dot_general(lhs, rhs_t, (((lhs.ndim - 1,), (1,)), ((), ())), preferre...  205 us
    pallas_call x1, Pallas kernels, attention(): pl.pallas_call(functools.partial(attention_kernel, head_dim, group_size),...  130 us
    dot_general x4, matrix products, layer_step(): mlp_out = jnp.dot(mid_act, down_use, preferred_element_type=jnp.float32)  76.1 us
    all_gather x1, waiting for transfers between devices, layer_step(): lax.all_gather(jnp.concatenate([w_qkv.T, w_o], axis=0), both, axis=0, til...  54 us
    ppermute x4, waiting for transfers between devices, layer_step(): lax.ppermute(part, 'tpa', down_ring)  51.4 us
    ppermute x2, waiting for transfers between devices, layer_step(): far = lax.ppermute(from_below, 'tpa', up_ring)  44 us
    ppermute x2, waiting for transfers between devices, layer_step(): far = lax.ppermute(from_above, 'tpa', down_ring)  31.2 us
    dynamic_update_slice x12, local copies, waits for them, and re-layouts, put(): lax.dynamic_update_slice(y_buf, piece[None, None], (slot, lax.rem(owner +...  29.4 us
  transfers between devices with their start and end apart: 15, of which 6 were waited for; matrix products, arithmetic and copies ran while one was open for 40% of the time, Pallas kernels for 17%

profile of v1, /device:TPU:97, one launch (start us, length us, event | category | flops | bytes accessed | tf_op | source)
XLA Modules:
  0.0 767.6 jit_solution(10535129978875227139)
XLA Ops:
  7.3 1.9 pad_maximum_fusion
  14.9 5.1 fusion.9
  20.0 12.7 %fusion = f32[8,1024]{1,0:T(8,128)S(1)} fusion(bf16[8,1024,2048]{2,1,0:T(8,128)(2,1)} %param.10), kind=kLoop, calls=%fused_computation.2 | loop fusion | flops 50323456 | bytes 33587200 | tf_op jit(solution)/shard_map/reduce_sum | solution.py:23
  33.3 54.0 %all-gather.9.cloned.1.call-done = bf16[4608,2048]{1,0:T(8,128)(2,1)} async-done(((bf16[144,2048]{1,0:T(8,128)(2,1)}), bf16[4608,2048]{1,0:T(8,128)(2,1)}) %all-gather.9.cloned.1.call-update) | async-done | bytes 18874384 | tf_op jit(solution)/shard_map/all_gather | solution.py:153
  87.3 8.2 %slice.79 = bf16[32,64,2048]{2,1,0:T(8,128)(2,1)} slice(bf16[32,144,2048]{2,1,0:T(8,128)(2,1)} %bitcast.239), slice={[0:32], [80:144], [0:2048]} | slice | bytes 16777216 | tf_op jit(solution)/shard_map/slice | solution.py:155
  95.5 10.6 %slice.78 = bf16[32,80,2048]{2,1,0:T(8,128)(2,1)} slice(bf16[32,144,2048]{2,1,0:T(8,128)(2,1)} %bitcast.240), slice={[0:32], [0:80], [0:2048]} | slice | bytes 20971520 | tf_op jit(solution)/shard_map/slice | solution.py:154
  106.1 29.8 %fusion.55.qkv_ref = bf16[2,1024,2560]{2,1,0:T(8,128)(2,1)} fusion(bf16[2560,2048,1]{1,0,2:T(8,128)(2,1)} %bitcast.241, f32[2048]{0:T(1024)S(1)} %convert_element_type.202, f32[2,1024]{1,0:T(2,128)S(1)} %add_rsqrt_fusion.1, bf16[2,4,1024,2048]{3,2,1,0:T(8,128)(2,1)} %bitcast.236, s32[]{:T(128)S(6)} %select_n.86), kind=kOutput, calls=%fused_computation.67 | convolution fusion | flops 21496856576 | bytes 29376516 | tf_op jit(solution)/shard_map/dot_general | solution.py:132
  135.9 129.8 %prefill_attention.1 = bf16[2,1024,2048]{2,1,0:T(8,128)(2,1)} custom-call(s32[2]{0:T(128)S(1)} %fusion.140.len_ref, bf16[2,1024,2560]{2,1,0:T(8,128)(2,1)} %fusion.55.qkv_ref, f32[1024,128]{1,0:T(8,128)S(1)} %copy.28.cos_ref, f32[1024,128]{1,0:T(8,128)S(1)} %copy.29.sin_ref), custom_call_target="tpu_custom_call" | custom-call | flops 68719476736 | bytes 18874368 | tf_op jit(solution)/shard_map/prefill_attention/pallas_call | solution.py:107
  265.8 22.6 %fusion.10 = bf16[2,1024,2048]{2,1,0:T(8,128)(2,1)} fusion(bf16[2,1024,2048]{2,1,0:T(8,128)(2,1)} %prefill_attention.1, bf16[2048,2048,1]{1,0,2:T(8,128)(2,1)S(1)} %bitcast.248, bf16[2,4,1024,2048]{3,2,1,0:T(8,128)(2,1)} %bitcast.237, s32[]{:T(128)S(6)} %select_n.86), kind=kOutput, calls=%fused_computation.15 | convolution fusion | flops 17192452096 | bytes 33554436 | tf_op jit(solution)/shard_map/dot_general | solution.py:165
  288.4 4.3 fusion.85
  293.3 1.9 dynamic-slice_bitcast_fusion.5
  295.2 17.5 %fusion.115 = bf16[8,1024,128]{1,2,0:T(8,128)(2,1)S(1)} fusion(bf16[8,1024,2048]{2,1,0:T(8,128)(2,1)} %param.10, f32[2048]{0:T(1024)S(1)} %convert_element_type.202, f32[8,1024]{1,0:T(8,128)S(1)} %copy-done.8, bf16[2560,2048]{1,0:T(8,128)(2,1)} %bitcast.243, s32[]{:T(128)S(6)} %add.215), kind=kOutput, calls=%fused_computation.136 | convolution fusion | flops 4363124736 | bytes 36216836 | tf_op jit(solution)/shard_map/dot_general | solution.py:132
  313.1 3.4 dynamic-slice_bitcast_fusion.2
  316.5 3.2 constant_dynamic-slice_fusion
  319.7 2.4 fusion.128
  322.1 6.2 constant_dynamic-slice_fusion.1
  328.3 19.0 %fusion.42 = bf16[512,5632]{1,0:T(8,128)(2,1)} fusion(bf16[2,5632,2048]{2,1,0:T(8,128)(2,1)} %all-gather.7.cloned.1.call-done, f32[512]{0:T(512)S(1)} %get-tuple-element.79, f32[2048]{0:T(1024)S(1)} %copy-done.9, bf16[2,1024,2048]{2,1,0:T(8,128)(2,1)} %fusion.10), kind=kOutput, calls=%fused_computation.55 | convolution fusion | flops 11818237952 | bytes 30943232 | tf_op jit(solution)/shard_map/dot_general | solution.py:132
  347.3 20.7 %fusion.39 = bf16[512,5632]{1,0:T(8,128)(2,1)} fusion(bf16[512,5632]{1,0:T(8,128)(2,1)} %fusion.42, bf16[2,5632,2048]{2,1,0:T(8,128)(2,1)} %all-gather.7.cloned.1.call-done, f32[512]{0:T(512)S(1)} %get-tuple-element.79, f32[2048]{0:T(1024)S(1)} %copy-done.9, bf16[2,1024,2048]{2,1,0:T(8,128)(2,1)} %fusion.10), kind=kOutput, calls=%fused_computation.52 | convolution fusion | flops 11841306624 | bytes 36710400 | tf_op jit(solution)/shard_map/dot_general | solution.py:132
  368.0 18.8 %fusion.41 = bf16[512,5632]{1,0:T(8,128)(2,1)} fusion(bf16[2,5632,2048]{2,1,0:T(8,128)(2,1)} %all-gather.7.cloned.1.call-done, f32[2048]{0:T(1024)S(1)} %copy-done.9, f32[512]{0:T(512)S(1)} %get-tuple-element.80, bf16[2,1024,2048]{2,1,0:T(8,128)(2,1)} %fusion.10), kind=kOutput, calls=%fused_computation.54 | convolution fusion | flops 11818237952 | bytes 30943232 | tf_op jit(solution)/shard_map/dot_general | solution.py:132
  386.8 19.9 %fusion.40 = bf16[512,5632]{1,0:T(8,128)(2,1)S(1)} fusion(bf16[512,5632]{1,0:T(8,128)(2,1)} %fusion.41, bf16[2,5632,2048]{2,1,0:T(8,128)(2,1)} %all-gather.7.cloned.1.call-done, f32[2048]{0:T(1024)S(1)} %copy-done.9, f32[512]{0:T(512)S(1)} %get-tuple-element.80, bf16[2,1024,2048]{2,1,0:T(8,128)(2,1)} %fusion.10), kind=kOutput, calls=%fused_computation.53 | convolution fusion | flops 11841306624 | bytes 36710400 | tf_op jit(solution)/shard_map/dot_general | solution.py:132
  406.6 18.2 %bitcast_dynamic-update-slice_fusion.15 = (bf16[2,4,1024,2048]{3,2,1,0:T(8,128)(2,1)}, bf16[512,2048]{1,0:T(8,128)(2,1)}) fusion(bf16[2,4,1024,2048]{3,2,1,0:T(8,128)(2,1)} %output_buffer.1, s32[]{:T(128)S(6)} %select_n.93, bf16[512,5632]{1,0:T(8,128)(2,1)S(1)} %fusion.40, bf16[5632,2048]{1,0:T(8,128)(2,1)} %all-gather.5.cloned.1.call-done, ...), kind=kOutput, calls=%fused_computation.127 | convolution fusion | flops 11814305792 | bytes 35127300 | tf_op jit(solution)/shard_map/dot_general | solution.py:187
  424.9 18.1 %bitcast_dynamic-update-slice_fusion.14 = (bf16[2,4,1024,2048]{3,2,1,0:T(8,128)(2,1)}, bf16[512,2048]{1,0:T(8,128)(2,1)}) fusion(bf16[2,4,1024,2048]{3,2,1,0:T(8,128)(2,1)} %get-tuple-element.69, s32[]{:T(128)S(6)} %select_n.93, bf16[512,5632]{1,0:T(8,128)(2,1)S(1)} %copy-done.16, bf16[5632,2048]{1,0:T(8,128)(2,1)} %all-gather.5.cloned.1.call-done, ...), kind=kOutput, calls=%fused_computation.126 | convolution fusion | flops 11814305792 | bytes 35127300 | tf_op jit(solution)/shard_map/dot_general | solution.py:187
  443.9 1.7 collective-permute-start.3
  447.1 19.0 %fusion.43 = bf16[512,5632]{1,0:T(8,128)(2,1)} fusion(bf16[2,5632,2048]{2,1,0:T(8,128)(2,1)} %all-gather.7.cloned.1.call-done, f32[512]{0:T(512)S(1)} %copy-done.13, f32[2048]{0:T(1024)S(1)} %copy-done.9, bf16[2,1024,2048]{2,1,0:T(8,128)(2,1)} %fusion.10), kind=kOutput, calls=%fused_computation.56 | convolution fusion | flops 11818237952 | bytes 30943232 | tf_op jit(solution)/shard_map/dot_general | solution.py:132
  466.1 20.7 %fusion.92.clone.4 = bf16[512,5632]{1,0:T(8,128)(2,1)} fusion(bf16[512,5632]{1,0:T(8,128)(2,1)} %fusion.43, bf16[2,5632,2048]{2,1,0:T(8,128)(2,1)} %all-gather.7.cloned.1.call-done, f32[512]{0:T(512)S(1)} %copy-done.13, f32[2048]{0:T(1024)S(1)} %copy-done.9, bf16[2,1024,2048]{2,1,0:T(8,128)(2,1)} %fusion.10), kind=kOutput, calls=%fused_computation.51.clone.clone.clone.clone.clone.clone.1 | convolution fusion | flops 11841306624 | bytes 36710400 | tf_op jit(solution)/shard_map/dot_general | solution.py:132
  486.7 19.8 %bitcast_dynamic-update-slice_fusion.13 = (bf16[2,4,1024,2048]{3,2,1,0:T(8,128)(2,1)}, bf16[512,2048]{1,0:T(8,128)(2,1)}) fusion(bf16[2,4,1024,2048]{3,2,1,0:T(8,128)(2,1)} %get-tuple-element.71, s32[]{:T(128)S(6)} %select_n.93, bf16[5632,2048]{1,0:T(8,128)(2,1)} %all-gather.5.cloned.1.call-done, bf16[2,1024,2048]{2,1,0:T(8,128)(2,1)} %fusion.10, ...), kind=kOutput, calls=%fused_computation.125 | convolution fusion | flops 11814305792 | bytes 35127300 | tf_op jit(solution)/shard_map/dot_general | solution.py:187
  506.6 19.0 %fusion.44 = bf16[512,5632]{1,0:T(8,128)(2,1)} fusion(bf16[2,5632,2048]{2,1,0:T(8,128)(2,1)} %all-gather.7.cloned.1.call-done, f32[512]{0:T(512)S(1)} %copy-done.12, f32[2048]{0:T(1024)S(1)} %copy-done.9, bf16[2,1024,2048]{2,1,0:T(8,128)(2,1)} %fusion.10), kind=kOutput, calls=%fused_computation.57 | convolution fusion | flops 11818237952 | bytes 30943232 | tf_op jit(solution)/shard_map/dot_general | solution.py:132
  525.6 20.7 %fusion.90.clone.4 = bf16[512,5632]{1,0:T(8,128)(2,1)} fusion(bf16[512,5632]{1,0:T(8,128)(2,1)} %fusion.44, bf16[2,5632,2048]{2,1,0:T(8,128)(2,1)} %all-gather.7.cloned.1.call-done, f32[512]{0:T(512)S(1)} %copy-done.12, f32[2048]{0:T(1024)S(1)} %copy-done.9, bf16[2,1024,2048]{2,1,0:T(8,128)(2,1)} %fusion.10), kind=kOutput, calls=%fused_computation.50.clone.clone.clone.clone.clone.clone.1 | convolution fusion | flops 11841306624 | bytes 36710400 | tf_op jit(solution)/shard_map/dot_general | solution.py:132
  546.3 20.0 %bitcast_dynamic-update-slice_fusion.12 = (bf16[2,4,1024,2048]{3,2,1,0:T(8,128)(2,1)}, bf16[512,2048]{1,0:T(8,128)(2,1)}) fusion(bf16[2,4,1024,2048]{3,2,1,0:T(8,128)(2,1)} %get-tuple-element.73, s32[]{:T(128)S(6)} %select_n.93, bf16[5632,2048]{1,0:T(8,128)(2,1)} %all-gather.5.cloned.1.call-done, bf16[2,1024,2048]{2,1,0:T(8,128)(2,1)} %fusion.10, ...), kind=kOutput, calls=%fused_computation.124 | convolution fusion | flops 11814305792 | bytes 35127300 | tf_op jit(solution)/shard_map/dot_general | solution.py:187
  566.3 11.4 %dynamic-slice_bitcast_fusion = (bf16[2048,1408]{0,1:T(8,128)(2,1)}, bf16[2048,1408]{0,1:T(8,128)(2,1)}) fusion(bf16[2,5632,2048]{2,1,0:T(8,128)(2,1)} %all-gather.7.cloned.1.call-done, s32[]{:T(128)S(6)} %add.214, s32[]{:T(128)S(6)} %select_n.90), kind=kLoop, calls=%fused_computation.71 | loop fusion | bytes 23068680 | tf_op jit(solution)/shard_map/transpose | solution.py:203
  577.7 2.6 collective-permute-start.5
  581.2 2.5 copy.34
  583.6 8.3 %copy.35 = bf16[2048,1408]{1,0:T(8,128)(2,1)} copy(bf16[2048,1408]{0,1:T(8,128)(2,1)} %get-tuple-element.51) | data formatting | bytes 11534336
  592.0 8.5 %copy.36 = bf16[2048,1408]{1,0:T(8,128)(2,1)} copy(bf16[2048,1408]{0,1:T(8,128)(2,1)} %get-tuple-element.52) | data formatting | bytes 11534336
  600.4 3.2 bitcast_dynamic-update-slice_fusion.11
  603.6 3.2 bitcast_dynamic-update-slice_fusion.10
  607.4 3.2 bitcast_dynamic-update-slice_fusion.9
  610.9 3.2 bitcast_dynamic-update-slice_fusion.8
  614.0 3.2 bitcast_dynamic-update-slice_fusion.7
  617.2 51.4 %collective-permute-done.7 = bf16[512,2048]{1,0:T(8,128)(2,1)} collective-permute-done((bf16[512,2048]{1,0:T(8,128)(2,1)}, bf16[512,2048]{1,0:T(8,128)(2,1)}, u32[]{:S(2)}, u32[]{:S(2)}) %collective-permute-start.7) | collective-permute-done | bytes 2097184 | tf_op jit(solution)/shard_map/ppermute | solution.py:191
  668.6 3.4 collective-permute-start.9
  672.0 3.2 bitcast_dynamic-update-slice_fusion.6
  675.2 1.5 bitcast_dynamic-update-slice_fusion.5
  676.6 3.2 bitcast_dynamic-update-slice_fusion.4
  679.8 17.6 %collective-permute-done.8 = bf16[512,2048]{1,0:T(8,128)(2,1)S(1)} collective-permute-done((bf16[512,2048]{1,0:T(8,128)(2,1)}, bf16[512,2048]{1,0:T(8,128)(2,1)S(1)}, u32[]{:S(2)}, u32[]{:S(2)}) %collective-permute-start.8) | collective-permute-done | bytes 2097184 | tf_op jit(solution)/shard_map/ppermute | solution.py:220
  698.8 15.6 %collective-permute-done.9 = bf16[512,2048]{1,0:T(8,128)(2,1)S(1)} collective-permute-done((bf16[512,2048]{1,0:T(8,128)(2,1)}, bf16[512,2048]{1,0:T(8,128)(2,1)S(1)}, u32[]{:S(2)}, u32[]{:S(2)}) %collective-permute-start.9) | collective-permute-done | bytes 2097184 | tf_op jit(solution)/shard_map/ppermute | solution.py:222
  715.9 26.4 %collective-permute-done.10 = bf16[512,2048]{1,0:T(8,128)(2,1)S(1)} collective-permute-done((bf16[512,2048]{1,0:T(8,128)(2,1)}, bf16[512,2048]{1,0:T(8,128)(2,1)S(1)}, u32[]{:S(2)}, u32[]{:S(2)}) %collective-permute-start.10) | collective-permute-done | bytes 2097184 | tf_op jit(solution)/shard_map/ppermute | solution.py:220
  743.8 15.6 %collective-permute-done.11 = bf16[512,2048]{1,0:T(8,128)(2,1)S(1)} collective-permute-done((bf16[512,2048]{1,0:T(8,128)(2,1)}, bf16[512,2048]{1,0:T(8,128)(2,1)S(1)}, u32[]{:S(2)}, u32[]{:S(2)}) %collective-permute-start.11) | collective-permute-done | bytes 2097184 | tf_op jit(solution)/shard_map/ppermute | solution.py:222
  (85 shorter events, 17.3 us)
Async XLA Ops:
  7.2 80.1 %all-gather.9.cloned.1.call-start = ((), (), s32[]{:S(2)}) async-start(), calls=%async_computation.2 | async-start | bytes 19464192 | tf_op jit(solution)/shard_map/all_gather | solution.py:153
  9.2 312.9 %all-gather.5.cloned.1.call-start = ((), (), s32[]{:S(2)}) async-start(), calls=%async_computation | async-start | bytes 23789568 | tf_op jit(solution)/shard_map/all_gather | solution.py:157
  10.1 318.2 %all-gather.7.cloned.1.call-start = ((), (), s32[]{:S(2)}) async-start(), calls=%async_computation.1 | async-start | bytes 47579136 | tf_op jit(solution)/shard_map/all_gather | solution.py:156
  10.9 0.7 copy-start.14
  10.9 0.7 copy-start.10
  10.9 1.3 copy-start.11
  12.8 0.7 copy-start.3
  12.8 19.9 %copy-start.1 = (f32[1024,32]{0,1:T(8,128)}, f32[1024,32]{0,1:T(8,128)S(1)}, u32[]{:S(2)}) copy-start(f32[1024,32]{0,1:T(8,128)S(1)} %get-tuple-element.68) | copy-start | bytes 393220
  106.1 159.6 %slice-start = ((s8[8388608]{0:T(1024)(128)(4,1)}), s8[4194304]{0:T(1024)(128)(4,1)S(1)}, s32[]{:S(2)}) async-start(s8[8388608]{0:T(1024)(128)(4,1)} %bitcast.246), calls=%async_computation.3 | async-start | bytes 8388608
  135.9 129.8 %slice-start.1 = ((s8[8388608]{0:T(1024)(128)(4,1)}), s8[4194304]{0:T(1024)(128)(4,1)S(1)}, s32[]{:S(2)}) async-start(s8[8388608]{0:T(1024)(128)(4,1)} %bitcast.246), calls=%async_computation.4 | async-start | bytes 8388608
  288.4 6.8 copy-start.8
  295.2 17.5 %copy-start.2 = (f32[1024,32]{0,1:T(8,128)S(1)}, f32[1024,32]{0,1:T(8,128)}, u32[]{:S(2)}) copy-start(f32[1024,32]{0,1:T(8,128)} %copy-done.1) | copy-start | bytes 393220
  295.2 17.5 %copy-start.4 = (f32[1024,32]{0,1:T(8,128)S(1)}, f32[1024,32]{0,1:T(8,128)}, u32[]{:S(2)}) copy-start(f32[1024,32]{0,1:T(8,128)} %copy-done.3) | copy-start | bytes 393220
  312.7 6.9 copy-start.5
  312.7 6.9 copy-start.6
  312.7 6.9 copy-start.7
  319.6 8.6 %copy-start.9 = (f32[2048]{0:T(1024)S(1)}, f32[2048]{0:T(1024)}, u32[]{:S(2)}) copy-start(f32[2048]{0:T(1024)} %convert_element_type.210) | copy-start | bytes 24580
  406.6 18.2 %copy-start.16 = (bf16[512,5632]{1,0:T(8,128)(2,1)S(1)}, bf16[512,5632]{1,0:T(8,128)(2,1)}, u32[]{:S(2)}) copy-start(bf16[512,5632]{1,0:T(8,128)(2,1)} %fusion.39) | copy-start | bytes 17301508
  424.9 22.2 %copy-start.13 = (f32[512]{0:T(512)S(1)}, f32[512]{0:T(512)}, u32[]{:S(2)}) copy-start(f32[512]{0:T(512)} %get-tuple-element.78) | copy-start | bytes 6148
  442.9 163.8 %collective-permute-start.2 = (bf16[512,2048]{1,0:T(8,128)(2,1)}, bf16[512,2048]{1,0:T(8,128)(2,1)}, u32[]{:S(2)}, u32[]{:S(2)}) collective-permute-start(bf16[512,2048]{1,0:T(8,128)(2,1)} %get-tuple-element.72), channel_id=1, source_target_pairs={{0,8},{8,16},{16,24},{24,0},{1,9},{9,17},{17,25},{25,1},{2,10},{10... | collective-permute-start | bytes 6291464 | tf_op jit(solution)/shard_map/ppermute | solution.py:191
  443.9 166.7 %collective-permute-start.3 = (bf16[512,2048]{1,0:T(8,128)(2,1)}, bf16[512,2048]{1,0:T(8,128)(2,1)}, u32[]{:S(2)}, u32[]{:S(2)}) collective-permute-start(bf16[512,2048]{1,0:T(8,128)(2,1)} %get-tuple-element.72), channel_id=1, source_target_pairs={{0,24},{8,0},{16,8},{24,16},{1,25},{9,1},{17,9},{25,17},{2,26},{10... | collective-permute-start | bytes 6291464 | tf_op jit(solution)/shard_map/ppermute | solution.py:191
  445.6 132.1 %collective-permute-start.1 = (bf16[512,2048]{1,0:T(8,128)(2,1)}, bf16[512,2048]{1,0:T(8,128)(2,1)}, u32[]{:S(2)}, u32[]{:S(2)}) collective-permute-start(bf16[512,2048]{1,0:T(8,128)(2,1)} %get-tuple-element.70), channel_id=1, source_target_pairs={{0,24},{8,0},{16,8},{24,16},{1,25},{9,1},{17,9},{25,17},{2,26},{10... | collective-permute-start | bytes 6291464 | tf_op jit(solution)/shard_map/ppermute | solution.py:191
  446.4 133.9 %collective-permute-start = (bf16[512,2048]{1,0:T(8,128)(2,1)}, bf16[512,2048]{1,0:T(8,128)(2,1)}, u32[]{:S(2)}, u32[]{:S(2)}) collective-permute-start(bf16[512,2048]{1,0:T(8,128)(2,1)} %get-tuple-element.70), channel_id=1, source_target_pairs={{0,8},{8,16},{16,24},{24,0},{1,9},{9,17},{17,25},{25,1},{2,10},{10... | collective-permute-start | bytes 6291464 | tf_op jit(solution)/shard_map/ppermute | solution.py:191
  486.7 19.8 %copy-start.12 = (f32[512]{0:T(512)S(1)}, f32[512]{0:T(512)}, u32[]{:S(2)}) copy-start(f32[512]{0:T(512)} %get-tuple-element.77) | copy-start | bytes 6148
  506.5 104.0 %collective-permute-start.4 = (bf16[512,2048]{1,0:T(8,128)(2,1)}, bf16[512,2048]{1,0:T(8,128)(2,1)}, u32[]{:S(2)}, u32[]{:S(2)}) collective-permute-start(bf16[512,2048]{1,0:T(8,128)(2,1)} %get-tuple-element.74), channel_id=1, source_target_pairs={{0,8},{8,16},{16,24},{24,0},{1,9},{9,17},{17,25},{25,1},{2,10},{10... | collective-permute-start | bytes 6291464 | tf_op jit(solution)/shard_map/ppermute | solution.py:191
  566.3 14.9 %copy-start = (bf16[2048,512]{0,1:T(8,128)(2,1)S(1)}, bf16[2048,512]{0,1:T(8,128)(2,1)}, u32[]{:S(2)}) copy-start(bf16[2048,512]{0,1:T(8,128)(2,1)} %dynamic-slice_bitcast_fusion.2) | copy-start | bytes 6291460
  577.7 94.3 %collective-permute-start.5 = (bf16[512,2048]{1,0:T(8,128)(2,1)}, bf16[512,2048]{1,0:T(8,128)(2,1)}, u32[]{:S(2)}, u32[]{:S(2)}) collective-permute-start(bf16[512,2048]{1,0:T(8,128)(2,1)} %get-tuple-element.74), channel_id=1, source_target_pairs={{0,24},{8,0},{16,8},{24,16},{1,25},{9,1},{17,9},{25,17},{2,26},{10... | collective-permute-start | bytes 6291464 | tf_op jit(solution)/shard_map/ppermute | solution.py:191
  580.3 88.2 %collective-permute-start.7 = (bf16[512,2048]{1,0:T(8,128)(2,1)}, bf16[512,2048]{1,0:T(8,128)(2,1)}, u32[]{:S(2)}, u32[]{:S(2)}) collective-permute-start(bf16[512,2048]{1,0:T(8,128)(2,1)} %get-tuple-element.76), channel_id=1, source_target_pairs={{0,24},{8,0},{16,8},{24,16},{1,25},{9,1},{17,9},{25,17},{2,26},{10... | collective-permute-start | bytes 6291464 | tf_op jit(solution)/shard_map/ppermute | solution.py:191
  592.0 14.8 %copy-start.15 = (bf16[512,2048]{1,0:T(8,128)(2,1)S(1)}, bf16[512,2048]{1,0:T(8,128)(2,1)}, u32[]{:S(2)}) copy-start(bf16[512,2048]{1,0:T(8,128)(2,1)} %get-tuple-element.76) | copy-start | bytes 6291460
  606.8 68.4 %collective-permute-start.6 = (bf16[512,2048]{1,0:T(8,128)(2,1)S(1)}, bf16[512,2048]{1,0:T(8,128)(2,1)S(1)}, u32[]{:S(2)}, u32[]{:S(2)}) collective-permute-start(bf16[512,2048]{1,0:T(8,128)(2,1)S(1)} %copy-done.15), channel_id=1, source_target_pairs={{0,8},{8,16},{16,24},{24,0},{1,9},{9,17},{17,25},{25,1},{2,10},{10... | collective-permute-start | bytes 6291464 | tf_op jit(solution)/shard_map/ppermute | solution.py:191
  610.6 86.8 %collective-permute-start.8 = (bf16[512,2048]{1,0:T(8,128)(2,1)}, bf16[512,2048]{1,0:T(8,128)(2,1)S(1)}, u32[]{:S(2)}, u32[]{:S(2)}) collective-permute-start(bf16[512,2048]{1,0:T(8,128)(2,1)} %collective-permute-done), channel_id=1, source_target_pairs={{0,8},{8,16},{16,24},{24,0},{1,9},{9,17},{17,25},{25,1},{2,10},{10... | collective-permute-start | bytes 6291464 | tf_op jit(solution)/shard_map/ppermute | solution.py:220
  610.6 131.7 %collective-permute-start.10 = (bf16[512,2048]{1,0:T(8,128)(2,1)}, bf16[512,2048]{1,0:T(8,128)(2,1)S(1)}, u32[]{:S(2)}, u32[]{:S(2)}) collective-permute-start(bf16[512,2048]{1,0:T(8,128)(2,1)} %collective-permute-done.4), channel_id=1, source_target_pairs={{0,8},{8,16},{16,24},{24,0},{1,9},{9,17},{17,25},{25,1},{2,10},{10... | collective-permute-start | bytes 6291464 | tf_op jit(solution)/shard_map/ppermute | solution.py:220
  668.6 45.9 %collective-permute-start.9 = (bf16[512,2048]{1,0:T(8,128)(2,1)}, bf16[512,2048]{1,0:T(8,128)(2,1)S(1)}, u32[]{:S(2)}, u32[]{:S(2)}) collective-permute-start(bf16[512,2048]{1,0:T(8,128)(2,1)} %collective-permute-done.3), channel_id=1, source_target_pairs={{0,24},{8,0},{16,8},{24,16},{1,25},{9,1},{17,9},{25,17},{2,26},{10... | collective-permute-start | bytes 6291464 | tf_op jit(solution)/shard_map/ppermute | solution.py:222
  672.0 87.4 %collective-permute-start.11 = (bf16[512,2048]{1,0:T(8,128)(2,1)}, bf16[512,2048]{1,0:T(8,128)(2,1)S(1)}, u32[]{:S(2)}, u32[]{:S(2)}) collective-permute-start(bf16[512,2048]{1,0:T(8,128)(2,1)} %collective-permute-done.7), channel_id=1, source_target_pairs={{0,24},{8,0},{16,8},{24,16},{1,25},{9,1},{17,9},{25,17},{2,26},{10... | collective-permute-start | bytes 6291464 | tf_op jit(solution)/shard_map/ppermute | solution.py:222
Sparse Core Ops, SparseCore 0:
  10.7 76.5 all-gather.8
  89.3 81.1 all-gather.4
  172.7 140.6 all-gather.6

commit v2 on v1

v2 whole, which is shorter than its diff:
```python
import functools
import math
import jax
import jax.numpy as jnp
from jax import lax
from jax.experimental import pallas as pl
from jax.experimental.pallas import tpu as pltpu
from jax.sharding import PartitionSpec as P

ROPE_BASE = 500000.0
ROPE_FACTOR = 8.0
LOW_FREQ = 1.0
HIGH_FREQ = 4.0
ORIG_CONTEXT = 8192.0
NORM_EPS = 1e-5
MASK_VALUE = -1e30
Q_TILE = 256
FF_TILE = 512
OUT_TILE = 512
ROW_TILE = 512
FIRST_SPLIT = (4, 4, 2)
LATER_SPLIT = (2, 2)


def inv_rms(x_in):
    x_wide = x_in.astype(jnp.float32)
    return lax.rsqrt(jnp.mean(x_wide * x_wide, axis=-1, keepdims=True) + NORM_EPS)


def scaled(x_in, inv_scale, gain_vec):
    return (x_in.astype(jnp.float32) * inv_scale * gain_vec.astype(jnp.float32)).astype(jnp.bfloat16)


def rope_tables(seq_len, head_dim):
    exponent = jnp.arange(head_dim // 2, dtype=jnp.float32) * (2.0 / head_dim)
    inv_freq = 1.0 / jnp.power(ROPE_BASE, exponent)
    wavelen = 2.0 * math.pi / inv_freq
    smooth = (ORIG_CONTEXT / wavelen - LOW_FREQ) / (HIGH_FREQ - LOW_FREQ)
    blended = (1.0 - smooth) * inv_freq / ROPE_FACTOR + smooth * inv_freq
    rope_freq = jnp.where(wavelen < ORIG_CONTEXT / HIGH_FREQ, inv_freq, jnp.where(wavelen > ORIG_CONTEXT / LOW_FREQ, inv_freq / ROPE_FACTOR, blended))
    angles = jnp.arange(seq_len, dtype=jnp.float32)[:, None] * rope_freq[None, :]
    return jnp.cos(angles), jnp.sin(angles)


def attention_kernel(head_dim, group_size, len_ref, qkv_ref, cos_ref, sin_ref, out_ref, kl_scr, kr_scr, vl_scr, vr_scr):
    seq_len = qkv_ref.shape[1]
    pair = 2 * head_dim
    length = len_ref[pl.program_id(0)]
    lane = lax.broadcasted_iota(jnp.int32, (1, pair), 1)
    low_lane = lane < head_dim
    first_half = lax.rem(lane, head_dim) < head_dim // 2
    one_low = jnp.where(lane == 0, 1.0, 0.0)
    one_high = jnp.where(lane == head_dim, 1.0, 0.0)

    def rope(vec, rows):
        ahead = pltpu.roll(vec, pair - head_dim // 2, 1)
        behind = pltpu.roll(vec, head_dim // 2, 1)
        return vec * cos_ref[rows, :] + jnp.where(first_half, ahead, behind) * sin_ref[rows, :]

    q_cols = group_size * head_dim
    for start in range(0, seq_len, Q_TILE):
        rows = pl.ds(start, Q_TILE)
        kv = qkv_ref[0, rows, q_cols:q_cols + pair].astype(jnp.float32)
        k_rot = rope(kv, rows)
        key_id = start + lax.broadcasted_iota(jnp.int32, (Q_TILE, pair), 0)
        bias = jnp.where(key_id < length, 0.0, MASK_VALUE)
        kl_scr[rows, :] = jnp.where(low_lane, k_rot, bias * one_high).astype(jnp.bfloat16)
        kr_scr[rows, :] = jnp.where(low_lane, bias * one_low, pltpu.roll(k_rot, head_dim, 1)).astype(jnp.bfloat16)
        vl_scr[rows, :] = jnp.where(low_lane, pltpu.roll(kv, head_dim, 1), 0.0).astype(jnp.bfloat16)
        vr_scr[rows, :] = jnp.where(low_lane, 0.0, kv).astype(jnp.bfloat16)

    for start in range(0, seq_len, Q_TILE):
        rows = pl.ds(start, Q_TILE)
        keys = start + Q_TILE
        causal = lax.broadcasted_iota(jnp.int32, (Q_TILE, Q_TILE), 1) <= lax.broadcasted_iota(jnp.int32, (Q_TILE, Q_TILE), 0)

        def weights(query, k_scr):
            scores = lax.dot_general(query, k_scr[:keys, :], (((1,), (1,)), ((), ())), preferred_element_type=jnp.float32)
            parts = [scores[:, block:block + Q_TILE] for block in range(0, keys, Q_TILE)]
            parts[-1] = jnp.where(causal, parts[-1], MASK_VALUE)
            top = parts[0]
            for part in parts[1:]:
                top = jnp.maximum(top, part)
            top = jnp.max(top, axis=1, keepdims=True)
            parts = [jnp.exp(part - top) for part in parts]
            total = parts[0]
            for part in parts[1:]:
                total = total + part
            scale = 1.0 / jnp.sum(total, axis=1, keepdims=True)
            return jnp.concatenate([(part * scale).astype(jnp.bfloat16) for part in parts], axis=1)

        def head_pair(index, carry):
            cols = pl.ds(pl.multiple_of(index * pair, pair), pair)
            query = rope(qkv_ref[0, rows, cols].astype(jnp.float32), rows).astype(jnp.bfloat16).astype(jnp.float32) * head_dim ** -0.5
            left = weights(jnp.where(low_lane, query, one_high).astype(jnp.bfloat16), kl_scr)
            right = weights(jnp.where(low_lane, one_low, query).astype(jnp.bfloat16), kr_scr)
            acc = jnp.dot(left, vl_scr[:keys, :], preferred_element_type=jnp.float32)
            acc = acc + jnp.dot(right, vr_scr[:keys, :], preferred_element_type=jnp.float32)
            out_ref[0, rows, cols] = acc.astype(jnp.bfloat16)
            return carry

        lax.fori_loop(0, group_size // 2, head_pair, 0, unroll=2)


def attention(qkv_act, lengths, cos_tab, sin_tab, kv_heads, head_dim):
    batch, seq_len, qkv_cols = qkv_act.shape
    group_cols = qkv_cols // kv_heads
    group_size = group_cols // head_dim - 2
    out_cols = group_size * head_dim
    pair = 2 * head_dim
    cos_pair = jnp.tile(cos_tab, (1, 4))
    sin_pair = jnp.tile(jnp.concatenate([-sin_tab, sin_tab], axis=1), (1, 2))
    flops = 2 * 2 * batch * kv_heads * group_size * seq_len * seq_len * head_dim
    return pl.pallas_call(
        functools.partial(attention_kernel, head_dim, group_size),
        out_shape=jax.ShapeDtypeStruct((batch, seq_len, kv_heads * out_cols), jnp.bfloat16),
        grid_spec=pltpu.PrefetchScalarGridSpec(
            num_scalar_prefetch=1,
            grid=(batch, kv_heads),
            in_specs=[
                pl.BlockSpec((1, seq_len, group_cols), lambda b, g, _: (b, 0, g)),
                pl.BlockSpec((seq_len, pair), lambda b, g, _: (0, 0)),
                pl.BlockSpec((seq_len, pair), lambda b, g, _: (0, 0)),
            ],
            out_specs=pl.BlockSpec((1, seq_len, out_cols), lambda b, g, _: (b, 0, g)),
            scratch_shapes=[pltpu.VMEM((seq_len, pair), jnp.bfloat16)] * 4,
        ),
        compiler_params=pltpu.CompilerParams(dimension_semantics=('arbitrary', 'arbitrary'), vmem_limit_bytes=48 * 1024 * 1024),
        cost_estimate=pl.CostEstimate(flops=4 * flops, bytes_accessed=2 * batch * seq_len * (qkv_cols + kv_heads * out_cols), transcendentals=batch * kv_heads * group_size * seq_len * seq_len),
        name='prefill_attention',
    )(lengths, qkv_act, cos_pair, sin_pair)


def empty(shape, dtype):
    return pl.pallas_call(lambda out_ref: None, out_shape=jax.ShapeDtypeStruct(shape, dtype), out_specs=pl.BlockSpec(memory_space=pl.ANY), name='output_buffer')()


def row_tiles(rows, body):
    tile = min(ROW_TILE, rows)

    def step(index, carry):
        body(pl.ds(pl.multiple_of(index * tile, tile), tile))
        return carry

    lax.fori_loop(0, rows // tile, step, 0)


def gate_up_kernel(h_ref, gain_ref, gate_ref, up_ref, mid_ref, norm_scr):
    rows = norm_scr.shape[0]
    contract = (((1,), (1,)), ((), ()))

    @pl.when(pl.program_id(0) == 0)
    def _():
        def step(index, carry):
            part = pl.ds(pl.multiple_of(index * 64, 64), 64)
            wide = h_ref[0, part, :].astype(jnp.float32)
            mean_sq = jnp.mean(wide * wide, axis=1, keepdims=True)
            norm_scr[part, :] = (wide * lax.rsqrt(mean_sq + NORM_EPS) * gain_ref[...].astype(jnp.float32)).astype(jnp.bfloat16)
            return carry

        lax.fori_loop(0, rows // 64, step, 0)

    def body(part):
        normed = norm_scr[part, :]
        gate = lax.dot_general(normed, gate_ref[0], contract, preferred_element_type=jnp.float32).astype(jnp.bfloat16).astype(jnp.float32)
        up = lax.dot_general(normed, up_ref[0], contract, preferred_element_type=jnp.float32).astype(jnp.bfloat16).astype(jnp.float32)
        mid_ref[part, :] = (jax.nn.silu(gate) * up).astype(jnp.bfloat16)

    row_tiles(rows, body)


def gate_up(hidden, gain, weights, slot, start, rows):
    dim = hidden.shape[2]
    ff = weights.shape[1]
    tile = min(FF_TILE, ff)
    return pl.pallas_call(
        gate_up_kernel,
        out_shape=jax.ShapeDtypeStruct((rows, ff), jnp.bfloat16),
        grid=(ff // tile,),
        in_specs=[
            pl.BlockSpec((1, rows, dim), lambda j: (slot, start // rows, 0)),
            pl.BlockSpec((1, dim), lambda j: (0, 0)),
            pl.BlockSpec((1, tile, dim), lambda j: (0, j, 0)),
            pl.BlockSpec((1, tile, dim), lambda j: (1, j, 0)),
        ],
        out_specs=pl.BlockSpec((rows, tile), lambda j: (0, j)),
        scratch_shapes=[pltpu.VMEM((rows, dim), jnp.bfloat16)],
        compiler_params=pltpu.CompilerParams(dimension_semantics=('arbitrary',), vmem_limit_bytes=56 * 1024 * 1024),
        cost_estimate=pl.CostEstimate(flops=4 * rows * dim * ff, bytes_accessed=4 * dim * ff + 2 * rows * (dim + ff), transcendentals=rows * ff),
        name='gate_up',
    )(hidden, gain[None, :], weights, weights)


def down_kernel(row_ref, h_ref, mid_ref, w_ref, y_in, y_ref, part_ref):
    def body(part):
        acc = jnp.dot(mid_ref[part, :], w_ref[0], preferred_element_type=jnp.float32)
        y_part = (h_ref[0, part, :].astype(jnp.float32) + acc).astype(jnp.bfloat16)
        part_ref[part, :] = y_part
        y_ref[0, 0, part, :] = y_part

    row_tiles(mid_ref.shape[0], body)


def down_proj(row, hidden, mid, weights, y_all, slot, start):
    rows, ff = mid.shape
    dim = hidden.shape[2]
    tile = min(OUT_TILE, dim)
    return pl.pallas_call(
        down_kernel,
        out_shape=(jax.ShapeDtypeStruct(y_all.shape, jnp.bfloat16), jax.ShapeDtypeStruct((rows, dim), jnp.bfloat16)),
        grid_spec=pltpu.PrefetchScalarGridSpec(
            num_scalar_prefetch=1,
            grid=(dim // tile,),
            in_specs=[
                pl.BlockSpec((1, rows, tile), lambda j, _: (slot, start // rows, j)),
                pl.BlockSpec((rows, ff), lambda j, _: (0, 0)),
                pl.BlockSpec((1, ff, tile), lambda j, _: (2, 0, j)),
                pl.BlockSpec(memory_space=pl.ANY),
            ],
            out_specs=(
                pl.BlockSpec((1, 1, rows, tile), lambda j, own: (slot, own[0], start // rows, j)),
                pl.BlockSpec((rows, tile), lambda j, _: (0, j)),
            ),
        ),
        input_output_aliases={4: 0},
        compiler_params=pltpu.CompilerParams(dimension_semantics=('arbitrary',), vmem_limit_bytes=56 * 1024 * 1024),
        cost_estimate=pl.CostEstimate(flops=2 * rows * dim * ff, bytes_accessed=2 * dim * ff + 2 * rows * (3 * dim + ff), transcendentals=0),
        name='down_proj',
    )(row, hidden, mid, weights, y_all)


def matmul_t(lhs, rhs_t):
    return lax.dot_general(lhs, rhs_t, (((lhs.ndim - 1,), (1,)), ((), ())), preferred_element_type=jnp.float32)


def solution(mesh):
    n_tpa = mesh.shape['tpa']
    n_tpb = mesh.shape['tpb']
    up_ring = [(i, (i + 1) % n_tpa) for i in range(n_tpa)]
    down_ring = [(i, (i - 1) % n_tpa) for i in range(n_tpa)]
    both = ('tpa', 'tpb')

    def layer_step(x_loc, len_loc, k_buf, v_buf, w_qkv, w_o, w_gate_up, w_down, g_attn, g_mlp):
        row = lax.axis_index('tpa')
        batch_loc, seq_len, model_dim = x_loc.shape
        head_dim = k_buf.shape[3]
        own_batch = batch_loc // n_tpa
        ff_block = w_gate_up.shape[1] // 2
        qkv_row = w_qkv.shape[1] * n_tpb
        o_row = w_o.shape[0] * n_tpb
        ff_row = ff_block * n_tpb

        qkv_block = w_qkv.shape[1]
        qkvo = lax.all_gather(jnp.concatenate([w_qkv.T, w_o], axis=0), both, axis=0, tiled=False)
        mlp_full = lax.all_gather(jnp.concatenate([w_gate_up.T.reshape(2, ff_block, model_dim), w_down[None]], axis=0), both, axis=1, tiled=True)
        qkv_t = qkvo[:, :qkv_block].reshape(-1, model_dim)

        cos_tab, sin_tab = rope_tables(seq_len, head_dim)
        x_own = lax.dynamic_index_in_dim(x_loc.reshape(own_batch, n_tpa, seq_len, model_dim), row, 1, keepdims=False)
        inv_all = inv_rms(x_loc)
        inv_own = lax.dynamic_index_in_dim(inv_all.reshape(own_batch, n_tpa, seq_len, 1), row, 1, keepdims=False)
        len_own = lax.dynamic_index_in_dim(len_loc.reshape(own_batch, n_tpa), row, 1, keepdims=False)

        qkv_act = matmul_t(scaled(x_own, inv_own, g_attn), qkv_t).astype(jnp.bfloat16)
        attn_out = attention(qkv_act, len_own, cos_tab, sin_tab, n_tpa * k_buf.shape[2], head_dim)
        attn_out, qkvo = lax.optimization_barrier((attn_out, qkvo))
        o_full = qkvo[:, qkv_block:].reshape(-1, model_dim)
        attn_proj = jnp.dot(attn_out, o_full, preferred_element_type=jnp.float32)
        hidden = (x_own.astype(jnp.float32) + attn_proj).astype(jnp.bfloat16)

        y_all = empty((own_batch, n_tpa, seq_len, model_dim), jnp.bfloat16)

        def put(y_buf, piece, slot, owner, start):
            return lax.dynamic_update_slice(y_buf, piece[None, None], (slot, lax.rem(owner + n_tpa, n_tpa), start, 0))

        spots = []
        for slot in range(own_batch):
            start = 0
            for share in FIRST_SPLIT if slot == 0 else LATER_SPLIT:
                spots.append((slot, start, seq_len // share))
                start += seq_len // share
        fars = []
        near = []
        upward = [0, 0]
        row_arg = row.astype(jnp.int32)[None]
        for slot, start, rows in spots:
            mid_act = gate_up(hidden, g_mlp, mlp_full, slot, start, rows)
            y_all, part = down_proj(row_arg, hidden, mid_act, mlp_full, y_all, slot, start)
            near.append((lax.ppermute(part, 'tpa', up_ring), lax.ppermute(part, 'tpa', down_ring)))

        y_all, x_late, qkvo_late, mlp_late = lax.optimization_barrier((y_all, x_loc, qkvo, mlp_full))
        kv_cols = k_buf.shape[2] * head_dim
        q_cols = qkv_row - 2 * kv_cols
        own_blocks = lax.dynamic_slice_in_dim(qkvo_late, row * n_tpb, n_tpb, 0)
        qkv_own = own_blocks[:, :qkv_block].reshape(qkv_row, model_dim)
        o_rows = own_blocks[:, qkv_block:].reshape(o_row, model_dim)
        w_query = qkv_own[:q_cols].T
        w_key = qkv_own[q_cols:q_cols + kv_cols].T
        w_value = qkv_own[q_cols + kv_cols:].T
        kv_new = matmul_t(scaled(x_late, inv_all, g_attn), qkv_own[q_cols:]).astype(jnp.bfloat16)
        half_dim = head_dim // 2
        k_first = kv_new[..., :half_dim].astype(jnp.float32)
        k_second = kv_new[..., half_dim:head_dim].astype(jnp.float32)
        k_rot = jnp.concatenate([k_first * cos_tab - k_second * sin_tab, k_second * cos_tab + k_first * sin_tab], axis=-1).astype(jnp.bfloat16)
        valid_pos = (jnp.arange(seq_len)[None, :] < len_loc[:, None])[:, :, None, None]
        k_cache = jnp.where(valid_pos, k_rot[:, :, None, :], k_buf)
        v_cache = jnp.where(valid_pos, kv_new[:, :, None, head_dim:], v_buf)
        mlp_own = lax.dynamic_slice_in_dim(mlp_late, row * ff_row, ff_row, 1)
        w_gate = mlp_own[0].T
        w_up = mlp_own[1].T
        down_rows = mlp_own[2]
        cache_outs = (k_cache, v_cache, w_query, w_key, w_value, o_rows)
        weight_outs = (w_gate, w_up, down_rows)
        near[-2], cache_outs = lax.optimization_barrier((near[-2], cache_outs))
        near[-1], weight_outs = lax.optimization_barrier((near[-1], weight_outs))
        k_cache, v_cache, w_query, w_key, w_value, o_rows = cache_outs
        w_gate, w_up, down_rows = weight_outs
        for (from_below, from_above), (slot, start, rows) in zip(near, spots):
            if upward[0] <= upward[1]:
                upward[0] += rows
                far = lax.ppermute(from_below, 'tpa', up_ring)
            else:
                upward[1] += rows
                far = lax.ppermute(from_above, 'tpa', down_ring)
            y_all = put(y_all, from_below, slot, row - 1, start)
            y_all = put(y_all, from_above, slot, row + 1, start)
            fars.append(far)
        for far, (slot, start, rows) in zip(fars, spots):
            y_all = put(y_all, far, slot, row - 2, start)
        layer_out = y_all.reshape(batch_loc, seq_len, model_dim)
        return (layer_out, k_cache, v_cache, w_query, w_key, w_value, o_rows, w_gate, w_up, down_rows)

    batch_spec = P(('part', 'tpb'), None, None)
    len_spec = P(('part', 'tpb'))
    cache_spec = P(('part', 'tpb'), None, 'tpa', None)
    train_cols = P('part', ('tpa', 'tpb'))
    train_rows = P(('part', 'tpa', 'tpb'), None)
    gain_spec = P('part')
    gen_cols = P('part', 'tpa')
    gen_rows = P(('part', 'tpa'), None)
    return jax.shard_map(layer_step, mesh=mesh, in_specs=(batch_spec, len_spec, cache_spec, cache_spec, train_cols, train_rows, train_cols, train_rows, gain_spec, gain_spec), out_specs=(batch_spec, cache_spec, cache_spec, gen_cols, gen_cols, gen_cols, gen_rows, gen_cols, gen_cols, gen_rows), check_vma=False)
```

time: 774 us -> 820 us (1.059)
  matrix products: 304 us -> 74.4 us
  Pallas kernels: 130 us -> 335 us
  waiting for transfers between devices: 182 us -> 244 us
    pallas_call x0 -> x10, Pallas kernels: none -> 223 us  [the longest x5 142 us: gate_up(): pl.pallas_call(gate_up_kernel, out_shape=jax.ShapeDtypeStruct((rows, ff),...]
    dot_general x10 -> x2, matrix products: 205 us -> 49 us  [matmul_t(): lax.dot_general(lhs, rhs_t, (((lhs.ndim - 1,), (1,)), ((), ())), preferre...]
    dot_general x4 -> x0, matrix products: 76.1 us -> none  [layer_step(): mlp_out = jnp.dot(mid_act, down_use, preferred_element_type=jnp.float32)]
    ppermute x4 -> x5, waiting for transfers between devices: 51.4 us -> 107 us  [layer_step(): lax.ppermute(part, 'tpa', down_ring)]
    ppermute x2, waiting for transfers between devices: 31.2 us -> 0.01 us  [layer_step(): far = lax.ppermute(from_above, 'tpa', down_ring)]
    pallas_call x1, Pallas kernels: 130 us -> 113 us  [attention(): pl.pallas_call(functools.partial(attention_kernel, head_dim, group_size),...]
    all_gather x2 -> x1, waiting for transfers between devices: 0.01 us -> 15.4 us  [layer_step(): lax.all_gather(jnp.concatenate([w_gate_up.T.reshape(2, ff_block, model_di...]
    ppermute x2 -> x3, waiting for transfers between devices: 44 us -> 59.2 us  [layer_step(): far = lax.ppermute(from_below, 'tpa', up_ring)]
  transfers between devices with their start and end apart: 15 -> 17, of which waited for: 6 -> 7; matrix products, arithmetic and copies ran while one was open for 40% -> 23% of each run, Pallas kernels for 17% -> 37%
where the time goes in v2:
time: 820 us; the launch traced here: 809 us
  Pallas kernels  335 us (41%)
  waiting for transfers between devices  244 us (30%)
  local copies, waits for them, and re-layouts  98.1 us (12%)
  matrix products  74.4 us (9%)
  other arithmetic  23.8 us (3%)
  starting transfers between devices  19.2 us (2%)
  between operations  14.7 us (2%)
    pallas_call x5, Pallas kernels, gate_up(): pl.pallas_call(gate_up_kernel, out_shape=jax.ShapeDtypeStruct((rows, ff),...  142 us
    pallas_call x1, Pallas kernels, attention(): pl.pallas_call(functools.partial(attention_kernel, head_dim, group_size),...  113 us
    ppermute x5, waiting for transfers between devices, layer_step(): lax.ppermute(part, 'tpa', down_ring)  107 us
    pallas_call x5, Pallas kernels, down_proj(): pl.pallas_call(down_kernel, out_shape=(jax.ShapeDtypeStruct(y_all.shape,...  80.2 us
    ppermute x3, waiting for transfers between devices, layer_step(): far = lax.ppermute(from_below, 'tpa', up_ring)  59.2 us
    all_gather x1, waiting for transfers between devices, layer_step(): lax.all_gather(jnp.concatenate([w_qkv.T, w_o], axis=0), both, axis=0, til...  59.1 us
    dot_general x2, matrix products, matmul_t(): lax.dot_general(lhs, rhs_t, (((lhs.ndim - 1,), (1,)), ((), ())), preferre...  49 us
    dynamic_update_slice x15, local copies, waits for them, and re-layouts, put(): lax.dynamic_update_slice(y_buf, piece[None, None], (slot, lax.rem(owner +...  34.3 us
  transfers between devices with their start and end apart: 17, of which 7 were waited for; matrix products, arithmetic and copies ran while one was open for 23% of the time, Pallas kernels for 37%

profile of v2, /device:TPU:97, one launch (start us, length us, event | category | flops | bytes accessed | tf_op | source)
XLA Modules:
  0.0 809.3 jit_solution(6771996577939520671)
XLA Ops:
  7.3 1.9 pad_maximum_fusion.1
  9.3 3.1 pad_maximum_fusion
  12.6 11.8 %multiply_reduce_fusion = f32[8,1024]{1,0:T(8,128)S(1)} fusion(bf16[8,1024,2048]{2,1,0:T(8,128)(2,1)} %param.10), kind=kLoop, calls=%fused_computation.1 | loop fusion | flops 50323456 | bytes 33587200 | tf_op jit(solution)/shard_map/reduce_sum | solution.py:27
  28.2 59.1 %all-gather.6.cloned.1.call-done = bf16[4608,2048]{1,0:T(8,128)(2,1)} async-done(((bf16[144,2048]{1,0:T(8,128)(2,1)}), bf16[4608,2048]{1,0:T(8,128)(2,1)}) %all-gather.6.cloned.1.call-update) | async-done | bytes 18874384 | tf_op jit(solution)/shard_map/all_gather | solution.py:254
  87.3 10.8 %slice.56 = bf16[32,80,2048]{2,1,0:T(8,128)(2,1)} slice(bf16[32,144,2048]{2,1,0:T(8,128)(2,1)} %bitcast.110), slice={[0:32], [0:80], [0:2048]} | slice | bytes 20971520 | tf_op jit(solution)/shard_map/slice | solution.py:256
  98.1 30.4 %fusion.13.qkv_ref = bf16[2,1024,2560]{2,1,0:T(8,128)(2,1)} fusion(bf16[2560,2048,1]{1,0,2:T(8,128)(2,1)} %bitcast.114, f32[2048]{0:T(1024)S(1)} %convert_element_type.56, f32[2,1024]{1,0:T(2,128)S(1)} %bitcast.127, bf16[2,4,1024,2048]{3,2,1,0:T(8,128)(2,1)} %bitcast.108, s32[]{:T(128)S(6)} %select_n.81), kind=kOutput, calls=%fused_computation.16 | convolution fusion | flops 21496856576 | bytes 29376516 | tf_op jit(solution)/shard_map/dot_general | solution.py:233
  128.5 112.7 %prefill_attention.1 = bf16[2,1024,2048]{2,1,0:T(8,128)(2,1)} custom-call(s32[2]{0:T(128)S(1)} %fusion.29.len_ref, bf16[2,1024,2560]{2,1,0:T(8,128)(2,1)} %fusion.13.qkv_ref, f32[1024,128]{1,0:T(8,128)S(1)} %copy.37.cos_ref, f32[1024,128]{1,0:T(8,128)S(1)} %copy.38.sin_ref), custom_call_target="tpu_custom_call" | custom-call | flops 68719476736 | bytes 18874368 | tf_op jit(solution)/shard_map/prefill_attention/pallas_call | solution.py:114
  241.2 8.7 %slice.43 = bf16[32,64,2048]{2,1,0:T(8,128)(2,1)} slice(bf16[32,144,2048]{2,1,0:T(8,128)(2,1)} %bitcast.111), slice={[0:32], [80:144], [0:2048]} | slice | bytes 16777216 | tf_op jit(solution)/shard_map/slice | solution.py:267
  249.9 25.4 %fusion.4.h_ref = bf16[2,1024,2048]{2,1,0:T(8,128)(2,1)} fusion(bf16[2,4,1024,2048]{3,2,1,0:T(8,128)(2,1)} %bitcast.109, s32[]{:T(128)S(6)} %select_n.81, bf16[2,1024,2048]{2,1,0:T(8,128)(2,1)} %prefill_attention.1, bf16[2048,2048,1]{1,0,2:T(8,128)(2,1)} %bitcast.118), kind=kOutput, calls=%fused_computation.8 | convolution fusion | flops 17192452096 | bytes 33554436 | tf_op jit(solution)/shard_map/dot_general | solution.py:268
  275.3 15.4 %all-gather.4.cloned.1.call-done.gate_ref.up_ref.w_ref = bf16[3,5632,2048]{2,1,0:T(8,128)(2,1)} async-done(((bf16[3,176,2048]{2,1,0:T(8,128)(2,1)}), bf16[3,5632,2048]{2,1,0:T(8,128)(2,1)}) %all-gather.4.cloned.1.call-update) | async-done | bytes 69206032 | tf_op jit(solution)/shard_map/all_gather | solution.py:255
  290.7 23.8 %gate_up.9.mid_ref = bf16[256,5632]{1,0:T(8,128)(2,1)} custom-call(bf16[2,1024,2048]{2,1,0:T(8,128)(2,1)} %fusion.4.h_ref, bf16[1,2048]{1,0:T(2,128)(2,1)} %broadcast_in_dim.86.gain_ref, bf16[3,5632,2048]{2,1,0:T(8,128)(2,1)} %all-gather.4.cloned.1.call-done.gate_ref.up_ref.w_ref, bf16[3,5632,2048]{2,1,0:T(8,128)(2,1)} %all-gather.4.cloned.1.call-done.gate_ref.up_ref.w_ref), custom_call_target="tpu_custom_call" | custom-call | flops 11811160064 | bytes 50069504 | tf_op jit(solution)/shard_map/gate_up/pallas_call | solution.py:176
  314.6 12.9 %down_proj.5 = (bf16[2,4,1024,2048]{3,2,1,0:T(8,128)(2,1)}, bf16[256,2048]{1,0:T(8,128)(2,1)}) custom-call(s32[1]{0:T(128)} %bitcast.row_ref, bf16[2,1024,2048]{2,1,0:T(8,128)(2,1)} %fusion.4.h_ref, bf16[256,5632]{1,0:T(8,128)(2,1)} %gate_up.9.mid_ref, ...), custom_call_target="tpu_custom_call", output_to_operand_aliasing={{0}: (4, {})} | custom-call | flops 5905580032 | bytes 29097984 | tf_op jit(solution)/shard_map/down_proj/pallas_call | solution.py:208
  327.4 2.7 collective-permute-start.1
  330.1 23.7 %gate_up.8.mid_ref = bf16[256,5632]{1,0:T(8,128)(2,1)} custom-call(bf16[2,1024,2048]{2,1,0:T(8,128)(2,1)} %fusion.4.h_ref, bf16[1,2048]{1,0:T(2,128)(2,1)} %broadcast_in_dim.86.gain_ref, bf16[3,5632,2048]{2,1,0:T(8,128)(2,1)} %all-gather.4.cloned.1.call-done.gate_ref.up_ref.w_ref, bf16[3,5632,2048]{2,1,0:T(8,128)(2,1)} %all-gather.4.cloned.1.call-done.gate_ref.up_ref.w_ref), custom_call_target="tpu_custom_call" | custom-call | flops 11811160064 | bytes 50069504 | tf_op jit(solution)/shard_map/gate_up/pallas_call | solution.py:176
  353.8 12.8 %down_proj.6 = (bf16[2,4,1024,2048]{3,2,1,0:T(8,128)(2,1)}, bf16[256,2048]{1,0:T(8,128)(2,1)}) custom-call(s32[1]{0:T(128)} %bitcast.row_ref, bf16[2,1024,2048]{2,1,0:T(8,128)(2,1)} %fusion.4.h_ref, bf16[256,5632]{1,0:T(8,128)(2,1)} %gate_up.8.mid_ref, ...), custom_call_target="tpu_custom_call", output_to_operand_aliasing={{0}: (4, {})} | custom-call | flops 5905580032 | bytes 29097984 | tf_op jit(solution)/shard_map/down_proj/pallas_call | solution.py:208
  366.6 2.7 collective-permute-start.3
  369.3 31.6 %gate_up.7.mid_ref = bf16[512,5632]{1,0:T(8,128)(2,1)} custom-call(bf16[2,1024,2048]{2,1,0:T(8,128)(2,1)} %fusion.4.h_ref, bf16[1,2048]{1,0:T(2,128)(2,1)} %broadcast_in_dim.86.gain_ref, bf16[3,5632,2048]{2,1,0:T(8,128)(2,1)} %all-gather.4.cloned.1.call-done.gate_ref.up_ref.w_ref, bf16[3,5632,2048]{2,1,0:T(8,128)(2,1)} %all-gather.4.cloned.1.call-done.gate_ref.up_ref.w_ref), custom_call_target="tpu_custom_call" | custom-call | flops 23622320128 | bytes 54001664 | tf_op jit(solution)/shard_map/gate_up/pallas_call | solution.py:176
  400.9 31.6 %gate_up.6.mid_ref = bf16[512,5632]{1,0:T(8,128)(2,1)} custom-call(bf16[2,1024,2048]{2,1,0:T(8,128)(2,1)} %fusion.4.h_ref, bf16[1,2048]{1,0:T(2,128)(2,1)} %broadcast_in_dim.86.gain_ref, bf16[3,5632,2048]{2,1,0:T(8,128)(2,1)} %all-gather.4.cloned.1.call-done.gate_ref.up_ref.w_ref, bf16[3,5632,2048]{2,1,0:T(8,128)(2,1)} %all-gather.4.cloned.1.call-done.gate_ref.up_ref.w_ref), custom_call_target="tpu_custom_call" | custom-call | flops 23622320128 | bytes 54001664 | tf_op jit(solution)/shard_map/gate_up/pallas_call | solution.py:176
  432.6 31.6 %gate_up.5.mid_ref = bf16[512,5632]{1,0:T(8,128)(2,1)} custom-call(bf16[2,1024,2048]{2,1,0:T(8,128)(2,1)} %fusion.4.h_ref, bf16[1,2048]{1,0:T(2,128)(2,1)} %broadcast_in_dim.86.gain_ref, bf16[3,5632,2048]{2,1,0:T(8,128)(2,1)} %all-gather.4.cloned.1.call-done.gate_ref.up_ref.w_ref, bf16[3,5632,2048]{2,1,0:T(8,128)(2,1)} %all-gather.4.cloned.1.call-done.gate_ref.up_ref.w_ref), custom_call_target="tpu_custom_call" | custom-call | flops 23622320128 | bytes 54001664 | tf_op jit(solution)/shard_map/gate_up/pallas_call | solution.py:176
  464.2 18.2 %down_proj.7 = (bf16[2,4,1024,2048]{3,2,1,0:T(8,128)(2,1)}, bf16[512,2048]{1,0:T(8,128)(2,1)}) custom-call(s32[1]{0:T(128)} %bitcast.row_ref, bf16[2,1024,2048]{2,1,0:T(8,128)(2,1)} %fusion.4.h_ref, bf16[512,5632]{1,0:T(8,128)(2,1)} %gate_up.7.mid_ref, ...), custom_call_target="tpu_custom_call", output_to_operand_aliasing={{0}: (4, {})} | custom-call | flops 11811160064 | bytes 35127296 | tf_op jit(solution)/shard_map/down_proj/pallas_call | solution.py:208
  482.4 18.2 %down_proj.8 = (bf16[2,4,1024,2048]{3,2,1,0:T(8,128)(2,1)}, bf16[512,2048]{1,0:T(8,128)(2,1)}) custom-call(s32[1]{0:T(128)} %bitcast.row_ref, bf16[2,1024,2048]{2,1,0:T(8,128)(2,1)} %fusion.4.h_ref, bf16[512,5632]{1,0:T(8,128)(2,1)} %gate_up.6.mid_ref, ...), custom_call_target="tpu_custom_call", output_to_operand_aliasing={{0}: (4, {})} | custom-call | flops 11811160064 | bytes 35127296 | tf_op jit(solution)/shard_map/down_proj/pallas_call | solution.py:208
  500.5 18.2 %down_proj.9 = (bf16[2,4,1024,2048]{3,2,1,0:T(8,128)(2,1)}, bf16[512,2048]{1,0:T(8,128)(2,1)}) custom-call(s32[1]{0:T(128)} %bitcast.row_ref, bf16[2,1024,2048]{2,1,0:T(8,128)(2,1)} %fusion.4.h_ref, bf16[512,5632]{1,0:T(8,128)(2,1)} %gate_up.5.mid_ref, ...), custom_call_target="tpu_custom_call", output_to_operand_aliasing={{0}: (4, {})} | custom-call | flops 11811160064 | bytes 35127296 | tf_op jit(solution)/shard_map/down_proj/pallas_call | solution.py:208
  521.5 18.6 %fusion.17 = bf16[8,1024,128]{1,2,0:T(8,128)(2,1)} fusion(bf16[8,1024,2048]{2,1,0:T(8,128)(2,1)} %param.10, f32[2048]{0:T(1024)S(1)} %copy-done.11, f32[8,1024]{1,0:T(8,128)S(1)} %copy-done.8, bf16[640,2048]{1,0:T(8,128)(2,1)S(1)} %bitcast.116), kind=kOutput, calls=%fused_computation.32 | convolution fusion | flops 4363124736 | bytes 36216832 | tf_op jit(solution)/shard_map/dot_general | solution.py:233
  541.7 4.2 fusion.22
  547.3 15.0 %dynamic-slice_bitcast_fusion = (bf16[1408,2048]{1,0:T(8,128)(2,1)}, bf16[2048,1408]{0,1:T(8,128)(2,1)}, bf16[2048,1408]{0,1:T(8,128)(2,1)}) fusion(bf16[3,5632,2048]{2,1,0:T(8,128)(2,1)} %all-gather.4.cloned.1.call-done.gate_ref.up_ref.w_ref, s32[]{:T(128)S(6)} %add.135, s32[]{:T(128)S(6)} %select_n.89, s32[]{:T(128)S(6)} %add.134), kind=kLoop, calls=%fused_computation.18 | loop fusion | bytes 34603020 | tf_op jit(solution)/shard_map/squeeze | solution.py:311
  562.4 2.7 collective-permute-start.9
  565.1 2.7 collective-permute-start.7
  567.8 3.2 constant_dynamic-slice_fusion.1
  571.0 2.7 collective-permute-start.5
  573.7 2.3 bitcast_dynamic-update-slice_fusion.14
  576.0 2.3 bitcast_dynamic-update-slice_fusion.13
  578.3 2.3 bitcast_dynamic-update-slice_fusion.12
  580.6 2.3 bitcast_dynamic-update-slice_fusion.11
  582.9 25.6 %collective-permute-done.9 = bf16[512,2048]{1,0:T(8,128)(2,1)S(1)} collective-permute-done((bf16[512,2048]{1,0:T(8,128)(2,1)S(1)}, bf16[512,2048]{1,0:T(8,128)(2,1)S(1)}, u32[]{:S(2)}, u32[]{:S(2)}) %collective-permute-start.9) | collective-permute-done | bytes 2097184 | tf_op jit(solution)/shard_map/ppermute | solution.py:289
  608.5 3.1 collective-permute-done.6
  612.0 41.4 %collective-permute-done.7 = bf16[512,2048]{1,0:T(8,128)(2,1)} collective-permute-done((bf16[512,2048]{1,0:T(8,128)(2,1)S(1)}, bf16[512,2048]{1,0:T(8,128)(2,1)}, u32[]{:S(2)}, u32[]{:S(2)}) %collective-permute-start.7) | collective-permute-done | bytes 2097184 | tf_op jit(solution)/shard_map/ppermute | solution.py:289
  653.4 3.5 collective-permute-start.13
  658.5 39.8 %collective-permute-done.5 = bf16[512,2048]{1,0:T(8,128)(2,1)S(1)} collective-permute-done((bf16[512,2048]{1,0:T(8,128)(2,1)S(1)}, bf16[512,2048]{1,0:T(8,128)(2,1)S(1)}, u32[]{:S(2)}, u32[]{:S(2)}) %collective-permute-start.5) | collective-permute-done | bytes 2097184 | tf_op jit(solution)/shard_map/ppermute | solution.py:289
  701.2 3.2 bitcast_dynamic-update-slice_fusion.5
  704.4 8.5 %copy.44 = bf16[2048,1408]{1,0:T(8,128)(2,1)} copy(bf16[2048,1408]{0,1:T(8,128)(2,1)} %get-tuple-element.85) | data formatting | bytes 11534336
  712.9 8.3 %copy.45 = bf16[2048,1408]{1,0:T(8,128)(2,1)} copy(bf16[2048,1408]{0,1:T(8,128)(2,1)} %get-tuple-element.86) | data formatting | bytes 11534336
  721.2 2.5 copy.43
  725.4 3.2 bitcast_dynamic-update-slice_fusion.4
  728.6 3.2 bitcast_dynamic-update-slice_fusion.3
  732.8 2.3 bitcast_dynamic-update-slice_fusion.9
  735.1 59.2 %collective-permute-done.12 = bf16[512,2048]{1,0:T(8,128)(2,1)S(1)} collective-permute-done((bf16[512,2048]{1,0:T(8,128)(2,1)}, bf16[512,2048]{1,0:T(8,128)(2,1)S(1)}, u32[]{:S(2)}, u32[]{:S(2)}) %collective-permute-start.12) | collective-permute-done | bytes 2097184 | tf_op jit(solution)/shard_map/ppermute | solution.py:321
  795.8 3.2 bitcast_dynamic-update-slice_fusion.1
  799.0 3.2 bitcast_dynamic-update-slice_fusion
  (85 shorter events, 19.0 us)
Async XLA Ops:
  7.2 80.1 %all-gather.6.cloned.1.call-start = ((), (), s32[]{:S(2)}) async-start(), calls=%async_computation.1 | async-start | bytes 19464192 | tf_op jit(solution)/shard_map/all_gather | solution.py:254
  9.2 281.5 %all-gather.4.cloned.1.call-start = ((), (), s32[]{:S(2)}) async-start(), calls=%async_computation | async-start | bytes 71368704 | tf_op jit(solution)/shard_map/all_gather | solution.py:255
  12.5 11.9 %copy-start.12 = (bf16[2048]{0:T(1024)(128)(2,1)S(1)}, bf16[2048]{0:T(1024)(128)(2,1)}, u32[]{:S(2)}) copy-start(bf16[2048]{0:T(1024)(128)(2,1)} %param.18) | copy-start | bytes 12292
  12.5 12.4 %copy-start.14 = (s32[8]{0:T(128)S(1)}, s32[8]{0:T(128)}, u32[]{:S(2)}) copy-start(s32[8]{0:T(128)} %param.11) | copy-start | bytes 100
  12.5 14.4 %copy-start.13 = (bf16[2048]{0:T(1024)(128)(2,1)S(1)}, bf16[2048]{0:T(1024)(128)(2,1)}, u32[]{:S(2)}) copy-start(bf16[2048]{0:T(1024)(128)(2,1)} %param.19) | copy-start | bytes 12292
  24.3 0.6 copy-start.7
  24.9 73.2 %copy-start.10 = (f32[2048]{0:T(1024)}, f32[2048]{0:T(1024)S(1)}, u32[]{:S(2)}) copy-start(f32[2048]{0:T(1024)S(1)} %convert_element_type.56) | copy-start | bytes 24580
  25.8 0.7 copy-start.5
  25.8 72.3 %copy-start.3 = (f32[1024,32]{0,1:T(8,128)}, f32[1024,32]{0,1:T(8,128)S(1)}, u32[]{:S(2)}) copy-start(f32[1024,32]{0,1:T(8,128)S(1)} %get-tuple-element.99) | copy-start | bytes 393220
  327.4 234.9 %collective-permute-start = (bf16[256,2048]{1,0:T(8,128)(2,1)}, bf16[256,2048]{1,0:T(8,128)(2,1)}, u32[]{:S(2)}, u32[]{:S(2)}) collective-permute-start(bf16[256,2048]{1,0:T(8,128)(2,1)} %get-tuple-element.47), channel_id=1, source_target_pairs={{0,8},{8,16},{16,24},{24,0},{1,9},{9,17},{17,25},{25,1},{2,10},{10... | collective-permute-start | bytes 3145736 | tf_op jit(solution)/shard_map/ppermute | solution.py:289
  327.4 237.7 %collective-permute-start.1 = (bf16[256,2048]{1,0:T(8,128)(2,1)}, bf16[256,2048]{1,0:T(8,128)(2,1)}, u32[]{:S(2)}, u32[]{:S(2)}) collective-permute-start(bf16[256,2048]{1,0:T(8,128)(2,1)} %get-tuple-element.47), channel_id=1, source_target_pairs={{0,24},{8,0},{16,8},{24,16},{1,25},{9,1},{17,9},{25,17},{2,26},{10... | collective-permute-start | bytes 3145736 | tf_op jit(solution)/shard_map/ppermute | solution.py:289
  366.6 198.5 %collective-permute-start.2 = (bf16[256,2048]{1,0:T(8,128)(2,1)}, bf16[256,2048]{1,0:T(8,128)(2,1)}, u32[]{:S(2)}, u32[]{:S(2)}) collective-permute-start(bf16[256,2048]{1,0:T(8,128)(2,1)} %get-tuple-element.48), channel_id=1, source_target_pairs={{0,8},{8,16},{16,24},{24,0},{1,9},{9,17},{17,25},{25,1},{2,10},{10... | collective-permute-start | bytes 3145736 | tf_op jit(solution)/shard_map/ppermute | solution.py:289
  366.6 201.2 %collective-permute-start.3 = (bf16[256,2048]{1,0:T(8,128)(2,1)}, bf16[256,2048]{1,0:T(8,128)(2,1)}, u32[]{:S(2)}, u32[]{:S(2)}) collective-permute-start(bf16[256,2048]{1,0:T(8,128)(2,1)} %get-tuple-element.48), channel_id=1, source_target_pairs={{0,24},{8,0},{16,8},{24,16},{1,25},{9,1},{17,9},{25,17},{2,26},{10... | collective-permute-start | bytes 3145736 | tf_op jit(solution)/shard_map/ppermute | solution.py:289
  500.5 20.9 %copy-start.8 = (f32[8,1024]{1,0:T(8,128)S(1)}, f32[8,1024]{1,0:T(8,128)}, u32[]{:S(2)}) copy-start(f32[8,1024]{1,0:T(8,128)} %copy-done.7) | copy-start | bytes 98308
  500.5 20.9 %copy-start.11 = (f32[2048]{0:T(1024)S(1)}, f32[2048]{0:T(1024)}, u32[]{:S(2)}) copy-start(f32[2048]{0:T(1024)} %copy-done.10) | copy-start | bytes 24580
  518.7 52.3 %collective-permute-start.8 = (bf16[512,2048]{1,0:T(8,128)(2,1)}, bf16[512,2048]{1,0:T(8,128)(2,1)}, u32[]{:S(2)}, u32[]{:S(2)}) collective-permute-start(bf16[512,2048]{1,0:T(8,128)(2,1)} %get-tuple-element.55), channel_id=1, source_target_pairs={{0,8},{8,16},{16,24},{24,0},{1,9},{9,17},{17,25},{25,1},{2,10},{10... | collective-permute-start | bytes 6291464 | tf_op jit(solution)/shard_map/ppermute | solution.py:289
  521.5 18.6 %copy-start.4 = (f32[1024,32]{0,1:T(8,128)S(1)}, f32[1024,32]{0,1:T(8,128)}, u32[]{:S(2)}) copy-start(f32[1024,32]{0,1:T(8,128)} %copy-done.3) | copy-start | bytes 393220
  521.5 18.6 %copy-start.6 = (f32[1024,32]{0,1:T(8,128)S(1)}, f32[1024,32]{0,1:T(8,128)}, u32[]{:S(2)}) copy-start(f32[1024,32]{0,1:T(8,128)} %copy-done.5) | copy-start | bytes 393220
  521.5 20.2 %copy-start.9 = (pred[8,1024]{1,0:T(8,128)(4,1)S(1)}, pred[8,1024]{1,0:T(8,128)(4,1)}, u32[]{:S(2)}) copy-start(pred[8,1024]{1,0:T(8,128)(4,1)} %iota_compare_fusion) | copy-start | bytes 24580
  547.3 15.0 %copy-start.17 = (bf16[512,2048]{1,0:T(8,128)(2,1)S(1)}, bf16[512,2048]{1,0:T(8,128)(2,1)}, u32[]{:S(2)}) copy-start(bf16[512,2048]{1,0:T(8,128)(2,1)} %get-tuple-element.55) | copy-start | bytes 6291460
  547.3 17.8 %copy-start.16 = (bf16[512,2048]{1,0:T(8,128)(2,1)S(1)}, bf16[512,2048]{1,0:T(8,128)(2,1)}, u32[]{:S(2)}) copy-start(bf16[512,2048]{1,0:T(8,128)(2,1)} %get-tuple-element.50) | copy-start | bytes 6291460
  547.3 20.5 %copy-start.15 = (bf16[512,2048]{1,0:T(8,128)(2,1)S(1)}, bf16[512,2048]{1,0:T(8,128)(2,1)}, u32[]{:S(2)}) copy-start(bf16[512,2048]{1,0:T(8,128)(2,1)} %get-tuple-element.49) | copy-start | bytes 6291460
  562.4 46.1 %collective-permute-start.9 = (bf16[512,2048]{1,0:T(8,128)(2,1)S(1)}, bf16[512,2048]{1,0:T(8,128)(2,1)S(1)}, u32[]{:S(2)}, u32[]{:S(2)}) collective-permute-start(bf16[512,2048]{1,0:T(8,128)(2,1)S(1)} %copy-done.17), channel_id=1, source_target_pairs={{0,24},{8,0},{16,8},{24,16},{1,25},{9,1},{17,9},{25,17},{2,26},{10... | collective-permute-start | bytes 6291464 | tf_op jit(solution)/shard_map/ppermute | solution.py:289
  565.1 46.5 %collective-permute-start.6 = (bf16[512,2048]{1,0:T(8,128)(2,1)S(1)}, bf16[512,2048]{1,0:T(8,128)(2,1)S(1)}, u32[]{:S(2)}, u32[]{:S(2)}) collective-permute-start(bf16[512,2048]{1,0:T(8,128)(2,1)S(1)} %copy-done.16), channel_id=1, source_target_pairs={{0,8},{8,16},{16,24},{24,0},{1,9},{9,17},{17,25},{25,1},{2,10},{10... | collective-permute-start | bytes 6291464 | tf_op jit(solution)/shard_map/ppermute | solution.py:289
  565.1 88.2 %collective-permute-start.7 = (bf16[512,2048]{1,0:T(8,128)(2,1)S(1)}, bf16[512,2048]{1,0:T(8,128)(2,1)}, u32[]{:S(2)}, u32[]{:S(2)}) collective-permute-start(bf16[512,2048]{1,0:T(8,128)(2,1)S(1)} %copy-done.16), channel_id=1, source_target_pairs={{0,24},{8,0},{16,8},{24,16},{1,25},{9,1},{17,9},{25,17},{2,26},{10... | collective-permute-start | bytes 6291464 | tf_op jit(solution)/shard_map/ppermute | solution.py:289
  567.8 89.1 %collective-permute-start.4 = (bf16[512,2048]{1,0:T(8,128)(2,1)S(1)}, bf16[512,2048]{1,0:T(8,128)(2,1)S(1)}, u32[]{:S(2)}, u32[]{:S(2)}) collective-permute-start(bf16[512,2048]{1,0:T(8,128)(2,1)S(1)} %copy-done.15), channel_id=1, source_target_pairs={{0,8},{8,16},{16,24},{24,0},{1,9},{9,17},{17,25},{25,1},{2,10},{10... | collective-permute-start | bytes 6291464 | tf_op jit(solution)/shard_map/ppermute | solution.py:289
  571.0 127.3 %collective-permute-start.5 = (bf16[512,2048]{1,0:T(8,128)(2,1)S(1)}, bf16[512,2048]{1,0:T(8,128)(2,1)S(1)}, u32[]{:S(2)}, u32[]{:S(2)}) collective-permute-start(bf16[512,2048]{1,0:T(8,128)(2,1)S(1)} %copy-done.15), channel_id=1, source_target_pairs={{0,24},{8,0},{16,8},{24,16},{1,25},{9,1},{17,9},{25,17},{2,26},{10... | collective-permute-start | bytes 6291464 | tf_op jit(solution)/shard_map/ppermute | solution.py:289
  608.4 92.8 %copy-start.1 = (bf16[512,2048]{1,0:T(8,128)(2,1)}, bf16[512,2048]{1,0:T(8,128)(2,1)S(1)}, u32[]{:S(2)}) copy-start(bf16[512,2048]{1,0:T(8,128)(2,1)S(1)} %collective-permute-done.9) | copy-start | bytes 6291460
  608.4 123.3 %collective-permute-start.10 = (bf16[256,2048]{1,0:T(8,128)(2,1)}, bf16[256,2048]{1,0:T(8,128)(2,1)S(1)}, u32[]{:S(2)}, u32[]{:S(2)}) collective-permute-start(bf16[256,2048]{1,0:T(8,128)(2,1)} %collective-permute-done), channel_id=1, source_target_pairs={{0,8},{8,16},{16,24},{24,0},{1,9},{9,17},{17,25},{25,1},{2,10},{10... | collective-permute-start | bytes 3145736 | tf_op jit(solution)/shard_map/ppermute | solution.py:321
  611.6 121.2 %collective-permute-start.11 = (bf16[256,2048]{1,0:T(8,128)(2,1)}, bf16[256,2048]{1,0:T(8,128)(2,1)}, u32[]{:S(2)}, u32[]{:S(2)}) collective-permute-start(bf16[256,2048]{1,0:T(8,128)(2,1)} %collective-permute-done.3), channel_id=1, source_target_pairs={{0,24},{8,0},{16,8},{24,16},{1,25},{9,1},{17,9},{25,17},{2,26},{10... | collective-permute-start | bytes 3145736 | tf_op jit(solution)/shard_map/ppermute | solution.py:324
  653.4 142.4 %collective-permute-start.13 = (bf16[512,2048]{1,0:T(8,128)(2,1)}, bf16[512,2048]{1,0:T(8,128)(2,1)}, u32[]{:S(2)}, u32[]{:S(2)}) collective-permute-start(bf16[512,2048]{1,0:T(8,128)(2,1)} %collective-permute-done.7), channel_id=1, source_target_pairs={{0,24},{8,0},{16,8},{24,16},{1,25},{9,1},{17,9},{25,17},{2,26},{10... | collective-permute-start | bytes 6291464 | tf_op jit(solution)/shard_map/ppermute | solution.py:324
  656.9 47.5 %copy-start.2 = (bf16[512,2048]{1,0:T(8,128)(2,1)}, bf16[512,2048]{1,0:T(8,128)(2,1)S(1)}, u32[]{:S(2)}) copy-start(bf16[512,2048]{1,0:T(8,128)(2,1)S(1)} %collective-permute-done.4) | copy-start | bytes 6291460
  704.4 16.8 %copy-start = (bf16[2048,512]{0,1:T(8,128)(2,1)S(1)}, bf16[2048,512]{0,1:T(8,128)(2,1)}, u32[]{:S(2)}) copy-start(bf16[2048,512]{0,1:T(8,128)(2,1)} %slice_bitcast_fusion) | copy-start | bytes 6291460
  704.4 94.6 %collective-permute-start.14 = (bf16[512,2048]{1,0:T(8,128)(2,1)}, bf16[512,2048]{1,0:T(8,128)(2,1)}, u32[]{:S(2)}, u32[]{:S(2)}) collective-permute-start(bf16[512,2048]{1,0:T(8,128)(2,1)} %collective-permute-done.8), channel_id=1, source_target_pairs={{0,8},{8,16},{16,24},{24,0},{1,9},{9,17},{17,25},{25,1},{2,10},{10... | collective-permute-start | bytes 6291464 | tf_op jit(solution)/shard_map/ppermute | solution.py:321
  723.7 70.6 %collective-permute-start.12 = (bf16[512,2048]{1,0:T(8,128)(2,1)}, bf16[512,2048]{1,0:T(8,128)(2,1)S(1)}, u32[]{:S(2)}, u32[]{:S(2)}) collective-permute-start(bf16[512,2048]{1,0:T(8,128)(2,1)} %copy-done.2), channel_id=1, source_target_pairs={{0,8},{8,16},{16,24},{24,0},{1,9},{9,17},{17,25},{25,1},{2,10},{10... | collective-permute-start | bytes 6291464 | tf_op jit(solution)/shard_map/ppermute | solution.py:321
Sparse Core Ops, SparseCore 0:
  10.7 76.5 all-gather.5
  90.0 200.7 all-gather.3

commit v3 on v2

--- a/solution.py
+++ b/solution.py
@@ -17,7 +17,7 @@
 Q_TILE = 256
 FF_TILE = 512
 OUT_TILE = 512
-ROW_TILE = 512
+NT_DIMS = (((1,), (1,)), ((), ()))
 FIRST_SPLIT = (4, 4, 2)
 LATER_SPLIT = (2, 2)
 
@@ -135,98 +135,212 @@
     return pl.pallas_call(lambda out_ref: None, out_shape=jax.ShapeDtypeStruct(shape, dtype), out_specs=pl.BlockSpec(memory_space=pl.ANY), name='output_buffer')()
 
 
-def row_tiles(rows, body):
-    tile = min(ROW_TILE, rows)
-
+def normalise(src, gain, dst, rows):
     def step(index, carry):
-        body(pl.ds(pl.multiple_of(index * tile, tile), tile))
+        part = pl.ds(pl.multiple_of(index * 64, 64), 64)
+        wide = src[part, :].astype(jnp.float32)
+        mean_sq = jnp.mean(wide * wide, axis=1, keepdims=True)
+        dst[part, :] = (wide * lax.rsqrt(mean_sq + NORM_EPS) * gain).astype(jnp.bfloat16)
         return carry
 
-    lax.fori_loop(0, rows // tile, step, 0)
-
-
-def gate_up_kernel(h_ref, gain_ref, gate_ref, up_ref, mid_ref, norm_scr):
-    rows = norm_scr.shape[0]
-    contract = (((1,), (1,)), ((), ()))
-
-    @pl.when(pl.program_id(0) == 0)
-    def _():
-        def step(index, carry):
-            part = pl.ds(pl.multiple_of(index * 64, 64), 64)
-            wide = h_ref[0, part, :].astype(jnp.float32)
-            mean_sq = jnp.mean(wide * wide, axis=1, keepdims=True)
-            norm_scr[part, :] = (wide * lax.rsqrt(mean_sq + NORM_EPS) * gain_ref[...].astype(jnp.float32)).astype(jnp.bfloat16)
-            return carry
-
-        lax.fori_loop(0, rows // 64, step, 0)
-
-    def body(part):
-        normed = norm_scr[part, :]
-        gate = lax.dot_general(normed, gate_ref[0], contract, preferred_element_type=jnp.float32).astype(jnp.bfloat16).astype(jnp.float32)
-        up = lax.dot_general(normed, up_ref[0], contract, preferred_element_type=jnp.float32).astype(jnp.bfloat16).astype(jnp.float32)
-        mid_ref[part, :] = (jax.nn.silu(gate) * up).astype(jnp.bfloat16)
-
-    row_tiles(rows, body)
-
-
-def gate_up(hidden, gain, weights, slot, start, rows):
+    lax.fori_loop(0, rows // 64, step, 0)
+
+
+def mlp_kernel(slot, start, row_ref, h_ref, gain_ref, w_ref, y_in, y_ref, part_ref, h_scr, u_scr, acc_scr, mid_scr, gu_buf, down_buf, gu_sem, down_sem, h_sem, out_sem):
+    rows, dim = h_scr.shape
+    depth, _, tile, _ = gu_buf.shape
+    steps = w_ref.shape[1] // tile
+    out_tile = min(OUT_TILE, dim)
+
+    def gu_copy(step):
+        return pltpu.make_async_copy(w_ref.at[0:2, pl.ds(pl.multiple_of(step * tile, tile), tile), :], gu_buf.at[lax.rem(step, depth)], gu_sem.at[lax.rem(step, depth)])
+
+    def down_copy(step):
+        return pltpu.make_async_copy(w_ref.at[2, pl.ds(pl.multiple_of(step * tile, tile), tile), :], down_buf.at[lax.rem(step, depth)], down_sem.at[lax.rem(step, depth)])
+
+    h_copy = pltpu.make_async_copy(h_ref.at[slot, pl.ds(start, rows), :], h_scr, h_sem)
+    h_copy.start()
+    for step in range(min(depth - 1, steps)):
+        gu_copy(step).start()
+    for step in range(min(depth - 2, steps)):
+        down_copy(step).start()
+    mid_scr[...] = jnp.zeros_like(mid_scr)
+    h_copy.wait()
+    normalise(h_scr, gain_ref[...].astype(jnp.float32), u_scr, rows)
+
+    def widen(index, carry):
+        part = pl.ds(pl.multiple_of(index * 64, 64), 64)
+        acc_scr[part, :] = h_scr[part, :].astype(jnp.float32)
+        return carry
+
+    lax.fori_loop(0, rows // 64, widen, 0)
+
+    def add_down(index):
+        for col in range(0, dim, out_tile):
+            cols = slice(col, col + out_tile)
+            acc_scr[:, cols] += jnp.dot(mid_scr[...], down_buf[index, :, cols], preferred_element_type=jnp.float32)
+
+    def body(step, carry):
+        @pl.when(step + depth - 1 < steps)
+        def _():
+            gu_copy(step + depth - 1).start()
+
+        @pl.when(step + depth - 2 < steps)
+        def _():
+            down_copy(step + depth - 2).start()
+
+        gu_copy(step).wait()
+        before = jnp.maximum(step - 1, 0)
+
+        @pl.when(step != 1)
+        def _():
+            down_copy(before).wait()
+
+        index = lax.rem(step, depth)
+        gate = lax.dot_general(u_scr[...], gu_buf[index, 0], NT_DIMS, preferred_element_type=jnp.float32)
+        up = lax.dot_general(u_scr[...], gu_buf[index, 1], NT_DIMS, preferred_element_type=jnp.float32)
+        add_down(lax.rem(before, depth))
+        gate = gate.astype(jnp.bfloat16).astype(jnp.float32)
+        up = up.astype(jnp.bfloat16).astype(jnp.float32)
+        mid_scr[...] = (jax.nn.silu(gate) * up).astype(jnp.bfloat16)
+        return carry
+
+    lax.fori_loop(0, steps, body, 0)
+    if steps > 1:
+        down_copy(steps - 1).wait()
+    add_down((steps - 1) % depth)
+
+    def narrow(index, carry):
+        part = pl.ds(pl.multiple_of(index * 64, 64), 64)
+        h_scr[part, :] = acc_scr[part, :].astype(jnp.bfloat16)
+        return carry
+
+    lax.fori_loop(0, rows // 64, narrow, 0)
+    part_out = pltpu.make_async_copy(h_scr, part_ref, out_sem.at[0])
+    y_out = pltpu.make_async_copy(h_scr, y_ref.at[slot, row_ref[0], pl.ds(start, rows), :], out_sem.at[1])
+    part_out.start()
+    y_out.start()
+    part_out.wait()
+    y_out.wait()
+
+
+def mlp(row, hidden, gain, weights, y_all, slot, start, rows):
     dim = hidden.shape[2]
     ff = weights.shape[1]
     tile = min(FF_TILE, ff)
+    depth = 3
+    anywhere = pl.BlockSpec(memory_space=pl.ANY)
     return pl.pallas_call(
-        gate_up_kernel,
-        out_shape=jax.ShapeDtypeStruct((rows, ff), jnp.bfloat16),
-        grid=(ff // tile,),
-        in_specs=[
-            pl.BlockSpec((1, rows, dim), lambda j: (slot, start // rows, 0)),
-            pl.BlockSpec((1, dim), lambda j: (0, 0)),
-            pl.BlockSpec((1, tile, dim), lambda j: (0, j, 0)),
-            pl.BlockSpec((1, tile, dim), lambda j: (1, j, 0)),
+        functools.partial(mlp_kernel, slot, start),
+        out_shape=(jax.ShapeDtypeStruct(y_all.shape, jnp.bfloat16), jax.ShapeDtypeStruct((rows, dim), jnp.bfloat16)),
+        in_specs=[pl.BlockSpec(memory_space=pltpu.SMEM), anywhere, pl.BlockSpec(memory_space=pltpu.VMEM), anywhere, anywhere],
+        out_specs=(anywhere, anywhere),
+        scratch_shapes=[
+            pltpu.VMEM((rows, dim), jnp.bfloat16),
+            pltpu.VMEM((rows, dim), jnp.bfloat16),
+            pltpu.VMEM((rows, dim), jnp.float32),
+            pltpu.VMEM((rows, tile), jnp.bfloat16),
+            pltpu.VMEM((depth, 2, tile, dim), jnp.bfloat16),
+            pltpu.VMEM((depth, tile, dim), jnp.bfloat16),
+            pltpu.SemaphoreType.DMA((depth,)),
+            pltpu.SemaphoreType.DMA((depth,)),
+            pltpu.SemaphoreType.DMA,
+            pltpu.SemaphoreType.DMA((2,)),
         ],
-        out_specs=pl.BlockSpec((rows, tile), lambda j: (0, j)),
-        scratch_shapes=[pltpu.VMEM((rows, dim), jnp.bfloat16)],
-        compiler_params=pltpu.CompilerParams(dimension_semantics=('arbitrary',), vmem_limit_bytes=56 * 1024 * 1024),
-        cost_estimate=pl.CostEstimate(flops=4 * rows * dim * ff, bytes_accessed=4 * dim * ff + 2 * rows * (dim + ff), transcendentals=rows * ff),
-        name='gate_up',
-    )(hidden, gain[None, :], weights, weights)
-
-
-def down_kernel(row_ref, h_ref, mid_ref, w_ref, y_in, y_ref, part_ref):
-    def body(part):
-        acc = jnp.dot(mid_ref[part, :], w_ref[0], preferred_element_type=jnp.float32)
-        y_part = (h_ref[0, part, :].astype(jnp.float32) + acc).astype(jnp.bfloat16)
-        part_ref[part, :] = y_part
-        y_ref[0, 0, part, :] = y_part
-
-    row_tiles(mid_ref.shape[0], body)
-
-
-def down_proj(row, hidden, mid, weights, y_all, slot, start):
-    rows, ff = mid.shape
-    dim = hidden.shape[2]
-    tile = min(OUT_TILE, dim)
+        input_output_aliases={4: 0},
+        compiler_params=pltpu.CompilerParams(vmem_limit_bytes=58 * 1024 * 1024),
+        cost_estimate=pl.CostEstimate(flops=6 * rows * dim * ff, bytes_accessed=6 * dim * ff + 8 * rows * dim, transcendentals=rows * ff),
+        name='mlp_block',
+    )(row, hidden, gain[None, :], weights, y_all)
+
+
+def qkv_kernel(qkv_block, row_ref, x_ref, gain_ref, w_ref, out_ref, u_scr, w_scr):
+    piece, tile = pl.program_id(0), pl.program_id(1)
+    rows = x_ref.shape[2]
+
+    @pl.when(tile == 0)
+    def _():
+        for block in range(w_ref.shape[0]):
+            w_scr[block * qkv_block:(block + 1) * qkv_block, :] = w_ref[block, :qkv_block, :]
+
+    @pl.when(piece == 0)
+    def _():
+        normalise(x_ref.at[0, 0], gain_ref[...].astype(jnp.float32), u_scr.at[tile], rows)
+
+    out_ref[0] = lax.dot_general(u_scr[tile], w_scr[...], NT_DIMS, preferred_element_type=jnp.float32).astype(jnp.bfloat16)
+
+
+def qkv_proj(row, x_rows, gain, qkvo, qkv_block, pieces):
+    own_batch, _, seq_len, dim = x_rows.shape
+    blocks = qkvo.shape[0] // pieces
+    rows = min(512, seq_len)
+    per = seq_len // rows
+    tiles = own_batch * per
+    cols = blocks * qkv_block
+
+    def x_index(piece, tile, own):
+        at = jnp.where(piece == 0, tile, tiles - 1)
+        return (at // per, own[0], at % per, 0)
+
     return pl.pallas_call(
-        down_kernel,
-        out_shape=(jax.ShapeDtypeStruct(y_all.shape, jnp.bfloat16), jax.ShapeDtypeStruct((rows, dim), jnp.bfloat16)),
+        functools.partial(qkv_kernel, qkv_block),
+        out_shape=jax.ShapeDtypeStruct((own_batch, seq_len, pieces * cols), jnp.bfloat16),
         grid_spec=pltpu.PrefetchScalarGridSpec(
             num_scalar_prefetch=1,
-            grid=(dim // tile,),
+            grid=(pieces, tiles),
             in_specs=[
-                pl.BlockSpec((1, rows, tile), lambda j, _: (slot, start // rows, j)),
-                pl.BlockSpec((rows, ff), lambda j, _: (0, 0)),
-                pl.BlockSpec((1, ff, tile), lambda j, _: (2, 0, j)),
+                pl.BlockSpec((1, 1, rows, dim), x_index),
+                pl.BlockSpec((1, dim), lambda p, t, _: (0, 0)),
+                pl.BlockSpec((blocks,) + qkvo.shape[1:], lambda p, t, _: (p, 0, 0)),
+            ],
+            out_specs=pl.BlockSpec((1, rows, cols), lambda p, t, _: (t // per, t % per, p)),
+            scratch_shapes=[pltpu.VMEM((tiles, rows, dim), jnp.bfloat16), pltpu.VMEM((cols, dim), jnp.bfloat16)],
+        ),
+        compiler_params=pltpu.CompilerParams(dimension_semantics=('arbitrary', 'arbitrary'), vmem_limit_bytes=60 * 1024 * 1024),
+        cost_estimate=pl.CostEstimate(flops=2 * own_batch * seq_len * dim * pieces * cols, bytes_accessed=2 * dim * (pieces * cols + 2 * own_batch * seq_len), transcendentals=0),
+        name='qkv_proj',
+    )(row, x_rows, gain[None, :], qkvo)
+
+
+def out_kernel(qkv_block, row_ref, a_ref, x_ref, w_ref, h_ref, w_scr, sem):
+    @pl.when(pl.program_id(0) == 0)
+    def _():
+        copy = pltpu.make_async_copy(w_ref.at[:, pl.ds(qkv_block, w_scr.shape[1]), :], w_scr, sem)
+        copy.start()
+        copy.wait()
+
+    dim = h_ref.shape[2]
+    depth = w_scr.shape[0] * w_scr.shape[1]
+    out_tile = min(OUT_TILE, dim)
+    for col in range(0, dim, out_tile):
+        cols = slice(col, col + out_tile)
+        acc = jnp.dot(a_ref[0], w_scr[:, :, cols].reshape(depth, out_tile), preferred_element_type=jnp.float32)
+        h_ref[0, :, cols] = (x_ref[0, 0, :, cols].astype(jnp.float32) + acc).astype(jnp.bfloat16)
+
+
+def out_proj(row, attn, x_rows, qkvo, qkv_block):
+    own_batch, seq_len, depth = attn.shape
+    dim = x_rows.shape[3]
+    rows = min(512, seq_len)
+    per = seq_len // rows
+    return pl.pallas_call(
+        functools.partial(out_kernel, qkv_block),
+        out_shape=jax.ShapeDtypeStruct((own_batch, seq_len, dim), jnp.bfloat16),
+        grid_spec=pltpu.PrefetchScalarGridSpec(
+            num_scalar_prefetch=1,
+            grid=(own_batch * per,),
+            in_specs=[
+                pl.BlockSpec((1, rows, depth), lambda t, _: (t // per, t % per, 0)),
+                pl.BlockSpec((1, 1, rows, dim), lambda t, own: (t // per, own[0], t % per, 0)),
                 pl.BlockSpec(memory_space=pl.ANY),
             ],
-            out_specs=(
-                pl.BlockSpec((1, 1, rows, tile), lambda j, own: (slot, own[0], start // rows, j)),
-                pl.BlockSpec((rows, tile), lambda j, _: (0, j)),
-            ),
+            out_specs=pl.BlockSpec((1, rows, dim), lambda t, _: (t // per, t % per, 0)),
+            scratch_shapes=[pltpu.VMEM((qkvo.shape[0], qkvo.shape[1] - qkv_block, dim), jnp.bfloat16), pltpu.SemaphoreType.DMA],
         ),
-        input_output_aliases={4: 0},
         compiler_params=pltpu.CompilerParams(dimension_semantics=('arbitrary',), vmem_limit_bytes=56 * 1024 * 1024),
-        cost_estimate=pl.CostEstimate(flops=2 * rows * dim * ff, bytes_accessed=2 * dim * ff + 2 * rows * (3 * dim + ff), transcendentals=0),
-        name='down_proj',
-    )(row, hidden, mid, weights, y_all)
+        cost_estimate=pl.CostEstimate(flops=2 * own_batch * seq_len * dim * depth, bytes_accessed=2 * dim * (depth + 3 * own_batch * seq_len), transcendentals=0),
+        name='out_proj',
+    )(row, attn, x_rows, qkvo)
 
 
 def matmul_t(lhs, rhs_t):
@@ -253,42 +367,17 @@
         qkv_block = w_qkv.shape[1]
         qkvo = lax.all_gather(jnp.concatenate([w_qkv.T, w_o], axis=0), both, axis=0, tiled=False)
         mlp_full = lax.all_gather(jnp.concatenate([w_gate_up.T.reshape(2, ff_block, model_dim), w_down[None]], axis=0), both, axis=1, tiled=True)
-        qkv_t = qkvo[:, :qkv_block].reshape(-1, model_dim)
-
+        row_arg = row.astype(jnp.int32)[None]
         cos_tab, sin_tab = rope_tables(seq_len, head_dim)
-        x_own = lax.dynamic_index_in_dim(x_loc.reshape(own_batch, n_tpa, seq_len, model_dim), row, 1, keepdims=False)
+        x_rows = x_loc.reshape(own_batch, n_tpa, seq_len, model_dim)
         inv_all = inv_rms(x_loc)
-        inv_own = lax.dynamic_index_in_dim(inv_all.reshape(own_batch, n_tpa, seq_len, 1), row, 1, keepdims=False)
         len_own = lax.dynamic_index_in_dim(len_loc.reshape(own_batch, n_tpa), row, 1, keepdims=False)
 
-        qkv_act = matmul_t(scaled(x_own, inv_own, g_attn), qkv_t).astype(jnp.bfloat16)
+        qkv_act = qkv_proj(row_arg, x_rows, g_attn, qkvo, qkv_block, 2)
         attn_out = attention(qkv_act, len_own, cos_tab, sin_tab, n_tpa * k_buf.shape[2], head_dim)
-        attn_out, qkvo = lax.optimization_barrier((attn_out, qkvo))
-        o_full = qkvo[:, qkv_block:].reshape(-1, model_dim)
-        attn_proj = jnp.dot(attn_out, o_full, preferred_element_type=jnp.float32)
-        hidden = (x_own.astype(jnp.float32) + attn_proj).astype(jnp.bfloat16)
-
-        y_all = empty((own_batch, n_tpa, seq_len, model_dim), jnp.bfloat16)
-
-        def put(y_buf, piece, slot, owner, start):
-            return lax.dynamic_update_slice(y_buf, piece[None, None], (slot, lax.rem(owner + n_tpa, n_tpa), start, 0))
-
-        spots = []
-        for slot in range(own_batch):
-            start = 0
-            for share in FIRST_SPLIT if slot == 0 else LATER_SPLIT:
-                spots.append((slot, start, seq_len // share))
-                start += seq_len // share
-        fars = []
-        near = []
-        upward = [0, 0]
-        row_arg = row.astype(jnp.int32)[None]
-        for slot, start, rows in spots:
-            mid_act = gate_up(hidden, g_mlp, mlp_full, slot, start, rows)
-            y_all, part = down_proj(row_arg, hidden, mid_act, mlp_full, y_all, slot, start)
-            near.append((lax.ppermute(part, 'tpa', up_ring), lax.ppermute(part, 'tpa', down_ring)))
-
-        y_all, x_late, qkvo_late, mlp_late = lax.optimization_barrier((y_all, x_loc, qkvo, mlp_full))
+        hidden = out_proj(row_arg, attn_out, x_rows, qkvo, qkv_block)
+
+        hidden, x_late, qkvo_late = lax.optimization_barrier((hidden, x_loc, qkvo))
         kv_cols = k_buf.shape[2] * head_dim
         q_cols = qkv_row - 2 * kv_cols
         own_blocks = lax.dynamic_slice_in_dim(qkvo_late, row * n_tpb, n_tpb, 0)
@@ -305,16 +394,34 @@
         valid_pos = (jnp.arange(seq_len)[None, :] < len_loc[:, None])[:, :, None, None]
         k_cache = jnp.where(valid_pos, k_rot[:, :, None, :], k_buf)
         v_cache = jnp.where(valid_pos, kv_new[:, :, None, head_dim:], v_buf)
+        cache_outs = (k_cache, v_cache, w_query, w_key, w_value, o_rows)
+        mlp_full, cache_outs = lax.optimization_barrier((mlp_full, cache_outs))
+        k_cache, v_cache, w_query, w_key, w_value, o_rows = cache_outs
+
+        y_all = empty((own_batch, n_tpa, seq_len, model_dim), jnp.bfloat16)
+
+        def put(y_buf, piece, slot, owner, start):
+            return lax.dynamic_update_slice(y_buf, piece[None, None], (slot, lax.rem(owner + n_tpa, n_tpa), start, 0))
+
+        spots = []
+        for slot in range(own_batch):
+            start = 0
+            for share in FIRST_SPLIT if slot == 0 else LATER_SPLIT:
+                spots.append((slot, start, seq_len // share))
+                start += seq_len // share
+        fars = []
+        near = []
+        upward = [0, 0]
+        for slot, start, rows in spots:
+            y_all, part = mlp(row_arg, hidden, g_mlp, mlp_full, y_all, slot, start, rows)
+            near.append((lax.ppermute(part, 'tpa', up_ring), lax.ppermute(part, 'tpa', down_ring)))
+
+        y_all, mlp_late = lax.optimization_barrier((y_all, mlp_full))
         mlp_own = lax.dynamic_slice_in_dim(mlp_late, row * ff_row, ff_row, 1)
         w_gate = mlp_own[0].T
         w_up = mlp_own[1].T
         down_rows = mlp_own[2]
-        cache_outs = (k_cache, v_cache, w_query, w_key, w_value, o_rows)
-        weight_outs = (w_gate, w_up, down_rows)
-        near[-2], cache_outs = lax.optimization_barrier((near[-2], cache_outs))
-        near[-1], weight_outs = lax.optimization_barrier((near[-1], weight_outs))
-        k_cache, v_cache, w_query, w_key, w_value, o_rows = cache_outs
-        w_gate, w_up, down_rows = weight_outs
+        near[-1], (w_gate, w_up, down_rows) = lax.optimization_barrier((near[-1], (w_gate, w_up, down_rows)))
         for (from_below, from_above), (slot, start, rows) in zip(near, spots):
             if upward[0] <= upward[1]:
                 upward[0] += rows

time: 820 us -> 791 us (0.965)
  matrix products: 74.4 us -> 19.1 us
  Pallas kernels: 335 us -> 374 us
  local copies, waits for them, and re-layouts: 98.1 us -> 76.1 us
  waiting for transfers between devices: 244 us -> 258 us
    ppermute x5, waiting for transfers between devices: 107 us -> 0.59 us  [layer_step(): lax.ppermute(part, 'tpa', down_ring)]
    ppermute x5, waiting for transfers between devices: 3.14 us -> 104 us  [layer_step(): lax.ppermute(part, 'tpa', up_ring)]
    pallas_call x10 -> x7, Pallas kernels: 223 us -> 262 us  [the longest x5 201 us: mlp(): pl.pallas_call(functools.partial(mlp_kernel, slot, start), out_shape=(jax...]
    ppermute x3, waiting for transfers between devices: 59.2 us -> 95.3 us  [layer_step(): far = lax.ppermute(from_below, 'tpa', up_ring)]
    dot_general x2 -> x1, matrix products: 49 us -> 19.1 us  [matmul_t(): lax.dot_general(lhs, rhs_t, (((lhs.ndim - 1,), (1,)), ((), ())), preferre...]
    dot_general x1 -> x0, matrix products: 25.4 us -> none  [layer_step(): attn_proj = jnp.dot(attn_out, o_full, preferred_element_type=jnp.float32)]
    slice x2 -> x0, local copies, waits for them, and re-layouts: 19.5 us -> none  [the longest x1 10.8 us: layer_step(): qkv_t = qkvo[:, :qkv_block].reshape(-1, model_dim)]
    all_gather x1, waiting for transfers between devices: 15.4 us -> 0.01 us  [layer_step(): lax.all_gather(jnp.concatenate([w_gate_up.T.reshape(2, ff_block, model_di...]
  transfers between devices with their start and end apart: 17 -> 17, of which waited for: 7 -> 7; matrix products, arithmetic and copies ran while one was open for 23% -> 15% of each run, Pallas kernels for 37% -> 44%
where the time goes in v3:
time: 791 us; the launch traced here: 781 us
  Pallas kernels  374 us (47%)
  waiting for transfers between devices  258 us (33%)
  local copies, waits for them, and re-layouts  76.1 us (10%)
  other arithmetic  24.8 us (3%)
  matrix products  19.1 us (2%)
  starting transfers between devices  15 us (2%)
  between operations  14.5 us (2%)
    pallas_call x5, Pallas kernels, mlp(): pl.pallas_call(functools.partial(mlp_kernel, slot, start), out_shape=(jax...  201 us
    pallas_call x1, Pallas kernels, attention(): pl.pallas_call(functools.partial(attention_kernel, head_dim, group_size),...  112 us
    ppermute x5, waiting for transfers between devices, layer_step(): lax.ppermute(part, 'tpa', up_ring)  104 us
    ppermute x3, waiting for transfers between devices, layer_step(): far = lax.ppermute(from_below, 'tpa', up_ring)  95.3 us
    all_gather x1, waiting for transfers between devices, layer_step(): lax.all_gather(jnp.concatenate([w_qkv.T, w_o], axis=0), both, axis=0, til...  58.7 us
    pallas_call x1, Pallas kernels, qkv_proj(): pl.pallas_call(functools.partial(qkv_kernel, qkv_block), out_shape=jax.Sh...  35.3 us
    dynamic_update_slice x15, local copies, waits for them, and re-layouts, put(): lax.dynamic_update_slice(y_buf, piece[None, None], (slot, lax.rem(owner +...  32.9 us
    pallas_call x1, Pallas kernels, out_proj(): pl.pallas_call(functools.partial(out_kernel, qkv_block), out_shape=jax.Sh...  26 us
  transfers between devices with their start and end apart: 17, of which 7 were waited for; matrix products, arithmetic and copies ran while one was open for 15% of the time, Pallas kernels for 44%

profile of v3, /device:TPU:97, one launch (start us, length us, event | category | flops | bytes accessed | tf_op | source)
XLA Modules:
  0.0 781.4 jit_solution(5464029038660227490)
XLA Ops:
  7.3 1.9 pad_maximum_fusion.1
  9.3 3.1 pad_maximum_fusion
  12.5 1.3 broadcast_in_dim.88.gain_ref
  16.6 12.0 %multiply_reduce_fusion = f32[8,1024]{1,0:T(8,128)S(1)} fusion(bf16[8,1024,2048]{2,1,0:T(8,128)(2,1)} %param.10), kind=kLoop, calls=%fused_computation.1 | loop fusion | flops 50323456 | bytes 33587200 | tf_op jit(solution)/shard_map/reduce_sum | solution.py:27
  28.6 58.7 %all-gather.6.cloned.1.call-done = bf16[4608,2048]{1,0:T(8,128)(2,1)} async-done(((bf16[144,2048]{1,0:T(8,128)(2,1)}), bf16[4608,2048]{1,0:T(8,128)(2,1)}) %all-gather.6.cloned.1.call-update) | async-done | bytes 18874384 | tf_op jit(solution)/shard_map/all_gather | solution.py:368
  87.3 35.3 %qkv_proj.1.qkv_ref = bf16[2,1024,2560]{2,1,0:T(8,128)(2,1)} custom-call(s32[1]{0:T(128)} %bitcast.row_ref, bf16[2,4,1024,2048]{3,2,1,0:T(8,128)(2,1)} %bitcast.77, bf16[1,2048]{1,0:T(2,128)(2,1)} %broadcast_in_dim.88.gain_ref, bf16[32,144,2048]{2,1,0:T(8,128)(2,1)} %bitcast.79), custom_call_target="tpu_custom_call" | custom-call | flops 21474836480 | bytes 27262976 | tf_op jit(solution)/shard_map/qkv_proj/pallas_call | solution.py:285
  122.5 111.6 %prefill_attention.1.a_ref = bf16[2,1024,2048]{2,1,0:T(8,128)(2,1)} custom-call(s32[2]{0:T(128)S(1)} %fusion.14.len_ref, bf16[2,1024,2560]{2,1,0:T(8,128)(2,1)} %qkv_proj.1.qkv_ref, f32[1024,128]{1,0:T(8,128)S(1)} %copy.34.cos_ref, f32[1024,128]{1,0:T(8,128)S(1)} %copy.35.sin_ref), custom_call_target="tpu_custom_call" | custom-call | flops 68719476736 | bytes 18874368 | tf_op jit(solution)/shard_map/prefill_attention/pallas_call | solution.py:114
  234.1 26.0 %out_proj.1.h_ref = bf16[2,1024,2048]{2,1,0:T(8,128)(2,1)} custom-call(s32[1]{0:T(128)} %bitcast.row_ref, bf16[2,1024,2048]{2,1,0:T(8,128)(2,1)} %prefill_attention.1.a_ref, bf16[2,4,1024,2048]{3,2,1,0:T(8,128)(2,1)} %bitcast.78, bf16[32,144,2048]{2,1,0:T(8,128)(2,1)} %bitcast.80), custom_call_target="tpu_custom_call" | custom-call | flops 17179869184 | bytes 33554432 | tf_op jit(solution)/shard_map/out_proj/pallas_call | solution.py:326
  260.1 1.9 constant_dynamic-slice_fusion
  262.1 19.1 %fusion.3 = bf16[8,1024,128]{1,2,0:T(8,128)(2,1)} fusion(bf16[8,1024,2048]{2,1,0:T(8,128)(2,1)} %param.10, f32[2048]{0:T(1024)S(1)} %convert_element_type.31, f32[8,1024]{1,0:T(8,128)S(1)} %add_rsqrt_fusion, bf16[640,2048]{1,0:T(8,128)(2,1)S(1)} %bitcast.83), kind=kOutput, calls=%fused_computation.19 | convolution fusion | flops 4363124736 | bytes 36216832 | tf_op jit(solution)/shard_map/dot_general | solution.py:347
  281.2 1.6 fusion.10
  282.7 3.2 constant_dynamic-slice_fusion.1
  285.9 4.9 fusion.8
  291.6 1.5 slice_bitcast_fusion
  293.1 27.9 %mlp_block.5 = (bf16[2,4,1024,2048]{3,2,1,0:T(8,128)(2,1)}, bf16[256,2048]{1,0:T(8,128)(2,1)}) custom-call(s32[1]{0:T(128)} %bitcast.row_ref, bf16[2,1024,2048]{2,1,0:T(8,128)(2,1)} %out_proj.1.h_ref, bf16[1,2048]{1,0:T(2,128)(2,1)} %broadcast_in_dim.89.gain_ref, ...), custom_call_target="tpu_custom_call", output_to_operand_aliasing={{0}: (4, {})} | custom-call | flops 17716740096 | bytes 73400320 | tf_op jit(solution)/shard_map/mlp_block/pallas_call | solution.py:233
  321.8 2.0 collective-permute-start.1
  323.8 27.9 %mlp_block.6 = (bf16[2,4,1024,2048]{3,2,1,0:T(8,128)(2,1)}, bf16[256,2048]{1,0:T(8,128)(2,1)}) custom-call(s32[1]{0:T(128)} %bitcast.row_ref, bf16[2,1024,2048]{2,1,0:T(8,128)(2,1)} %out_proj.1.h_ref, bf16[1,2048]{1,0:T(2,128)(2,1)} %broadcast_in_dim.89.gain_ref, ...), custom_call_target="tpu_custom_call", output_to_operand_aliasing={{0}: (4, {})} | custom-call | flops 17716740096 | bytes 73400320 | tf_op jit(solution)/shard_map/mlp_block/pallas_call | solution.py:233
  351.7 48.4 %mlp_block.7 = (bf16[2,4,1024,2048]{3,2,1,0:T(8,128)(2,1)}, bf16[512,2048]{1,0:T(8,128)(2,1)}) custom-call(s32[1]{0:T(128)} %bitcast.row_ref, bf16[2,1024,2048]{2,1,0:T(8,128)(2,1)} %out_proj.1.h_ref, bf16[1,2048]{1,0:T(2,128)(2,1)} %broadcast_in_dim.89.gain_ref, ...), custom_call_target="tpu_custom_call", output_to_operand_aliasing={{0}: (4, {})} | custom-call | flops 35433480192 | bytes 77594624 | tf_op jit(solution)/shard_map/mlp_block/pallas_call | solution.py:233
  400.1 48.3 %mlp_block.8 = (bf16[2,4,1024,2048]{3,2,1,0:T(8,128)(2,1)}, bf16[512,2048]{1,0:T(8,128)(2,1)}) custom-call(s32[1]{0:T(128)} %bitcast.row_ref, bf16[2,1024,2048]{2,1,0:T(8,128)(2,1)} %out_proj.1.h_ref, bf16[1,2048]{1,0:T(2,128)(2,1)} %broadcast_in_dim.89.gain_ref, ...), custom_call_target="tpu_custom_call", output_to_operand_aliasing={{0}: (4, {})} | custom-call | flops 35433480192 | bytes 77594624 | tf_op jit(solution)/shard_map/mlp_block/pallas_call | solution.py:233
  448.4 48.4 %mlp_block.9 = (bf16[2,4,1024,2048]{3,2,1,0:T(8,128)(2,1)}, bf16[512,2048]{1,0:T(8,128)(2,1)}) custom-call(s32[1]{0:T(128)} %bitcast.row_ref, bf16[2,1024,2048]{2,1,0:T(8,128)(2,1)} %out_proj.1.h_ref, bf16[1,2048]{1,0:T(2,128)(2,1)} %broadcast_in_dim.89.gain_ref, ...), custom_call_target="tpu_custom_call", output_to_operand_aliasing={{0}: (4, {})} | custom-call | flops 35433480192 | bytes 77594624 | tf_op jit(solution)/shard_map/mlp_block/pallas_call | solution.py:233
  497.0 2.6 collective-permute-start.9
  499.6 2.7 collective-permute-start.3
  502.3 14.0 %dynamic-slice_bitcast_fusion = (bf16[1408,2048]{1,0:T(8,128)(2,1)}, bf16[2048,1408]{0,1:T(8,128)(2,1)}, bf16[2048,1408]{0,1:T(8,128)(2,1)}) fusion(bf16[3,5632,2048]{2,1,0:T(8,128)(2,1)} %all-gather.4.cloned.1.call-done.w_ref, s32[]{:T(128)S(6)} %add.119, s32[]{:T(128)S(6)} %select_n.85, s32[]{:T(128)S(6)} %add.118), kind=kLoop, calls=%fused_computation.5 | loop fusion | bytes 34603020 | tf_op jit(solution)/shard_map/squeeze | solution.py:423
  516.3 2.5 copy.40
  518.8 49.0 %collective-permute-done.2 = bf16[256,2048]{1,0:T(8,128)(2,1)} collective-permute-done((bf16[256,2048]{1,0:T(8,128)(2,1)}, bf16[256,2048]{1,0:T(8,128)(2,1)}, u32[]{:S(2)}, u32[]{:S(2)}) %collective-permute-start.2) | collective-permute-done | bytes 1048608 | tf_op jit(solution)/shard_map/ppermute | solution.py:417
  568.8 2.3 bitcast_dynamic-update-slice_fusion.13
  571.1 1.5 collective-permute-start.6
  572.6 1.2 collective-permute-start.7
  573.8 2.3 bitcast_dynamic-update-slice_fusion.12
  576.1 2.3 bitcast_dynamic-update-slice_fusion.11
  578.7 8.3 %copy.41 = bf16[2048,1408]{1,0:T(8,128)(2,1)} copy(bf16[2048,1408]{0,1:T(8,128)(2,1)} %get-tuple-element.81) | data formatting | bytes 11534336
  587.0 8.3 %copy.42 = bf16[2048,1408]{1,0:T(8,128)(2,1)} copy(bf16[2048,1408]{0,1:T(8,128)(2,1)} %get-tuple-element.82) | data formatting | bytes 11534336
  595.3 17.4 %collective-permute-done.4 = bf16[512,2048]{1,0:T(8,128)(2,1)} collective-permute-done((bf16[512,2048]{1,0:T(8,128)(2,1)}, bf16[512,2048]{1,0:T(8,128)(2,1)}, u32[]{:S(2)}, u32[]{:S(2)}) %collective-permute-start.4) | collective-permute-done | bytes 2097184 | tf_op jit(solution)/shard_map/ppermute | solution.py:417
  612.7 3.2 bitcast_dynamic-update-slice_fusion.8
  615.9 1.5 collective-permute-start.14
  617.4 3.2 bitcast_dynamic-update-slice_fusion.7
  620.5 37.2 %collective-permute-done.6 = bf16[512,2048]{1,0:T(8,128)(2,1)} collective-permute-done((bf16[512,2048]{1,0:T(8,128)(2,1)}, bf16[512,2048]{1,0:T(8,128)(2,1)}, u32[]{:S(2)}, u32[]{:S(2)}) %collective-permute-start.6) | collective-permute-done | bytes 2097184 | tf_op jit(solution)/shard_map/ppermute | solution.py:417
  658.2 2.1 collective-permute-start.13
  660.3 3.2 bitcast_dynamic-update-slice_fusion.6
  663.5 1.5 bitcast_dynamic-update-slice_fusion.5
  665.0 3.2 bitcast_dynamic-update-slice_fusion.4
  668.1 3.2 bitcast_dynamic-update-slice_fusion.3
  671.3 8.9 %collective-permute-done.10 = bf16[256,2048]{1,0:T(8,128)(2,1)} collective-permute-done((bf16[256,2048]{1,0:T(8,128)(2,1)S(1)}, bf16[256,2048]{1,0:T(8,128)(2,1)}, u32[]{:S(2)}, u32[]{:S(2)}) %collective-permute-start.10) | collective-permute-done | bytes 1048608 | tf_op jit(solution)/shard_map/ppermute | solution.py:428
  680.1 2.3 bitcast_dynamic-update-slice_fusion.10
  683.5 86.4 %collective-permute-done.12 = bf16[512,2048]{1,0:T(8,128)(2,1)S(1)} collective-permute-done((bf16[512,2048]{1,0:T(8,128)(2,1)}, bf16[512,2048]{1,0:T(8,128)(2,1)S(1)}, u32[]{:S(2)}, u32[]{:S(2)}) %collective-permute-start.12) | collective-permute-done | bytes 2097184 | tf_op jit(solution)/shard_map/ppermute | solution.py:428
  769.9 1.5 bitcast_dynamic-update-slice_fusion.2
  771.4 1.5 bitcast_dynamic-update-slice_fusion.1
  772.8 1.5 bitcast_dynamic-update-slice_fusion
  (46 shorter events, 7.8 us)
Async XLA Ops:
  7.2 7.3 copy-start.2
  7.2 8.5 %copy-start.1 = (bf16[2048]{0:T(1024)(128)(2,1)S(1)}, bf16[2048]{0:T(1024)(128)(2,1)}, u32[]{:S(2)}) copy-start(bf16[2048]{0:T(1024)(128)(2,1)} %param.19) | copy-start | bytes 12292
  7.2 80.1 %all-gather.6.cloned.1.call-start = ((), (), s32[]{:S(2)}) async-start(), calls=%async_computation.1 | async-start | bytes 19464192 | tf_op jit(solution)/shard_map/all_gather | solution.py:368
  9.3 283.8 %all-gather.4.cloned.1.call-start = ((), (), s32[]{:S(2)}) async-start(), calls=%async_computation | async-start | bytes 71368704 | tf_op jit(solution)/shard_map/all_gather | solution.py:369
  320.9 178.7 %collective-permute-start = (bf16[256,2048]{1,0:T(8,128)(2,1)}, bf16[256,2048]{1,0:T(8,128)(2,1)S(1)}, u32[]{:S(2)}, u32[]{:S(2)}) collective-permute-start(bf16[256,2048]{1,0:T(8,128)(2,1)} %get-tuple-element.47), channel_id=1, source_target_pairs={{0,8},{8,16},{16,24},{24,0},{1,9},{9,17},{17,25},{25,1},{2,10},{10... | collective-permute-start | bytes 3145736 | tf_op jit(solution)/shard_map/ppermute | solution.py:417
  321.8 180.4 %collective-permute-start.1 = (bf16[256,2048]{1,0:T(8,128)(2,1)}, bf16[256,2048]{1,0:T(8,128)(2,1)}, u32[]{:S(2)}, u32[]{:S(2)}) collective-permute-start(bf16[256,2048]{1,0:T(8,128)(2,1)} %get-tuple-element.47), channel_id=1, source_target_pairs={{0,24},{8,0},{16,8},{24,16},{1,25},{9,1},{17,9},{25,17},{2,26},{10... | collective-permute-start | bytes 3145736 | tf_op jit(solution)/shard_map/ppermute | solution.py:417
  496.8 19.5 %copy-start = (bf16[2048,512]{0,1:T(8,128)(2,1)S(1)}, bf16[2048,512]{0,1:T(8,128)(2,1)}, u32[]{:S(2)}) copy-start(bf16[2048,512]{0,1:T(8,128)(2,1)} %slice_bitcast_fusion) | copy-start | bytes 6291460
  496.8 75.8 %collective-permute-start.8 = (bf16[512,2048]{1,0:T(8,128)(2,1)}, bf16[512,2048]{1,0:T(8,128)(2,1)}, u32[]{:S(2)}, u32[]{:S(2)}) collective-permute-start(bf16[512,2048]{1,0:T(8,128)(2,1)} %get-tuple-element.51), channel_id=1, source_target_pairs={{0,8},{8,16},{16,24},{24,0},{1,9},{9,17},{17,25},{25,1},{2,10},{10... | collective-permute-start | bytes 6291464 | tf_op jit(solution)/shard_map/ppermute | solution.py:417
  497.0 81.4 %collective-permute-start.9 = (bf16[512,2048]{1,0:T(8,128)(2,1)}, bf16[512,2048]{1,0:T(8,128)(2,1)}, u32[]{:S(2)}, u32[]{:S(2)}) collective-permute-start(bf16[512,2048]{1,0:T(8,128)(2,1)} %get-tuple-element.51), channel_id=1, source_target_pairs={{0,24},{8,0},{16,8},{24,16},{1,25},{9,1},{17,9},{25,17},{2,26},{10... | collective-permute-start | bytes 6291464 | tf_op jit(solution)/shard_map/ppermute | solution.py:417
  499.6 68.2 %collective-permute-start.2 = (bf16[256,2048]{1,0:T(8,128)(2,1)}, bf16[256,2048]{1,0:T(8,128)(2,1)}, u32[]{:S(2)}, u32[]{:S(2)}) collective-permute-start(bf16[256,2048]{1,0:T(8,128)(2,1)} %get-tuple-element.48), channel_id=1, source_target_pairs={{0,8},{8,16},{16,24},{24,0},{1,9},{9,17},{17,25},{25,1},{2,10},{10... | collective-permute-start | bytes 3145736 | tf_op jit(solution)/shard_map/ppermute | solution.py:417
  499.6 71.5 %collective-permute-start.3 = (bf16[256,2048]{1,0:T(8,128)(2,1)}, bf16[256,2048]{1,0:T(8,128)(2,1)}, u32[]{:S(2)}, u32[]{:S(2)}) collective-permute-start(bf16[256,2048]{1,0:T(8,128)(2,1)} %get-tuple-element.48), channel_id=1, source_target_pairs={{0,24},{8,0},{16,8},{24,16},{1,25},{9,1},{17,9},{25,17},{2,26},{10... | collective-permute-start | bytes 3145736 | tf_op jit(solution)/shard_map/ppermute | solution.py:417
  502.3 110.4 %collective-permute-start.4 = (bf16[512,2048]{1,0:T(8,128)(2,1)}, bf16[512,2048]{1,0:T(8,128)(2,1)}, u32[]{:S(2)}, u32[]{:S(2)}) collective-permute-start(bf16[512,2048]{1,0:T(8,128)(2,1)} %get-tuple-element.49), channel_id=1, source_target_pairs={{0,8},{8,16},{16,24},{24,0},{1,9},{9,17},{17,25},{25,1},{2,10},{10... | collective-permute-start | bytes 6291464 | tf_op jit(solution)/shard_map/ppermute | solution.py:417
  567.8 48.1 %collective-permute-start.5 = (bf16[512,2048]{1,0:T(8,128)(2,1)}, bf16[512,2048]{1,0:T(8,128)(2,1)}, u32[]{:S(2)}, u32[]{:S(2)}) collective-permute-start(bf16[512,2048]{1,0:T(8,128)(2,1)} %get-tuple-element.49), channel_id=1, source_target_pairs={{0,24},{8,0},{16,8},{24,16},{1,25},{9,1},{17,9},{25,17},{2,26},{10... | collective-permute-start | bytes 6291464 | tf_op jit(solution)/shard_map/ppermute | solution.py:417
  571.1 86.5 %collective-permute-start.6 = (bf16[512,2048]{1,0:T(8,128)(2,1)}, bf16[512,2048]{1,0:T(8,128)(2,1)}, u32[]{:S(2)}, u32[]{:S(2)}) collective-permute-start(bf16[512,2048]{1,0:T(8,128)(2,1)} %get-tuple-element.50), channel_id=1, source_target_pairs={{0,8},{8,16},{16,24},{24,0},{1,9},{9,17},{17,25},{25,1},{2,10},{10... | collective-permute-start | bytes 6291464 | tf_op jit(solution)/shard_map/ppermute | solution.py:417
  572.6 85.7 %collective-permute-start.7 = (bf16[512,2048]{1,0:T(8,128)(2,1)}, bf16[512,2048]{1,0:T(8,128)(2,1)S(1)}, u32[]{:S(2)}, u32[]{:S(2)}) collective-permute-start(bf16[512,2048]{1,0:T(8,128)(2,1)} %get-tuple-element.50), channel_id=1, source_target_pairs={{0,24},{8,0},{16,8},{24,16},{1,25},{9,1},{17,9},{25,17},{2,26},{10... | collective-permute-start | bytes 6291464 | tf_op jit(solution)/shard_map/ppermute | solution.py:417
  578.4 101.7 %collective-permute-start.10 = (bf16[256,2048]{1,0:T(8,128)(2,1)S(1)}, bf16[256,2048]{1,0:T(8,128)(2,1)}, u32[]{:S(2)}, u32[]{:S(2)}) collective-permute-start(bf16[256,2048]{1,0:T(8,128)(2,1)S(1)} %collective-permute-done), channel_id=1, source_target_pairs={{0,8},{8,16},{16,24},{24,0},{1,9},{9,17},{17,25},{25,1},{2,10},{10... | collective-permute-start | bytes 3145736 | tf_op jit(solution)/shard_map/ppermute | solution.py:428
  612.7 69.7 %collective-permute-start.11 = (bf16[256,2048]{1,0:T(8,128)(2,1)}, bf16[256,2048]{1,0:T(8,128)(2,1)S(1)}, u32[]{:S(2)}, u32[]{:S(2)}) collective-permute-start(bf16[256,2048]{1,0:T(8,128)(2,1)} %collective-permute-done.3), channel_id=1, source_target_pairs={{0,24},{8,0},{16,8},{24,16},{1,25},{9,1},{17,9},{25,17},{2,26},{10... | collective-permute-start | bytes 3145736 | tf_op jit(solution)/shard_map/ppermute | solution.py:431
  615.9 156.9 %collective-permute-start.14 = (bf16[512,2048]{1,0:T(8,128)(2,1)}, bf16[512,2048]{1,0:T(8,128)(2,1)S(1)}, u32[]{:S(2)}, u32[]{:S(2)}) collective-permute-start(bf16[512,2048]{1,0:T(8,128)(2,1)} %collective-permute-done.8), channel_id=1, source_target_pairs={{0,8},{8,16},{16,24},{24,0},{1,9},{9,17},{17,25},{25,1},{2,10},{10... | collective-permute-start | bytes 6291464 | tf_op jit(solution)/shard_map/ppermute | solution.py:428
  657.7 112.2 %collective-permute-start.12 = (bf16[512,2048]{1,0:T(8,128)(2,1)}, bf16[512,2048]{1,0:T(8,128)(2,1)S(1)}, u32[]{:S(2)}, u32[]{:S(2)}) collective-permute-start(bf16[512,2048]{1,0:T(8,128)(2,1)} %collective-permute-done.4), channel_id=1, source_target_pairs={{0,8},{8,16},{16,24},{24,0},{1,9},{9,17},{17,25},{25,1},{2,10},{10... | collective-permute-start | bytes 6291464 | tf_op jit(solution)/shard_map/ppermute | solution.py:428
  658.2 113.1 %collective-permute-start.13 = (bf16[512,2048]{1,0:T(8,128)(2,1)S(1)}, bf16[512,2048]{1,0:T(8,128)(2,1)S(1)}, u32[]{:S(2)}, u32[]{:S(2)}) collective-permute-start(bf16[512,2048]{1,0:T(8,128)(2,1)S(1)} %collective-permute-done.7), channel_id=1, source_target_pairs={{0,24},{8,0},{16,8},{24,16},{1,25},{9,1},{17,9},{25,17},{2,26},{10... | collective-permute-start | bytes 6291464 | tf_op jit(solution)/shard_map/ppermute | solution.py:431
Sparse Core Ops, SparseCore 0:
  10.7 76.5 all-gather.5
  90.0 200.7 all-gather.3

commit v4 on v3

--- a/solution.py
+++ b/solution.py
@@ -19,7 +19,7 @@
 OUT_TILE = 512
 NT_DIMS = (((1,), (1,)), ((), ()))
 FIRST_SPLIT = (4, 4, 2)
-LATER_SPLIT = (2, 2)
+LATER_SPLIT = (2, 4, 4)
 
 
 def inv_rms(x_in):
@@ -146,27 +146,106 @@
     lax.fori_loop(0, rows // 64, step, 0)
 
 
-def mlp_kernel(slot, start, row_ref, h_ref, gain_ref, w_ref, y_in, y_ref, part_ref, h_scr, u_scr, acc_scr, mid_scr, gu_buf, down_buf, gu_sem, down_sem, h_sem, out_sem):
-    rows, dim = h_scr.shape
-    depth, _, tile, _ = gu_buf.shape
+def gate_up_kernel(slot, start, h_ref, gain_ref, w_ref, mid_ref, h_scr, u_scr, act_scr, mid_scr, w_buf, w_sem, h_sem, out_sem):
+    rows, _ = h_scr.shape
+    depth, _, tile, _ = w_buf.shape
     steps = w_ref.shape[1] // tile
-    out_tile = min(OUT_TILE, dim)
-
-    def gu_copy(step):
-        return pltpu.make_async_copy(w_ref.at[0:2, pl.ds(pl.multiple_of(step * tile, tile), tile), :], gu_buf.at[lax.rem(step, depth)], gu_sem.at[lax.rem(step, depth)])
-
-    def down_copy(step):
-        return pltpu.make_async_copy(w_ref.at[2, pl.ds(pl.multiple_of(step * tile, tile), tile), :], down_buf.at[lax.rem(step, depth)], down_sem.at[lax.rem(step, depth)])
+
+    def w_copy(step):
+        return pltpu.make_async_copy(w_ref.at[:, pl.ds(pl.multiple_of(step * tile, tile), tile), :], w_buf.at[lax.rem(step, depth)], w_sem.at[lax.rem(step, depth)])
+
+    def out_copy(step):
+        return pltpu.make_async_copy(mid_scr.at[lax.rem(step, 2)], mid_ref.at[:, pl.ds(pl.multiple_of(step * tile, tile), tile)], out_sem.at[lax.rem(step, 2)])
 
     h_copy = pltpu.make_async_copy(h_ref.at[slot, pl.ds(start, rows), :], h_scr, h_sem)
     h_copy.start()
     for step in range(min(depth - 1, steps)):
-        gu_copy(step).start()
-    for step in range(min(depth - 2, steps)):
-        down_copy(step).start()
-    mid_scr[...] = jnp.zeros_like(mid_scr)
+        w_copy(step).start()
     h_copy.wait()
     normalise(h_scr, gain_ref[...].astype(jnp.float32), u_scr, rows)
+
+    def finish(step):
+        gate = act_scr[0].astype(jnp.float32)
+        up = act_scr[1].astype(jnp.float32)
+        mid_scr[lax.rem(step, 2)] = (jax.nn.silu(gate) * up).astype(jnp.bfloat16)
+
+    def body(step, carry):
+        @pl.when(step + depth - 1 < steps)
+        def _():
+            w_copy(step + depth - 1).start()
+
+        @pl.when(step >= 3)
+        def _():
+            out_copy(step - 3).wait()
+
+        w_copy(step).wait()
+        index = lax.rem(step, depth)
+        gate = lax.dot_general(u_scr[...], w_buf[index, 0], NT_DIMS, preferred_element_type=jnp.float32)
+        up = lax.dot_general(u_scr[...], w_buf[index, 1], NT_DIMS, preferred_element_type=jnp.float32)
+        finish(step + 1)
+        act_scr[0] = gate.astype(jnp.bfloat16)
+        act_scr[1] = up.astype(jnp.bfloat16)
+
+        @pl.when(step >= 1)
+        def _():
+            out_copy(step - 1).start()
+
+        return carry
+
+    act_scr[...] = jnp.zeros_like(act_scr)
+    lax.fori_loop(0, steps, body, 0)
+    if steps >= 3:
+        out_copy(steps - 3).wait()
+    finish(steps - 1)
+    out_copy(steps - 1).start()
+    if steps >= 2:
+        out_copy(steps - 2).wait()
+    out_copy(steps - 1).wait()
+
+
+def gate_up(hidden, gain, weights, slot, start, rows):
+    dim = hidden.shape[2]
+    ff = weights.shape[1]
+    tile = min(FF_TILE, ff)
+    depth = 3
+    anywhere = pl.BlockSpec(memory_space=pl.ANY)
+    return pl.pallas_call(
+        functools.partial(gate_up_kernel, slot, start),
+        out_shape=jax.ShapeDtypeStruct((rows, ff), jnp.bfloat16),
+        in_specs=[anywhere, pl.BlockSpec(memory_space=pltpu.VMEM), anywhere],
+        out_specs=anywhere,
+        scratch_shapes=[
+            pltpu.VMEM((rows, dim), jnp.bfloat16),
+            pltpu.VMEM((rows, dim), jnp.bfloat16),
+            pltpu.VMEM((2, rows, tile), jnp.bfloat16),
+            pltpu.VMEM((2, rows, tile), jnp.bfloat16),
+            pltpu.VMEM((depth, 2, tile, dim), jnp.bfloat16),
+            pltpu.SemaphoreType.DMA((depth,)),
+            pltpu.SemaphoreType.DMA,
+            pltpu.SemaphoreType.DMA((2,)),
+        ],
+        compiler_params=pltpu.CompilerParams(vmem_limit_bytes=58 * 1024 * 1024),
+        cost_estimate=pl.CostEstimate(flops=4 * rows * dim * ff, bytes_accessed=4 * dim * ff + 2 * rows * (dim + ff), transcendentals=rows * ff),
+        name='gate_up',
+    )(hidden, gain[None, :], weights)
+
+
+def down_kernel(slot, start, first, row_ref, h_ref, mid_ref, w_ref, y_in, y_ref, part_ref, h_scr, mid_scr, acc_scr, w_buf, w_sem, in_sem, out_sem):
+    rows, dim = h_scr.shape
+    depth, tile, _ = w_buf.shape
+    steps = w_ref.shape[0] // tile
+    out_tile = min(OUT_TILE, dim)
+
+    def w_copy(step):
+        return pltpu.make_async_copy(w_ref.at[pl.ds(pl.multiple_of(step * tile, tile), tile), :], w_buf.at[lax.rem(step, depth)], w_sem.at[lax.rem(step, depth)])
+
+    h_copy = pltpu.make_async_copy(h_ref.at[slot, pl.ds(start, rows), :], h_scr, in_sem.at[0])
+    mid_copy = pltpu.make_async_copy(mid_ref.at[pl.ds(first, rows), :], mid_scr, in_sem.at[1])
+    h_copy.start()
+    mid_copy.start()
+    for step in range(min(depth - 1, steps)):
+        w_copy(step).start()
+    h_copy.wait()
 
     def widen(index, carry):
         part = pl.ds(pl.multiple_of(index * 64, 64), 64)
@@ -174,41 +253,22 @@
         return carry
 
     lax.fori_loop(0, rows // 64, widen, 0)
-
-    def add_down(index):
-        for col in range(0, dim, out_tile):
-            cols = slice(col, col + out_tile)
-            acc_scr[:, cols] += jnp.dot(mid_scr[...], down_buf[index, :, cols], preferred_element_type=jnp.float32)
+    mid_copy.wait()
 
     def body(step, carry):
         @pl.when(step + depth - 1 < steps)
         def _():
-            gu_copy(step + depth - 1).start()
-
-        @pl.when(step + depth - 2 < steps)
-        def _():
-            down_copy(step + depth - 2).start()
-
-        gu_copy(step).wait()
-        before = jnp.maximum(step - 1, 0)
-
-        @pl.when(step != 1)
-        def _():
-            down_copy(before).wait()
-
+            w_copy(step + depth - 1).start()
+
+        w_copy(step).wait()
         index = lax.rem(step, depth)
-        gate = lax.dot_general(u_scr[...], gu_buf[index, 0], NT_DIMS, preferred_element_type=jnp.float32)
-        up = lax.dot_general(u_scr[...], gu_buf[index, 1], NT_DIMS, preferred_element_type=jnp.float32)
-        add_down(lax.rem(before, depth))
-        gate = gate.astype(jnp.bfloat16).astype(jnp.float32)
-        up = up.astype(jnp.bfloat16).astype(jnp.float32)
-        mid_scr[...] = (jax.nn.silu(gate) * up).astype(jnp.bfloat16)
+        mid = mid_scr[:, pl.ds(pl.multiple_of(step * tile, tile), tile)]
+        for col in range(0, dim, out_tile):
+            cols = slice(col, col + out_tile)
+            acc_scr[:, cols] += jnp.dot(mid, w_buf[index, :, cols], preferred_element_type=jnp.float32)
         return carry
 
     lax.fori_loop(0, steps, body, 0)
-    if steps > 1:
-        down_copy(steps - 1).wait()
-    add_down((steps - 1) % depth)
 
     def narrow(index, carry):
         part = pl.ds(pl.multiple_of(index * 64, 64), 64)
@@ -224,34 +284,31 @@
     y_out.wait()
 
 
-def mlp(row, hidden, gain, weights, y_all, slot, start, rows):
+def down_proj(row, hidden, mid, weights, y_all, slot, start, first, rows):
     dim = hidden.shape[2]
-    ff = weights.shape[1]
+    ff = mid.shape[1]
     tile = min(FF_TILE, ff)
-    depth = 3
+    depth = 4
     anywhere = pl.BlockSpec(memory_space=pl.ANY)
     return pl.pallas_call(
-        functools.partial(mlp_kernel, slot, start),
+        functools.partial(down_kernel, slot, start, first),
         out_shape=(jax.ShapeDtypeStruct(y_all.shape, jnp.bfloat16), jax.ShapeDtypeStruct((rows, dim), jnp.bfloat16)),
-        in_specs=[pl.BlockSpec(memory_space=pltpu.SMEM), anywhere, pl.BlockSpec(memory_space=pltpu.VMEM), anywhere, anywhere],
+        in_specs=[pl.BlockSpec(memory_space=pltpu.SMEM), anywhere, anywhere, anywhere, anywhere],
         out_specs=(anywhere, anywhere),
         scratch_shapes=[
             pltpu.VMEM((rows, dim), jnp.bfloat16),
-            pltpu.VMEM((rows, dim), jnp.bfloat16),
+            pltpu.VMEM((rows, ff), jnp.bfloat16),
             pltpu.VMEM((rows, dim), jnp.float32),
-            pltpu.VMEM((rows, tile), jnp.bfloat16),
-            pltpu.VMEM((depth, 2, tile, dim), jnp.bfloat16),
             pltpu.VMEM((depth, tile, dim), jnp.bfloat16),
             pltpu.SemaphoreType.DMA((depth,)),
-            pltpu.SemaphoreType.DMA((depth,)),
-            pltpu.SemaphoreType.DMA,
+            pltpu.SemaphoreType.DMA((2,)),
             pltpu.SemaphoreType.DMA((2,)),
         ],
         input_output_aliases={4: 0},
         compiler_params=pltpu.CompilerParams(vmem_limit_bytes=58 * 1024 * 1024),
-        cost_estimate=pl.CostEstimate(flops=6 * rows * dim * ff, bytes_accessed=6 * dim * ff + 8 * rows * dim, transcendentals=rows * ff),
-        name='mlp_block',
-    )(row, hidden, gain[None, :], weights, y_all)
+        cost_estimate=pl.CostEstimate(flops=2 * rows * dim * ff, bytes_accessed=2 * dim * ff + 2 * rows * (4 * dim + ff), transcendentals=0),
+        name='down_proj',
+    )(row, hidden, mid, weights, y_all)
 
 
 def qkv_kernel(qkv_block, row_ref, x_ref, gain_ref, w_ref, out_ref, u_scr, w_scr):
@@ -366,7 +423,8 @@
 
         qkv_block = w_qkv.shape[1]
         qkvo = lax.all_gather(jnp.concatenate([w_qkv.T, w_o], axis=0), both, axis=0, tiled=False)
-        mlp_full = lax.all_gather(jnp.concatenate([w_gate_up.T.reshape(2, ff_block, model_dim), w_down[None]], axis=0), both, axis=1, tiled=True)
+        gu_full = lax.all_gather(w_gate_up.T.reshape(2, ff_block, model_dim), both, axis=1, tiled=True)
+        down_full = lax.all_gather(w_down, both, axis=0, tiled=True)
         row_arg = row.astype(jnp.int32)[None]
         cos_tab, sin_tab = rope_tables(seq_len, head_dim)
         x_rows = x_loc.reshape(own_batch, n_tpa, seq_len, model_dim)
@@ -377,7 +435,27 @@
         attn_out = attention(qkv_act, len_own, cos_tab, sin_tab, n_tpa * k_buf.shape[2], head_dim)
         hidden = out_proj(row_arg, attn_out, x_rows, qkvo, qkv_block)
 
-        hidden, x_late, qkvo_late = lax.optimization_barrier((hidden, x_loc, qkvo))
+        y_all = empty((own_batch, n_tpa, seq_len, model_dim), jnp.bfloat16)
+
+        def put(y_buf, piece, slot, owner, start):
+            return lax.dynamic_update_slice(y_buf, piece[None, None], (slot, lax.rem(owner + n_tpa, n_tpa), start, 0))
+
+        spots = []
+        for slot in range(own_batch):
+            start = 0
+            for share in FIRST_SPLIT if slot == 0 else LATER_SPLIT:
+                spots.append((slot, start, seq_len // share))
+                start += seq_len // share
+        mids = []
+        fars = []
+        near = []
+        for slot, start, rows in spots:
+            if start == 0:
+                mids.append(gate_up(hidden, g_mlp, gu_full, slot, 0, seq_len))
+            y_all, part = down_proj(row_arg, hidden, mids[slot], down_full, y_all, slot, start, start, rows)
+            near.append((lax.ppermute(part, 'tpa', up_ring), lax.ppermute(part, 'tpa', down_ring)))
+
+        y_all, x_late, qkvo_late, gu_late, down_late = lax.optimization_barrier((y_all, x_loc, qkvo, gu_full, down_full))
         kv_cols = k_buf.shape[2] * head_dim
         q_cols = qkv_row - 2 * kv_cols
         own_blocks = lax.dynamic_slice_in_dim(qkvo_late, row * n_tpb, n_tpb, 0)
@@ -394,40 +472,18 @@
         valid_pos = (jnp.arange(seq_len)[None, :] < len_loc[:, None])[:, :, None, None]
         k_cache = jnp.where(valid_pos, k_rot[:, :, None, :], k_buf)
         v_cache = jnp.where(valid_pos, kv_new[:, :, None, head_dim:], v_buf)
+        gu_own = lax.dynamic_slice_in_dim(gu_late, row * ff_row, ff_row, 1)
+        w_gate = gu_own[0].T
+        w_up = gu_own[1].T
+        down_rows = lax.dynamic_slice_in_dim(down_late, row * ff_row, ff_row, 0)
         cache_outs = (k_cache, v_cache, w_query, w_key, w_value, o_rows)
-        mlp_full, cache_outs = lax.optimization_barrier((mlp_full, cache_outs))
+        near[-3], cache_outs = lax.optimization_barrier((near[-3], cache_outs))
         k_cache, v_cache, w_query, w_key, w_value, o_rows = cache_outs
-
-        y_all = empty((own_batch, n_tpa, seq_len, model_dim), jnp.bfloat16)
-
-        def put(y_buf, piece, slot, owner, start):
-            return lax.dynamic_update_slice(y_buf, piece[None, None], (slot, lax.rem(owner + n_tpa, n_tpa), start, 0))
-
-        spots = []
-        for slot in range(own_batch):
-            start = 0
-            for share in FIRST_SPLIT if slot == 0 else LATER_SPLIT:
-                spots.append((slot, start, seq_len // share))
-                start += seq_len // share
-        fars = []
-        near = []
-        upward = [0, 0]
-        for slot, start, rows in spots:
-            y_all, part = mlp(row_arg, hidden, g_mlp, mlp_full, y_all, slot, start, rows)
-            near.append((lax.ppermute(part, 'tpa', up_ring), lax.ppermute(part, 'tpa', down_ring)))
-
-        y_all, mlp_late = lax.optimization_barrier((y_all, mlp_full))
-        mlp_own = lax.dynamic_slice_in_dim(mlp_late, row * ff_row, ff_row, 1)
-        w_gate = mlp_own[0].T
-        w_up = mlp_own[1].T
-        down_rows = mlp_own[2]
-        near[-1], (w_gate, w_up, down_rows) = lax.optimization_barrier((near[-1], (w_gate, w_up, down_rows)))
-        for (from_below, from_above), (slot, start, rows) in zip(near, spots):
-            if upward[0] <= upward[1]:
-                upward[0] += rows
+        near[-2], (w_gate, w_up, down_rows) = lax.optimization_barrier((near[-2], (w_gate, w_up, down_rows)))
+        for index, ((from_below, from_above), (slot, start, rows)) in enumerate(zip(near, spots)):
+            if index % 2 == 0:
                 far = lax.ppermute(from_below, 'tpa', up_ring)
             else:
-                upward[1] += rows
                 far = lax.ppermute(from_above, 'tpa', down_ring)
             y_all = put(y_all, from_below, slot, row - 1, start)
             y_all = put(y_all, from_above, slot, row + 1, start)

time: 791 us -> 771 us (0.975)
  waiting for transfers between devices: 258 us -> 208 us
  Pallas kernels: 374 us -> 388 us
  local copies, waits for them, and re-layouts: 76.1 us -> 88.1 us
    ppermute x5 -> x6, waiting for transfers between devices: 104 us -> 23.1 us  [layer_step(): lax.ppermute(part, 'tpa', up_ring)]
    ppermute x3, waiting for transfers between devices: 95.3 us -> 28.1 us  [layer_step(): far = lax.ppermute(from_below, 'tpa', up_ring)]
    ppermute x5 -> x6, waiting for transfers between devices: 0.59 us -> 51.3 us  [layer_step(): lax.ppermute(part, 'tpa', down_ring)]
    ppermute x2 -> x3, waiting for transfers between devices: 0.01 us -> 44.7 us  [layer_step(): far = lax.ppermute(from_above, 'tpa', down_ring)]
    squeeze x1 -> x0, local copies, waits for them, and re-layouts: 14 us -> none  [layer_step(): down_rows = mlp_own[2]]
    pallas_call x5 -> x8, Pallas kernels: 201 us -> 214 us  [the longest x2 122 us: gate_up(): pl.pallas_call(functools.partial(gate_up_kernel, slot, start), out_shape=...]
    transpose x0 -> x1, local copies, waits for them, and re-layouts: none -> 11.2 us  [layer_step(): w_up = gu_own[1].T]
    dynamic_update_slice x15 -> x18, local copies, waits for them, and re-layouts: 32.9 us -> 41.5 us  [put(): lax.dynamic_update_slice(y_buf, piece[None, None], (slot, lax.rem(owner +...]
  transfers between devices with their start and end apart: 17 -> 21, of which waited for: 7 -> 11; matrix products, arithmetic and copies ran while one was open for 15% -> 16% of each run, Pallas kernels for 44% -> 40%
where the time goes in v4:
time: 771 us; the launch traced here: 761 us
  Pallas kernels  388 us (50%)
  waiting for transfers between devices  208 us (27%)
  local copies, waits for them, and re-layouts  88.1 us (11%)
  starting transfers between devices  22.5 us (3%)
  other arithmetic  22 us (3%)
  matrix products  18.4 us (2%)
  between operations  14.3 us (2%)
    pallas_call x2, Pallas kernels, gate_up(): pl.pallas_call(functools.partial(gate_up_kernel, slot, start), out_shape=...  122 us
    pallas_call x1, Pallas kernels, attention(): pl.pallas_call(functools.partial(attention_kernel, head_dim, group_size),...  112 us
    pallas_call x6, Pallas kernels, down_proj(): pl.pallas_call(functools.partial(down_kernel, slot, start, first), out_sh...  92.6 us
    all_gather x1, waiting for transfers between devices, layer_step(): lax.all_gather(jnp.concatenate([w_qkv.T, w_o], axis=0), both, axis=0, til...  59.3 us
    ppermute x6, waiting for transfers between devices, layer_step(): lax.ppermute(part, 'tpa', down_ring)  51.3 us
    ppermute x3, waiting for transfers between devices, layer_step(): far = lax.ppermute(from_above, 'tpa', down_ring)  44.7 us
    dynamic_update_slice x18, local copies, waits for them, and re-layouts, put(): lax.dynamic_update_slice(y_buf, piece[None, None], (slot, lax.rem(owner +...  41.5 us
    pallas_call x1, Pallas kernels, qkv_proj(): pl.pallas_call(functools.partial(qkv_kernel, qkv_block), out_shape=jax.Sh...  35.2 us
  transfers between devices with their start and end apart: 21, of which 11 were waited for; matrix products, arithmetic and copies ran while one was open for 16% of the time, Pallas kernels for 40%

profile of v4, /device:TPU:97, one launch (start us, length us, event | category | flops | bytes accessed | tf_op | source)
XLA Modules:
  0.0 761.0 jit_solution(14400967357108951267)
XLA Ops:
  7.3 1.9 pad_maximum_fusion
  15.4 11.9 %multiply_reduce_fusion = f32[8,1024]{1,0:T(8,128)S(1)} fusion(bf16[8,1024,2048]{2,1,0:T(8,128)(2,1)} %param.10), kind=kLoop, calls=%fused_computation.1 | loop fusion | flops 50323456 | bytes 33587200 | tf_op jit(solution)/shard_map/reduce_sum | solution.py:27
  28.0 59.3 %all-gather.9.cloned.1.call-done = bf16[4608,2048]{1,0:T(8,128)(2,1)} async-done(((bf16[144,2048]{1,0:T(8,128)(2,1)}), bf16[4608,2048]{1,0:T(8,128)(2,1)}) %all-gather.9.cloned.1.call-update) | async-done | bytes 18874384 | tf_op jit(solution)/shard_map/all_gather | solution.py:425
  87.3 35.2 %qkv_proj.1.qkv_ref = bf16[2,1024,2560]{2,1,0:T(8,128)(2,1)} custom-call(s32[1]{0:T(128)} %bitcast.row_ref, bf16[2,4,1024,2048]{3,2,1,0:T(8,128)(2,1)} %bitcast.80, bf16[1,2048]{1,0:T(2,128)(2,1)} %broadcast_in_dim.91.gain_ref, bf16[32,144,2048]{2,1,0:T(8,128)(2,1)} %bitcast.82), custom_call_target="tpu_custom_call" | custom-call | flops 21474836480 | bytes 27262976 | tf_op jit(solution)/shard_map/qkv_proj/pallas_call | solution.py:342
  122.5 111.5 %prefill_attention.1.a_ref = bf16[2,1024,2048]{2,1,0:T(8,128)(2,1)} custom-call(s32[2]{0:T(128)S(1)} %fusion.14.len_ref, bf16[2,1024,2560]{2,1,0:T(8,128)(2,1)} %qkv_proj.1.qkv_ref, f32[1024,128]{1,0:T(8,128)S(1)} %copy.35.cos_ref, f32[1024,128]{1,0:T(8,128)S(1)} %copy.36.sin_ref), custom_call_target="tpu_custom_call" | custom-call | flops 68719476736 | bytes 18874368 | tf_op jit(solution)/shard_map/prefill_attention/pallas_call | solution.py:114
  234.1 26.7 %out_proj.1.h_ref = bf16[2,1024,2048]{2,1,0:T(8,128)(2,1)} custom-call(s32[1]{0:T(128)} %bitcast.row_ref, bf16[2,1024,2048]{2,1,0:T(8,128)(2,1)} %prefill_attention.1.a_ref, bf16[2,4,1024,2048]{3,2,1,0:T(8,128)(2,1)} %bitcast.81, bf16[32,144,2048]{2,1,0:T(8,128)(2,1)} %bitcast.83), custom_call_target="tpu_custom_call" | custom-call | flops 17179869184 | bytes 33554432 | tf_op jit(solution)/shard_map/out_proj/pallas_call | solution.py:383
  260.8 61.2 %gate_up.3.mid_ref = bf16[1024,5632]{1,0:T(8,128)(2,1)} custom-call(bf16[2,1024,2048]{2,1,0:T(8,128)(2,1)} %out_proj.1.h_ref, bf16[1,2048]{1,0:T(2,128)(2,1)} %broadcast_in_dim.92.gain_ref, bf16[2,5632,2048]{2,1,0:T(8,128)(2,1)} %all-gather.5.cloned.1.call-done.w_ref), custom_call_target="tpu_custom_call" | custom-call | flops 47244640256 | bytes 61865984 | tf_op jit(solution)/shard_map/gate_up/pallas_call | solution.py:212
  322.0 60.5 %gate_up.2.mid_ref = bf16[1024,5632]{1,0:T(8,128)(2,1)} custom-call(bf16[2,1024,2048]{2,1,0:T(8,128)(2,1)} %out_proj.1.h_ref, bf16[1,2048]{1,0:T(2,128)(2,1)} %broadcast_in_dim.92.gain_ref, bf16[2,5632,2048]{2,1,0:T(8,128)(2,1)} %all-gather.5.cloned.1.call-done.w_ref), custom_call_target="tpu_custom_call" | custom-call | flops 47244640256 | bytes 61865984 | tf_op jit(solution)/shard_map/gate_up/pallas_call | solution.py:212
  382.5 12.8 %down_proj.6 = (bf16[2,4,1024,2048]{3,2,1,0:T(8,128)(2,1)}, bf16[256,2048]{1,0:T(8,128)(2,1)}) custom-call(s32[1]{0:T(128)} %bitcast.row_ref, bf16[2,1024,2048]{2,1,0:T(8,128)(2,1)} %out_proj.1.h_ref, bf16[1024,5632]{1,0:T(8,128)(2,1)} %gate_up.3.mid_ref, bf16[5632,2048]{1,0:T(8,128)(2,1)} %all-gather.7.cloned.1.call-done.w_ref, ...), custom_call_target="tpu_custom_call", output_to_operand_aliasing={{0}: (4, {})} | custom-call | flops 5905580032 | bytes 30146560 | tf_op jit(solution)/shard_map/down_proj/pallas_call | solution.py:293
  395.3 12.8 %down_proj.7 = (bf16[2,4,1024,2048]{3,2,1,0:T(8,128)(2,1)}, bf16[256,2048]{1,0:T(8,128)(2,1)}) custom-call(s32[1]{0:T(128)} %bitcast.row_ref, bf16[2,1024,2048]{2,1,0:T(8,128)(2,1)} %out_proj.1.h_ref, bf16[1024,5632]{1,0:T(8,128)(2,1)} %gate_up.3.mid_ref, bf16[5632,2048]{1,0:T(8,128)(2,1)} %all-gather.7.cloned.1.call-done.w_ref, ...), custom_call_target="tpu_custom_call", output_to_operand_aliasing={{0}: (4, {})} | custom-call | flops 5905580032 | bytes 30146560 | tf_op jit(solution)/shard_map/down_proj/pallas_call | solution.py:293
  408.1 20.7 %down_proj.8 = (bf16[2,4,1024,2048]{3,2,1,0:T(8,128)(2,1)}, bf16[512,2048]{1,0:T(8,128)(2,1)}) custom-call(s32[1]{0:T(128)} %bitcast.row_ref, bf16[2,1024,2048]{2,1,0:T(8,128)(2,1)} %out_proj.1.h_ref, bf16[1024,5632]{1,0:T(8,128)(2,1)} %gate_up.3.mid_ref, bf16[5632,2048]{1,0:T(8,128)(2,1)} %all-gather.7.cloned.1.call-done.w_ref, ...), custom_call_target="tpu_custom_call", output_to_operand_aliasing={{0}: (4, {})} | custom-call | flops 11811160064 | bytes 37224448 | tf_op jit(solution)/shard_map/down_proj/pallas_call | solution.py:293
  428.9 20.7 %down_proj.9 = (bf16[2,4,1024,2048]{3,2,1,0:T(8,128)(2,1)}, bf16[512,2048]{1,0:T(8,128)(2,1)}) custom-call(s32[1]{0:T(128)} %bitcast.row_ref, bf16[2,1024,2048]{2,1,0:T(8,128)(2,1)} %out_proj.1.h_ref, bf16[1024,5632]{1,0:T(8,128)(2,1)} %gate_up.2.mid_ref, bf16[5632,2048]{1,0:T(8,128)(2,1)} %all-gather.7.cloned.1.call-done.w_ref, ...), custom_call_target="tpu_custom_call", output_to_operand_aliasing={{0}: (4, {})} | custom-call | flops 11811160064 | bytes 37224448 | tf_op jit(solution)/shard_map/down_proj/pallas_call | solution.py:293
  449.6 12.8 %down_proj.10 = (bf16[2,4,1024,2048]{3,2,1,0:T(8,128)(2,1)}, bf16[256,2048]{1,0:T(8,128)(2,1)}) custom-call(s32[1]{0:T(128)} %bitcast.row_ref, bf16[2,1024,2048]{2,1,0:T(8,128)(2,1)} %out_proj.1.h_ref, bf16[1024,5632]{1,0:T(8,128)(2,1)} %gate_up.2.mid_ref, bf16[5632,2048]{1,0:T(8,128)(2,1)} %all-gather.7.cloned.1.call-done.w_ref, ...), custom_call_target="tpu_custom_call", output_to_operand_aliasing={{0}: (4, {})} | custom-call | flops 5905580032 | bytes 30146560 | tf_op jit(solution)/shard_map/down_proj/pallas_call | solution.py:293
  465.3 12.8 %down_proj.11 = (bf16[2,4,1024,2048]{3,2,1,0:T(8,128)(2,1)}, bf16[256,2048]{1,0:T(8,128)(2,1)}) custom-call(s32[1]{0:T(128)} %bitcast.row_ref, bf16[2,1024,2048]{2,1,0:T(8,128)(2,1)} %out_proj.1.h_ref, bf16[1024,5632]{1,0:T(8,128)(2,1)} %gate_up.2.mid_ref, bf16[5632,2048]{1,0:T(8,128)(2,1)} %all-gather.7.cloned.1.call-done.w_ref, ...), custom_call_target="tpu_custom_call", output_to_operand_aliasing={{0}: (4, {})} | custom-call | flops 5905580032 | bytes 30146560 | tf_op jit(solution)/shard_map/down_proj/pallas_call | solution.py:293
  478.1 1.9 constant_dynamic-slice_fusion
  482.4 2.6 collective-permute-start.1
  485.0 18.4 %fusion.3 = bf16[8,1024,128]{1,2,0:T(8,128)(2,1)} fusion(bf16[8,1024,2048]{2,1,0:T(8,128)(2,1)} %param.10, f32[2048]{0:T(1024)S(1)} %copy-done.8, f32[8,1024]{1,0:T(8,128)S(1)} %copy-done.6, bf16[640,2048]{1,0:T(8,128)(2,1)S(1)} %bitcast.88), kind=kOutput, calls=%fused_computation.14 | convolution fusion | flops 4363124736 | bytes 36216832 | tf_op jit(solution)/shard_map/dot_general | solution.py:404
  505.3 6.2 constant_dynamic-slice_fusion.1
  511.5 4.2 fusion.8
  515.6 11.2 %dynamic-slice_bitcast_fusion = (bf16[2048,1408]{0,1:T(8,128)(2,1)}, bf16[2048,1408]{0,1:T(8,128)(2,1)}) fusion(bf16[2,5632,2048]{2,1,0:T(8,128)(2,1)} %all-gather.5.cloned.1.call-done.w_ref, s32[]{:T(128)S(6)} %add.126, s32[]{:T(128)S(6)} %select_n.89), kind=kLoop, calls=%fused_computation.5 | loop fusion | bytes 23068680 | tf_op jit(solution)/shard_map/transpose | solution.py:477
  526.9 2.7 collective-permute-start.7
  529.6 3.2 constant_dynamic-slice_fusion.2
  532.8 2.7 collective-permute-start.3
  535.6 2.3 bitcast_dynamic-update-slice_fusion.17
  537.9 8.3 %copy.42 = bf16[2048,1408]{1,0:T(8,128)(2,1)} copy(bf16[2048,1408]{0,1:T(8,128)(2,1)} %get-tuple-element.87) | data formatting | bytes 11534336
  546.2 8.3 %copy.43 = bf16[2048,1408]{1,0:T(8,128)(2,1)} copy(bf16[2048,1408]{0,1:T(8,128)(2,1)} %get-tuple-element.88) | data formatting | bytes 11534336
  554.6 2.3 bitcast_dynamic-update-slice_fusion.16
  556.9 2.3 bitcast_dynamic-update-slice_fusion.15
  559.2 36.7 %collective-permute-done.3 = bf16[256,2048]{1,0:T(8,128)(2,1)S(1)} collective-permute-done((bf16[256,2048]{1,0:T(8,128)(2,1)}, bf16[256,2048]{1,0:T(8,128)(2,1)S(1)}, u32[]{:S(2)}, u32[]{:S(2)}) %collective-permute-start.3) | collective-permute-done | bytes 1048608 | tf_op jit(solution)/shard_map/ppermute | solution.py:456
  600.3 23.1 %collective-permute-done.4 = bf16[512,2048]{1,0:T(8,128)(2,1)} collective-permute-done((bf16[512,2048]{1,0:T(8,128)(2,1)}, bf16[512,2048]{1,0:T(8,128)(2,1)}, u32[]{:S(2)}, u32[]{:S(2)}) %collective-permute-start.4) | collective-permute-done | bytes 2097184 | tf_op jit(solution)/shard_map/ppermute | solution.py:456
  624.6 3.2 bitcast_dynamic-update-slice_fusion.5
  627.8 13.1 %collective-permute-done.5 = bf16[512,2048]{1,0:T(8,128)(2,1)} collective-permute-done((bf16[512,2048]{1,0:T(8,128)(2,1)}, bf16[512,2048]{1,0:T(8,128)(2,1)}, u32[]{:S(2)}, u32[]{:S(2)}) %collective-permute-start.5) | collective-permute-done | bytes 2097184 | tf_op jit(solution)/shard_map/ppermute | solution.py:456
  640.9 3.2 bitcast_dynamic-update-slice_fusion.4
  644.0 3.2 bitcast_dynamic-update-slice_fusion.3
  647.2 3.2 bitcast_dynamic-update-slice_fusion.2
  650.3 2.3 bitcast_dynamic-update-slice_fusion.13
  654.2 2.3 bitcast_dynamic-update-slice_fusion.12
  656.5 1.9 collective-permute-start.15
  659.4 2.5 copy.41
  664.8 2.3 bitcast_dynamic-update-slice_fusion.10
  669.6 2.3 bitcast_dynamic-update-slice_fusion.9
  671.9 13.8 %collective-permute-done.13 = bf16[256,2048]{1,0:T(8,128)(2,1)} collective-permute-done((bf16[256,2048]{1,0:T(8,128)(2,1)S(1)}, bf16[256,2048]{1,0:T(8,128)(2,1)}, u32[]{:S(2)}, u32[]{:S(2)}) %collective-permute-start.13) | collective-permute-done | bytes 1048608 | tf_op jit(solution)/shard_map/ppermute | solution.py:487
  685.7 2.3 bitcast_dynamic-update-slice_fusion.8
  688.0 25.3 %collective-permute-done.14 = bf16[512,2048]{1,0:T(8,128)(2,1)} collective-permute-done((bf16[512,2048]{1,0:T(8,128)(2,1)}, bf16[512,2048]{1,0:T(8,128)(2,1)}, u32[]{:S(2)}, u32[]{:S(2)}) %collective-permute-start.14) | collective-permute-done | bytes 2097184 | tf_op jit(solution)/shard_map/ppermute | solution.py:485
  713.3 3.2 bitcast_dynamic-update-slice_fusion.1
  716.4 14.3 %collective-permute-done.15 = bf16[512,2048]{1,0:T(8,128)(2,1)} collective-permute-done((bf16[512,2048]{1,0:T(8,128)(2,1)}, bf16[512,2048]{1,0:T(8,128)(2,1)}, u32[]{:S(2)}, u32[]{:S(2)}) %collective-permute-start.15) | collective-permute-done | bytes 2097184 | tf_op jit(solution)/shard_map/ppermute | solution.py:487
  730.7 3.2 bitcast_dynamic-update-slice_fusion
  736.7 16.6 %collective-permute-done.17 = bf16[256,2048]{1,0:T(8,128)(2,1)S(1)} collective-permute-done((bf16[256,2048]{1,0:T(8,128)(2,1)}, bf16[256,2048]{1,0:T(8,128)(2,1)S(1)}, u32[]{:S(2)}, u32[]{:S(2)}) %collective-permute-start.17) | collective-permute-done | bytes 1048608 | tf_op jit(solution)/shard_map/ppermute | solution.py:487
  (77 shorter events, 31.6 us)
Async XLA Ops:
  7.2 3.7 copy-start.7
  7.2 4.9 copy-start.10
  7.2 6.7 copy-start.9
  7.2 80.1 %all-gather.9.cloned.1.call-start = ((), (), s32[]{:S(2)}) async-start(), calls=%async_computation.2 | async-start | bytes 19464192 | tf_op jit(solution)/shard_map/all_gather | solution.py:425
  9.3 251.5 %all-gather.5.cloned.1.call-start = ((), (), s32[]{:S(2)}) async-start(), calls=%async_computation | async-start | bytes 47579136 | tf_op jit(solution)/shard_map/all_gather | solution.py:426
  10.1 372.4 %all-gather.7.cloned.1.call-start = ((), (), s32[]{:S(2)}) async-start(), calls=%async_computation.1 | async-start | bytes 23789568 | tf_op jit(solution)/shard_map/all_gather | solution.py:427
  12.8 0.7 copy-start.3
  12.8 109.7 %copy-start.1 = (f32[1024,32]{0,1:T(8,128)}, f32[1024,32]{0,1:T(8,128)S(1)}, u32[]{:S(2)}) copy-start(f32[1024,32]{0,1:T(8,128)S(1)} %get-tuple-element.100) | copy-start | bytes 393220
  462.4 64.5 %collective-permute-start.8 = (bf16[256,2048]{1,0:T(8,128)(2,1)}, bf16[256,2048]{1,0:T(8,128)(2,1)}, u32[]{:S(2)}, u32[]{:S(2)}) collective-permute-start(bf16[256,2048]{1,0:T(8,128)(2,1)} %get-tuple-element.55), channel_id=1, source_target_pairs={{0,8},{8,16},{16,24},{24,0},{1,9},{9,17},{17,25},{25,1},{2,10},{10... | collective-permute-start | bytes 3145736 | tf_op jit(solution)/shard_map/ppermute | solution.py:456
  463.9 63.0 %collective-permute-start.9 = (bf16[256,2048]{1,0:T(8,128)(2,1)}, bf16[256,2048]{1,0:T(8,128)(2,1)}, u32[]{:S(2)}, u32[]{:S(2)}) collective-permute-start(bf16[256,2048]{1,0:T(8,128)(2,1)} %get-tuple-element.55), channel_id=1, source_target_pairs={{0,24},{8,0},{16,8},{24,16},{1,25},{9,1},{17,9},{25,17},{2,26},{10... | collective-permute-start | bytes 3145736 | tf_op jit(solution)/shard_map/ppermute | solution.py:456
  465.3 19.8 %copy-start.6 = (f32[8,1024]{1,0:T(8,128)S(1)}, f32[8,1024]{1,0:T(8,128)}, u32[]{:S(2)}) copy-start(f32[8,1024]{1,0:T(8,128)} %add_rsqrt_fusion) | copy-start | bytes 98308
  465.3 19.8 %copy-start.8 = (f32[2048]{0:T(1024)S(1)}, f32[2048]{0:T(1024)}, u32[]{:S(2)}) copy-start(f32[2048]{0:T(1024)} %convert_element_type.31) | copy-start | bytes 24580
  482.3 21.1 %copy-start.2 = (f32[1024,32]{0,1:T(8,128)S(1)}, f32[1024,32]{0,1:T(8,128)}, u32[]{:S(2)}) copy-start(f32[1024,32]{0,1:T(8,128)} %copy-done.1) | copy-start | bytes 393220
  482.3 21.1 %copy-start.4 = (f32[1024,32]{0,1:T(8,128)S(1)}, f32[1024,32]{0,1:T(8,128)}, u32[]{:S(2)}) copy-start(f32[1024,32]{0,1:T(8,128)} %copy-done.3) | copy-start | bytes 393220
  482.3 29.1 %copy-start.5 = (pred[8,1024]{1,0:T(8,128)(4,1)S(1)}, pred[8,1024]{1,0:T(8,128)(4,1)}, u32[]{:S(2)}) copy-start(pred[8,1024]{1,0:T(8,128)(4,1)} %iota_compare_fusion) | copy-start | bytes 24580
  482.3 47.3 %collective-permute-start = (bf16[256,2048]{1,0:T(8,128)(2,1)}, bf16[256,2048]{1,0:T(8,128)(2,1)}, u32[]{:S(2)}, u32[]{:S(2)}) collective-permute-start(bf16[256,2048]{1,0:T(8,128)(2,1)} %get-tuple-element.47), channel_id=1, source_target_pairs={{0,8},{8,16},{16,24},{24,0},{1,9},{9,17},{17,25},{25,1},{2,10},{10... | collective-permute-start | bytes 3145736 | tf_op jit(solution)/shard_map/ppermute | solution.py:456
  482.4 50.4 %collective-permute-start.1 = (bf16[256,2048]{1,0:T(8,128)(2,1)}, bf16[256,2048]{1,0:T(8,128)(2,1)}, u32[]{:S(2)}, u32[]{:S(2)}) collective-permute-start(bf16[256,2048]{1,0:T(8,128)(2,1)} %get-tuple-element.47), channel_id=1, source_target_pairs={{0,24},{8,0},{16,8},{24,16},{1,25},{9,1},{17,9},{25,17},{2,26},{10... | collective-permute-start | bytes 3145736 | tf_op jit(solution)/shard_map/ppermute | solution.py:456
  505.0 30.5 %collective-permute-start.2 = (bf16[256,2048]{1,0:T(8,128)(2,1)}, bf16[256,2048]{1,0:T(8,128)(2,1)}, u32[]{:S(2)}, u32[]{:S(2)}) collective-permute-start(bf16[256,2048]{1,0:T(8,128)(2,1)} %get-tuple-element.48), channel_id=1, source_target_pairs={{0,8},{8,16},{16,24},{24,0},{1,9},{9,17},{17,25},{25,1},{2,10},{10... | collective-permute-start | bytes 3145736 | tf_op jit(solution)/shard_map/ppermute | solution.py:456
  526.9 132.5 %copy-start = (bf16[2048,512]{0,1:T(8,128)(2,1)S(1)}, bf16[2048,512]{0,1:T(8,128)(2,1)}, u32[]{:S(2)}) copy-start(bf16[2048,512]{0,1:T(8,128)(2,1)} %slice_bitcast_fusion) | copy-start | bytes 6291460
  526.9 71.6 %collective-permute-start.6 = (bf16[512,2048]{1,0:T(8,128)(2,1)}, bf16[512,2048]{1,0:T(8,128)(2,1)}, u32[]{:S(2)}, u32[]{:S(2)}) collective-permute-start(bf16[512,2048]{1,0:T(8,128)(2,1)} %get-tuple-element.50), channel_id=1, source_target_pairs={{0,8},{8,16},{16,24},{24,0},{1,9},{9,17},{17,25},{25,1},{2,10},{10... | collective-permute-start | bytes 6291464 | tf_op jit(solution)/shard_map/ppermute | solution.py:456
  526.9 73.4 %collective-permute-start.7 = (bf16[512,2048]{1,0:T(8,128)(2,1)}, bf16[512,2048]{1,0:T(8,128)(2,1)}, u32[]{:S(2)}, u32[]{:S(2)}) collective-permute-start(bf16[512,2048]{1,0:T(8,128)(2,1)} %get-tuple-element.50), channel_id=1, source_target_pairs={{0,24},{8,0},{16,8},{24,16},{1,25},{9,1},{17,9},{25,17},{2,26},{10... | collective-permute-start | bytes 6291464 | tf_op jit(solution)/shard_map/ppermute | solution.py:456
  529.6 93.7 %collective-permute-start.4 = (bf16[512,2048]{1,0:T(8,128)(2,1)}, bf16[512,2048]{1,0:T(8,128)(2,1)}, u32[]{:S(2)}, u32[]{:S(2)}) collective-permute-start(bf16[512,2048]{1,0:T(8,128)(2,1)} %get-tuple-element.49), channel_id=1, source_target_pairs={{0,8},{8,16},{16,24},{24,0},{1,9},{9,17},{17,25},{25,1},{2,10},{10... | collective-permute-start | bytes 6291464 | tf_op jit(solution)/shard_map/ppermute | solution.py:456
  532.8 63.1 %collective-permute-start.3 = (bf16[256,2048]{1,0:T(8,128)(2,1)}, bf16[256,2048]{1,0:T(8,128)(2,1)S(1)}, u32[]{:S(2)}, u32[]{:S(2)}) collective-permute-start(bf16[256,2048]{1,0:T(8,128)(2,1)} %get-tuple-element.48), channel_id=1, source_target_pairs={{0,24},{8,0},{16,8},{24,16},{1,25},{9,1},{17,9},{25,17},{2,26},{10... | collective-permute-start | bytes 3145736 | tf_op jit(solution)/shard_map/ppermute | solution.py:456
  535.5 105.4 %collective-permute-start.5 = (bf16[512,2048]{1,0:T(8,128)(2,1)}, bf16[512,2048]{1,0:T(8,128)(2,1)}, u32[]{:S(2)}, u32[]{:S(2)}) collective-permute-start(bf16[512,2048]{1,0:T(8,128)(2,1)} %get-tuple-element.49), channel_id=1, source_target_pairs={{0,24},{8,0},{16,8},{24,16},{1,25},{9,1},{17,9},{25,17},{2,26},{10... | collective-permute-start | bytes 6291464 | tf_op jit(solution)/shard_map/ppermute | solution.py:456
  595.9 60.5 %collective-permute-start.10 = (bf16[256,2048]{1,0:T(8,128)(2,1)}, bf16[256,2048]{1,0:T(8,128)(2,1)S(1)}, u32[]{:S(2)}, u32[]{:S(2)}) collective-permute-start(bf16[256,2048]{1,0:T(8,128)(2,1)} %get-tuple-element.60), channel_id=1, source_target_pairs={{0,8},{8,16},{16,24},{24,0},{1,9},{9,17},{17,25},{25,1},{2,10},{10... | collective-permute-start | bytes 3145736 | tf_op jit(solution)/shard_map/ppermute | solution.py:456
  598.5 64.9 %collective-permute-start.11 = (bf16[256,2048]{1,0:T(8,128)(2,1)}, bf16[256,2048]{1,0:T(8,128)(2,1)}, u32[]{:S(2)}, u32[]{:S(2)}) collective-permute-start(bf16[256,2048]{1,0:T(8,128)(2,1)} %get-tuple-element.60), channel_id=1, source_target_pairs={{0,24},{8,0},{16,8},{24,16},{1,25},{9,1},{17,9},{25,17},{2,26},{10... | collective-permute-start | bytes 3145736 | tf_op jit(solution)/shard_map/ppermute | solution.py:456
  600.3 68.0 %collective-permute-start.12 = (bf16[256,2048]{1,0:T(8,128)(2,1)}, bf16[256,2048]{1,0:T(8,128)(2,1)}, u32[]{:S(2)}, u32[]{:S(2)}) collective-permute-start(bf16[256,2048]{1,0:T(8,128)(2,1)} %collective-permute-done), channel_id=1, source_target_pairs={{0,8},{8,16},{16,24},{24,0},{1,9},{9,17},{17,25},{25,1},{2,10},{10... | collective-permute-start | bytes 3145736 | tf_op jit(solution)/shard_map/ppermute | solution.py:485
  623.4 62.3 %collective-permute-start.13 = (bf16[256,2048]{1,0:T(8,128)(2,1)S(1)}, bf16[256,2048]{1,0:T(8,128)(2,1)}, u32[]{:S(2)}, u32[]{:S(2)}) collective-permute-start(bf16[256,2048]{1,0:T(8,128)(2,1)S(1)} %collective-permute-done.3), channel_id=1, source_target_pairs={{0,24},{8,0},{16,8},{24,16},{1,25},{9,1},{17,9},{25,17},{2,26},{10... | collective-permute-start | bytes 3145736 | tf_op jit(solution)/shard_map/ppermute | solution.py:487
  652.6 60.6 %collective-permute-start.14 = (bf16[512,2048]{1,0:T(8,128)(2,1)}, bf16[512,2048]{1,0:T(8,128)(2,1)}, u32[]{:S(2)}, u32[]{:S(2)}) collective-permute-start(bf16[512,2048]{1,0:T(8,128)(2,1)} %collective-permute-done.4), channel_id=1, source_target_pairs={{0,8},{8,16},{16,24},{24,0},{1,9},{9,17},{17,25},{25,1},{2,10},{10... | collective-permute-start | bytes 6291464 | tf_op jit(solution)/shard_map/ppermute | solution.py:485
  656.5 74.3 %collective-permute-start.15 = (bf16[512,2048]{1,0:T(8,128)(2,1)}, bf16[512,2048]{1,0:T(8,128)(2,1)}, u32[]{:S(2)}, u32[]{:S(2)}) collective-permute-start(bf16[512,2048]{1,0:T(8,128)(2,1)} %collective-permute-done.7), channel_id=1, source_target_pairs={{0,24},{8,0},{16,8},{24,16},{1,25},{9,1},{17,9},{25,17},{2,26},{10... | collective-permute-start | bytes 6291464 | tf_op jit(solution)/shard_map/ppermute | solution.py:487
  663.3 72.3 %collective-permute-start.16 = (bf16[256,2048]{1,0:T(8,128)(2,1)}, bf16[256,2048]{1,0:T(8,128)(2,1)S(1)}, u32[]{:S(2)}, u32[]{:S(2)}) collective-permute-start(bf16[256,2048]{1,0:T(8,128)(2,1)} %collective-permute-done.8), channel_id=1, source_target_pairs={{0,8},{8,16},{16,24},{24,0},{1,9},{9,17},{17,25},{25,1},{2,10},{10... | collective-permute-start | bytes 3145736 | tf_op jit(solution)/shard_map/ppermute | solution.py:485
  668.3 84.9 %collective-permute-start.17 = (bf16[256,2048]{1,0:T(8,128)(2,1)}, bf16[256,2048]{1,0:T(8,128)(2,1)S(1)}, u32[]{:S(2)}, u32[]{:S(2)}) collective-permute-start(bf16[256,2048]{1,0:T(8,128)(2,1)} %collective-permute-done.11), channel_id=1, source_target_pairs={{0,24},{8,0},{16,8},{24,16},{1,25},{9,1},{17,9},{25,17},{2,26},{10... | collective-permute-start | bytes 3145736 | tf_op jit(solution)/shard_map/ppermute | solution.py:487
Sparse Core Ops, SparseCore 0:
  10.7 76.5 all-gather.8
  89.4 140.7 all-gather.4
  232.3 80.8 all-gather.6

commit v5 on v4

--- a/solution.py
+++ b/solution.py
@@ -15,6 +15,7 @@
 NORM_EPS = 1e-5
 MASK_VALUE = -1e30
 Q_TILE = 256
+SCORE_LIMIT = 64.0
 FF_TILE = 512
 OUT_TILE = 512
 NT_DIMS = (((1,), (1,)), ((), ()))
@@ -58,6 +59,8 @@
         return vec * cos_ref[rows, :] + jnp.where(first_half, ahead, behind) * sin_ref[rows, :]
 
     q_cols = group_size * head_dim
+    q_top = jnp.zeros((Q_TILE, 1), jnp.float32)
+    k_top = jnp.zeros((Q_TILE, 1), jnp.float32)
     for start in range(0, seq_len, Q_TILE):
         rows = pl.ds(start, Q_TILE)
         kv = qkv_ref[0, rows, q_cols:q_cols + pair].astype(jnp.float32)
@@ -68,38 +71,54 @@
         kr_scr[rows, :] = jnp.where(low_lane, bias * one_low, pltpu.roll(k_rot, head_dim, 1)).astype(jnp.bfloat16)
         vl_scr[rows, :] = jnp.where(low_lane, pltpu.roll(kv, head_dim, 1), 0.0).astype(jnp.bfloat16)
         vr_scr[rows, :] = jnp.where(low_lane, 0.0, kv).astype(jnp.bfloat16)
-
-    for start in range(0, seq_len, Q_TILE):
-        rows = pl.ds(start, Q_TILE)
-        keys = start + Q_TILE
-        causal = lax.broadcasted_iota(jnp.int32, (Q_TILE, Q_TILE), 1) <= lax.broadcasted_iota(jnp.int32, (Q_TILE, Q_TILE), 0)
-
-        def weights(query, k_scr):
-            scores = lax.dot_general(query, k_scr[:keys, :], (((1,), (1,)), ((), ())), preferred_element_type=jnp.float32)
-            parts = [scores[:, block:block + Q_TILE] for block in range(0, keys, Q_TILE)]
-            parts[-1] = jnp.where(causal, parts[-1], MASK_VALUE)
-            top = parts[0]
-            for part in parts[1:]:
-                top = jnp.maximum(top, part)
-            top = jnp.max(top, axis=1, keepdims=True)
-            parts = [jnp.exp(part - top) for part in parts]
-            total = parts[0]
-            for part in parts[1:]:
-                total = total + part
-            scale = 1.0 / jnp.sum(total, axis=1, keepdims=True)
-            return jnp.concatenate([(part * scale).astype(jnp.bfloat16) for part in parts], axis=1)
-
-        def head_pair(index, carry):
-            cols = pl.ds(pl.multiple_of(index * pair, pair), pair)
-            query = rope(qkv_ref[0, rows, cols].astype(jnp.float32), rows).astype(jnp.bfloat16).astype(jnp.float32) * head_dim ** -0.5
-            left = weights(jnp.where(low_lane, query, one_high).astype(jnp.bfloat16), kl_scr)
-            right = weights(jnp.where(low_lane, one_low, query).astype(jnp.bfloat16), kr_scr)
-            acc = jnp.dot(left, vl_scr[:keys, :], preferred_element_type=jnp.float32)
-            acc = acc + jnp.dot(right, vr_scr[:keys, :], preferred_element_type=jnp.float32)
-            out_ref[0, rows, cols] = acc.astype(jnp.bfloat16)
-            return carry
-
-        lax.fori_loop(0, group_size // 2, head_pair, 0, unroll=2)
+        k_top = jnp.maximum(k_top, jnp.sum(jnp.where(low_lane, k_rot * k_rot, 0.0), axis=1, keepdims=True))
+        for col in range(0, q_cols, pair):
+            query = qkv_ref[0, rows, col:col + pair].astype(jnp.float32)
+            q_top = jnp.maximum(q_top, jnp.sum(query * query, axis=1, keepdims=True))
+    small = jnp.max(q_top) * jnp.max(k_top) < head_dim * SCORE_LIMIT ** 2
+
+    def attend(keep_top, unroll):
+        for start in range(0, seq_len, Q_TILE):
+            rows = pl.ds(start, Q_TILE)
+            keys = start + Q_TILE
+            causal = lax.broadcasted_iota(jnp.int32, (Q_TILE, Q_TILE), 1) <= lax.broadcasted_iota(jnp.int32, (Q_TILE, Q_TILE), 0)
+
+            def weights(query, k_scr):
+                scores = lax.dot_general(query, k_scr[:keys, :], NT_DIMS, preferred_element_type=jnp.float32)
+                parts = [scores[:, block:block + Q_TILE] for block in range(0, keys, Q_TILE)]
+                parts[-1] = jnp.where(causal, parts[-1], MASK_VALUE)
+                if keep_top:
+                    top = parts[0]
+                    for part in parts[1:]:
+                        top = jnp.maximum(top, part)
+                    top = jnp.max(top, axis=1, keepdims=True)
+                    parts = [part - top for part in parts]
+                parts = [jnp.exp(part) for part in parts]
+                total = parts[0]
+                for part in parts[1:]:
+                    total = total + part
+                scale = 1.0 / jnp.sum(total, axis=1, keepdims=True)
+                return jnp.concatenate([(part * scale).astype(jnp.bfloat16) for part in parts], axis=1)
+
+            def head_pair(index, carry):
+                cols = pl.ds(pl.multiple_of(index * pair, pair), pair)
+                query = rope(qkv_ref[0, rows, cols].astype(jnp.float32), rows).astype(jnp.bfloat16).astype(jnp.float32) * head_dim ** -0.5
+                left = weights(jnp.where(low_lane, query, one_high).astype(jnp.bfloat16), kl_scr)
+                right = weights(jnp.where(low_lane, one_low, query).astype(jnp.bfloat16), kr_scr)
+                acc = jnp.dot(left, vl_scr[:keys, :], preferred_element_type=jnp.float32)
+                acc = acc + jnp.dot(right, vr_scr[:keys, :], preferred_element_type=jnp.float32)
+                out_ref[0, rows, cols] = acc.astype(jnp.bfloat16)
+                return carry
+
+            lax.fori_loop(0, group_size // 2, head_pair, 0, unroll=unroll)
+
+    @pl.when(small)
+    def _():
+        attend(False, 2)
+
+    @pl.when(jnp.logical_not(small))
+    def _():
+        attend(True, 1)
 
 
 def attention(qkv_act, lengths, cos_tab, sin_tab, kv_heads, head_dim):
@@ -230,7 +249,7 @@
     )(hidden, gain[None, :], weights)
 
 
-def down_kernel(slot, start, first, row_ref, h_ref, mid_ref, w_ref, y_in, y_ref, part_ref, h_scr, mid_scr, acc_scr, w_buf, w_sem, in_sem, out_sem):
+def down_kernel(slot, start, first, row_ref, h_ref, mid_ref, w_ref, y_in, y_ref, part_ref, h_scr, mid_scr, acc_scr, w_buf, w_sem, mid_sem, h_sem, out_sem):
     rows, dim = h_scr.shape
     depth, tile, _ = w_buf.shape
     steps = w_ref.shape[0] // tile
@@ -239,12 +258,14 @@
     def w_copy(step):
         return pltpu.make_async_copy(w_ref.at[pl.ds(pl.multiple_of(step * tile, tile), tile), :], w_buf.at[lax.rem(step, depth)], w_sem.at[lax.rem(step, depth)])
 
-    h_copy = pltpu.make_async_copy(h_ref.at[slot, pl.ds(start, rows), :], h_scr, in_sem.at[0])
-    mid_copy = pltpu.make_async_copy(mid_ref.at[pl.ds(first, rows), :], mid_scr, in_sem.at[1])
+    def mid_copy(step):
+        return pltpu.make_async_copy(mid_ref.at[pl.ds(first, rows), pl.ds(pl.multiple_of(step * tile, tile), tile)], mid_scr.at[lax.rem(step, depth)], mid_sem.at[lax.rem(step, depth)])
+
+    h_copy = pltpu.make_async_copy(h_ref.at[slot, pl.ds(start, rows), :], h_scr, h_sem)
     h_copy.start()
-    mid_copy.start()
     for step in range(min(depth - 1, steps)):
         w_copy(step).start()
+        mid_copy(step).start()
     h_copy.wait()
 
     def widen(index, carry):
@@ -253,16 +274,17 @@
         return carry
 
     lax.fori_loop(0, rows // 64, widen, 0)
-    mid_copy.wait()
 
     def body(step, carry):
         @pl.when(step + depth - 1 < steps)
         def _():
             w_copy(step + depth - 1).start()
+            mid_copy(step + depth - 1).start()
 
         w_copy(step).wait()
+        mid_copy(step).wait()
         index = lax.rem(step, depth)
-        mid = mid_scr[:, pl.ds(pl.multiple_of(step * tile, tile), tile)]
+        mid = mid_scr[index]
         for col in range(0, dim, out_tile):
             cols = slice(col, col + out_tile)
             acc_scr[:, cols] += jnp.dot(mid, w_buf[index, :, cols], preferred_element_type=jnp.float32)
@@ -297,11 +319,12 @@
         out_specs=(anywhere, anywhere),
         scratch_shapes=[
             pltpu.VMEM((rows, dim), jnp.bfloat16),
-            pltpu.VMEM((rows, ff), jnp.bfloat16),
+            pltpu.VMEM((depth, rows, tile), jnp.bfloat16),
             pltpu.VMEM((rows, dim), jnp.float32),
             pltpu.VMEM((depth, tile, dim), jnp.bfloat16),
             pltpu.SemaphoreType.DMA((depth,)),
-            pltpu.SemaphoreType.DMA((2,)),
+            pltpu.SemaphoreType.DMA((depth,)),
+            pltpu.SemaphoreType.DMA,
             pltpu.SemaphoreType.DMA((2,)),
         ],
         input_output_aliases={4: 0},
@@ -309,6 +332,76 @@
         cost_estimate=pl.CostEstimate(flops=2 * rows * dim * ff, bytes_accessed=2 * dim * ff + 2 * rows * (4 * dim + ff), transcendentals=0),
         name='down_proj',
     )(row, hidden, mid, weights, y_all)
+
+
+def place_kernel(spots, n_rows, row_ref, y_in, *refs):
+    pieces, (y_ref, buf, in_sem, out_sem) = refs[:len(spots)], refs[len(spots):]
+    block = buf.shape[1]
+    loads, stores = [], []
+    for piece, (slot, offset, start, rows) in zip(pieces, spots):
+        owner = lax.rem(row_ref[0] + offset, n_rows)
+        for first in range(0, rows, block):
+            at = len(loads)
+            loads.append(pltpu.make_async_copy(piece.at[pl.ds(first, block), :], buf.at[at], in_sem.at[at]))
+            stores.append(pltpu.make_async_copy(buf.at[at], y_ref.at[slot, owner, pl.ds(start + first, block), :], out_sem.at[at]))
+    for load in loads:
+        load.start()
+    for load, store in zip(loads, stores):
+        load.wait()
+        store.start()
+    for store in stores:
+        store.wait()
+
+
+def place(row, y_all, pieces):
+    arrays = [piece for piece, _ in pieces]
+    spots = [spot for _, spot in pieces]
+    block = min(256, *(spot[3] for spot in spots))
+    count = sum(spot[3] for spot in spots) // block
+    dim = y_all.shape[3]
+    anywhere = pl.BlockSpec(memory_space=pl.ANY)
+    moved = 2 * dim * sum(spot[3] for spot in spots)
+    return pl.pallas_call(
+        functools.partial(place_kernel, spots, y_all.shape[1]),
+        out_shape=jax.ShapeDtypeStruct(y_all.shape, y_all.dtype),
+        in_specs=[pl.BlockSpec(memory_space=pltpu.SMEM)] + [anywhere] * (1 + len(arrays)),
+        out_specs=anywhere,
+        scratch_shapes=[pltpu.VMEM((count, block, dim), jnp.bfloat16), pltpu.SemaphoreType.DMA((count,)), pltpu.SemaphoreType.DMA((count,))],
+        input_output_aliases={1: 0},
+        compiler_params=pltpu.CompilerParams(vmem_limit_bytes=40 * 1024 * 1024),
+        cost_estimate=pl.CostEstimate(flops=moved * 100, bytes_accessed=2 * moved, transcendentals=0),
+        name='place_rows',
+    )(row, y_all, *arrays)
+
+
+def relayout_kernel(row_ref, gu_ref, d_ref, gate_ref, up_ref, down_ref):
+    gate_ref[...] = jnp.transpose(gu_ref[0].astype(jnp.float32)).astype(jnp.bfloat16)
+    up_ref[...] = jnp.transpose(gu_ref[1].astype(jnp.float32)).astype(jnp.bfloat16)
+    down_ref[...] = d_ref[...]
+
+
+def relayout(row, gu_full, down_full, n_rows):
+    _, ff, dim = gu_full.shape
+    own = ff // n_rows
+    tile = min(128, own)
+    steps = own // tile
+    column = pl.BlockSpec((dim, tile), lambda j, _: (0, j))
+    return pl.pallas_call(
+        relayout_kernel,
+        out_shape=(jax.ShapeDtypeStruct((dim, own), jnp.bfloat16), jax.ShapeDtypeStruct((dim, own), jnp.bfloat16), jax.ShapeDtypeStruct((own, dim), jnp.bfloat16)),
+        grid_spec=pltpu.PrefetchScalarGridSpec(
+            num_scalar_prefetch=1,
+            grid=(steps,),
+            in_specs=[
+                pl.BlockSpec((2, tile, dim), lambda j, at: (0, at[0] * steps + j, 0)),
+                pl.BlockSpec((tile, dim), lambda j, at: (at[0] * steps + j, 0)),
+            ],
+            out_specs=(column, column, pl.BlockSpec((tile, dim), lambda j, _: (j, 0))),
+        ),
+        compiler_params=pltpu.CompilerParams(dimension_semantics=('arbitrary',), vmem_limit_bytes=40 * 1024 * 1024),
+        cost_estimate=pl.CostEstimate(flops=600 * own * dim, bytes_accessed=12 * own * dim, transcendentals=0),
+        name='relayout',
+    )(row, gu_full, down_full)
 
 
 def qkv_kernel(qkv_block, row_ref, x_ref, gain_ref, w_ref, out_ref, u_scr, w_scr):
@@ -419,7 +512,6 @@
         ff_block = w_gate_up.shape[1] // 2
         qkv_row = w_qkv.shape[1] * n_tpb
         o_row = w_o.shape[0] * n_tpb
-        ff_row = ff_block * n_tpb
 
         qkv_block = w_qkv.shape[1]
         qkvo = lax.all_gather(jnp.concatenate([w_qkv.T, w_o], axis=0), both, axis=0, tiled=False)
@@ -436,9 +528,6 @@
         hidden = out_proj(row_arg, attn_out, x_rows, qkvo, qkv_block)
 
         y_all = empty((own_batch, n_tpa, seq_len, model_dim), jnp.bfloat16)
-
-        def put(y_buf, piece, slot, owner, start):
-            return lax.dynamic_update_slice(y_buf, piece[None, None], (slot, lax.rem(owner + n_tpa, n_tpa), start, 0))
 
         spots = []
         for slot in range(own_batch):
@@ -472,10 +561,7 @@
         valid_pos = (jnp.arange(seq_len)[None, :] < len_loc[:, None])[:, :, None, None]
         k_cache = jnp.where(valid_pos, k_rot[:, :, None, :], k_buf)
         v_cache = jnp.where(valid_pos, kv_new[:, :, None, head_dim:], v_buf)
-        gu_own = lax.dynamic_slice_in_dim(gu_late, row * ff_row, ff_row, 1)
-        w_gate = gu_own[0].T
-        w_up = gu_own[1].T
-        down_rows = lax.dynamic_slice_in_dim(down_late, row * ff_row, ff_row, 0)
+        w_gate, w_up, down_rows = relayout(row_arg, gu_late, down_late, n_tpa)
         cache_outs = (k_cache, v_cache, w_query, w_key, w_value, o_rows)
         near[-3], cache_outs = lax.optimization_barrier((near[-3], cache_outs))
         k_cache, v_cache, w_query, w_key, w_value, o_rows = cache_outs
@@ -485,11 +571,22 @@
                 far = lax.ppermute(from_below, 'tpa', up_ring)
             else:
                 far = lax.ppermute(from_above, 'tpa', down_ring)
-            y_all = put(y_all, from_below, slot, row - 1, start)
-            y_all = put(y_all, from_above, slot, row + 1, start)
             fars.append(far)
-        for far, (slot, start, rows) in zip(fars, spots):
-            y_all = put(y_all, far, slot, row - 2, start)
+
+        def near_pieces(first, last):
+            for (from_below, from_above), (slot, start, rows) in list(zip(near, spots))[first:last]:
+                yield from_below, (slot, n_tpa - 1, start, rows)
+                yield from_above, (slot, 1, start, rows)
+
+        def far_pieces(first, last):
+            for far, (slot, start, rows) in list(zip(fars, spots))[first:last]:
+                yield far, (slot, n_tpa - 2, start, rows)
+
+        n_first = len(FIRST_SPLIT)
+        y_all = place(row_arg, y_all, [*near_pieces(0, n_first), *far_pieces(0, 2)])
+        y_all = place(row_arg, y_all, [*near_pieces(n_first, len(spots)), *far_pieces(2, n_first)])
+        for index in range(n_first, len(spots)):
+            y_all = place(row_arg, y_all, [*far_pieces(index, index + 1)])
         layer_out = y_all.reshape(batch_loc, seq_len, model_dim)
         return (layer_out, k_cache, v_cache, w_query, w_key, w_value, o_rows, w_gate, w_up, down_rows)
 

time: 771 us -> 749 us (0.971)
  local copies, waits for them, and re-layouts: 88.1 us -> 30.3 us
  waiting for transfers between devices: 208 us -> 228 us
  Pallas kernels: 388 us -> 404 us
    dynamic_update_slice x18 -> x0, local copies, waits for them, and re-layouts: 41.5 us -> none  [put(): lax.dynamic_update_slice(y_buf, piece[None, None], (slot, lax.rem(owner +...]
    pallas_call x0 -> x6, Pallas kernels: none -> 36.5 us  [the longest x5 20.1 us: place(): pl.pallas_call(functools.partial(place_kernel, spots, y_all.shape[1]), ou...]
    ppermute x6, waiting for transfers between devices: 23.1 us -> 55.8 us  [layer_step(): lax.ppermute(part, 'tpa', up_ring)]
    ppermute x3, waiting for transfers between devices: 28.1 us -> 0.01 us  [layer_step(): far = lax.ppermute(from_below, 'tpa', up_ring)]
    pallas_call x1, Pallas kernels: 112 us -> 95.8 us  [attention(): pl.pallas_call(functools.partial(attention_kernel, head_dim, group_size),...]
    ppermute x6, waiting for transfers between devices: 51.3 us -> 64.4 us  [layer_step(): lax.ppermute(part, 'tpa', down_ring)]
    transpose x1 -> x0, local copies, waits for them, and re-layouts: 11.2 us -> none  [layer_step(): w_up = gu_own[1].T]
    unnamed x25 -> x47, local copies, waits for them, and re-layouts: 19.8 us -> 18 us
  transfers between devices with their start and end apart: 21 -> 21, of which waited for: 11 -> 8; matrix products, arithmetic and copies ran while one was open for 16% -> 7% of each run, Pallas kernels for 40% -> 44%
where the time goes in v5:
time: 749 us; the launch traced here: 738 us
  Pallas kernels  404 us (54%)
  waiting for transfers between devices  228 us (30%)
  local copies, waits for them, and re-layouts  30.3 us (4%)
  other arithmetic  21.5 us (3%)
  starting transfers between devices  21.1 us (3%)
  matrix products  18.5 us (2%)
  between operations  14.6 us (2%)
    pallas_call x2, Pallas kernels, gate_up(): pl.pallas_call(functools.partial(gate_up_kernel, slot, start), out_shape=...  121 us
    pallas_call x1, Pallas kernels, attention(): pl.pallas_call(functools.partial(attention_kernel, head_dim, group_size),...  95.8 us
    pallas_call x6, Pallas kernels, down_proj(): pl.pallas_call(functools.partial(down_kernel, slot, start, first), out_sh...  88.8 us
    ppermute x6, waiting for transfers between devices, layer_step(): lax.ppermute(part, 'tpa', down_ring)  64.4 us
    all_gather x1, waiting for transfers between devices, layer_step(): lax.all_gather(jnp.concatenate([w_qkv.T, w_o], axis=0), both, axis=0, til...  59.3 us
    ppermute x6, waiting for transfers between devices, layer_step(): lax.ppermute(part, 'tpa', up_ring)  55.8 us
    ppermute x3, waiting for transfers between devices, layer_step(): far = lax.ppermute(from_above, 'tpa', down_ring)  46.9 us
    pallas_call x1, Pallas kernels, qkv_proj(): pl.pallas_call(functools.partial(qkv_kernel, qkv_block), out_shape=jax.Sh...  35.2 us
  transfers between devices with their start and end apart: 21, of which 8 were waited for; matrix products, arithmetic and copies ran while one was open for 7% of the time, Pallas kernels for 44%

profile of v5, /device:TPU:97, one launch (start us, length us, event | category | flops | bytes accessed | tf_op | source)
XLA Modules:
  0.0 737.9 jit_solution(15429479317202436157)
XLA Ops:
  7.3 1.9 pad_maximum_fusion
  15.4 11.9 %multiply_reduce_fusion = f32[8,1024]{1,0:T(8,128)S(1)} fusion(bf16[8,1024,2048]{2,1,0:T(8,128)(2,1)} %param.10), kind=kLoop, calls=%fused_computation.1 | loop fusion | flops 50323456 | bytes 33587200 | tf_op jit(solution)/shard_map/reduce_sum | solution.py:28
  28.0 59.3 %all-gather.9.cloned.1.call-done = bf16[4608,2048]{1,0:T(8,128)(2,1)} async-done(((bf16[144,2048]{1,0:T(8,128)(2,1)}), bf16[4608,2048]{1,0:T(8,128)(2,1)}) %all-gather.9.cloned.1.call-update) | async-done | bytes 18874384 | tf_op jit(solution)/shard_map/all_gather | solution.py:517
  87.3 35.2 %qkv_proj.1.qkv_ref = bf16[2,1024,2560]{2,1,0:T(8,128)(2,1)} custom-call(s32[1]{0:T(128)} %bitcast.row_ref, bf16[2,4,1024,2048]{3,2,1,0:T(8,128)(2,1)} %bitcast.36, bf16[1,2048]{1,0:T(2,128)(2,1)} %broadcast_in_dim.17.gain_ref, bf16[32,144,2048]{2,1,0:T(8,128)(2,1)} %bitcast.38), custom_call_target="tpu_custom_call" | custom-call | flops 21474836480 | bytes 27262976 | tf_op jit(solution)/shard_map/qkv_proj/pallas_call | solution.py:435
  122.5 95.8 %prefill_attention.1.a_ref = bf16[2,1024,2048]{2,1,0:T(8,128)(2,1)} custom-call(s32[2]{0:T(128)S(1)} %dynamic-slice_reduce_fusion.len_ref, bf16[2,1024,2560]{2,1,0:T(8,128)(2,1)} %qkv_proj.1.qkv_ref, f32[1024,128]{1,0:T(8,128)S(1)} %copy.38.cos_ref, f32[1024,128]{1,0:T(8,128)S(1)} %copy.39.sin_ref), custom_call_target="tpu_custom_call" | custom-call | flops 68719476736 | bytes 18874368 | tf_op jit(solution)/shard_map/prefill_attention/pallas_call | solution.py:133
  218.3 26.2 %out_proj.1.h_ref = bf16[2,1024,2048]{2,1,0:T(8,128)(2,1)} custom-call(s32[1]{0:T(128)} %bitcast.row_ref, bf16[2,1024,2048]{2,1,0:T(8,128)(2,1)} %prefill_attention.1.a_ref, bf16[2,4,1024,2048]{3,2,1,0:T(8,128)(2,1)} %bitcast.37, bf16[32,144,2048]{2,1,0:T(8,128)(2,1)} %bitcast.39), custom_call_target="tpu_custom_call" | custom-call | flops 17179869184 | bytes 33554432 | tf_op jit(solution)/shard_map/out_proj/pallas_call | solution.py:476
  244.5 60.7 %gate_up.3.mid_ref = bf16[1024,5632]{1,0:T(8,128)(2,1)} custom-call(bf16[2,1024,2048]{2,1,0:T(8,128)(2,1)} %out_proj.1.h_ref, bf16[1,2048]{1,0:T(2,128)(2,1)} %broadcast_in_dim.18.gain_ref, bf16[2,5632,2048]{2,1,0:T(8,128)(2,1)} %all-gather.5.cloned.1.call-done.w_ref.gu_ref), custom_call_target="tpu_custom_call" | custom-call | flops 47244640256 | bytes 61865984 | tf_op jit(solution)/shard_map/gate_up/pallas_call | solution.py:231
  305.1 60.8 %gate_up.2.mid_ref = bf16[1024,5632]{1,0:T(8,128)(2,1)} custom-call(bf16[2,1024,2048]{2,1,0:T(8,128)(2,1)} %out_proj.1.h_ref, bf16[1,2048]{1,0:T(2,128)(2,1)} %broadcast_in_dim.18.gain_ref, bf16[2,5632,2048]{2,1,0:T(8,128)(2,1)} %all-gather.5.cloned.1.call-done.w_ref.gu_ref), custom_call_target="tpu_custom_call" | custom-call | flops 47244640256 | bytes 61865984 | tf_op jit(solution)/shard_map/gate_up/pallas_call | solution.py:231
  366.0 12.5 %down_proj.6 = (bf16[2,4,1024,2048]{3,2,1,0:T(8,128)(2,1)}, bf16[256,2048]{1,0:T(8,128)(2,1)}) custom-call(s32[1]{0:T(128)} %bitcast.row_ref, bf16[2,1024,2048]{2,1,0:T(8,128)(2,1)} %out_proj.1.h_ref, bf16[1024,5632]{1,0:T(8,128)(2,1)} %gate_up.3.mid_ref, ...), custom_call_target="tpu_custom_call", output_to_operand_aliasing={{0}: (4, {})} | custom-call | flops 5905580032 | bytes 30146560 | tf_op jit(solution)/shard_map/down_proj/pallas_call | solution.py:315
  378.4 12.3 %down_proj.7 = (bf16[2,4,1024,2048]{3,2,1,0:T(8,128)(2,1)}, bf16[256,2048]{1,0:T(8,128)(2,1)}) custom-call(s32[1]{0:T(128)} %bitcast.row_ref, bf16[2,1024,2048]{2,1,0:T(8,128)(2,1)} %out_proj.1.h_ref, bf16[1024,5632]{1,0:T(8,128)(2,1)} %gate_up.3.mid_ref, ...), custom_call_target="tpu_custom_call", output_to_operand_aliasing={{0}: (4, {})} | custom-call | flops 5905580032 | bytes 30146560 | tf_op jit(solution)/shard_map/down_proj/pallas_call | solution.py:315
  390.7 19.8 %down_proj.8 = (bf16[2,4,1024,2048]{3,2,1,0:T(8,128)(2,1)}, bf16[512,2048]{1,0:T(8,128)(2,1)}) custom-call(s32[1]{0:T(128)} %bitcast.row_ref, bf16[2,1024,2048]{2,1,0:T(8,128)(2,1)} %out_proj.1.h_ref, bf16[1024,5632]{1,0:T(8,128)(2,1)} %gate_up.3.mid_ref, ...), custom_call_target="tpu_custom_call", output_to_operand_aliasing={{0}: (4, {})} | custom-call | flops 11811160064 | bytes 37224448 | tf_op jit(solution)/shard_map/down_proj/pallas_call | solution.py:315
  410.5 19.8 %down_proj.9 = (bf16[2,4,1024,2048]{3,2,1,0:T(8,128)(2,1)}, bf16[512,2048]{1,0:T(8,128)(2,1)}) custom-call(s32[1]{0:T(128)} %bitcast.row_ref, bf16[2,1024,2048]{2,1,0:T(8,128)(2,1)} %out_proj.1.h_ref, bf16[1024,5632]{1,0:T(8,128)(2,1)} %gate_up.2.mid_ref, ...), custom_call_target="tpu_custom_call", output_to_operand_aliasing={{0}: (4, {})} | custom-call | flops 11811160064 | bytes 37224448 | tf_op jit(solution)/shard_map/down_proj/pallas_call | solution.py:315
  430.3 12.3 %down_proj.10 = (bf16[2,4,1024,2048]{3,2,1,0:T(8,128)(2,1)}, bf16[256,2048]{1,0:T(8,128)(2,1)}) custom-call(s32[1]{0:T(128)} %bitcast.row_ref, bf16[2,1024,2048]{2,1,0:T(8,128)(2,1)} %out_proj.1.h_ref, bf16[1024,5632]{1,0:T(8,128)(2,1)} %gate_up.2.mid_ref, ...), custom_call_target="tpu_custom_call", output_to_operand_aliasing={{0}: (4, {})} | custom-call | flops 5905580032 | bytes 30146560 | tf_op jit(solution)/shard_map/down_proj/pallas_call | solution.py:315
  443.1 2.2 collective-permute-start.11
  445.4 2.7 collective-permute-start.9
  448.1 12.3 %down_proj.11 = (bf16[2,4,1024,2048]{3,2,1,0:T(8,128)(2,1)}, bf16[256,2048]{1,0:T(8,128)(2,1)}) custom-call(s32[1]{0:T(128)} %bitcast.row_ref, bf16[2,1024,2048]{2,1,0:T(8,128)(2,1)} %out_proj.1.h_ref, bf16[1024,5632]{1,0:T(8,128)(2,1)} %gate_up.2.mid_ref, ...), custom_call_target="tpu_custom_call", output_to_operand_aliasing={{0}: (4, {})} | custom-call | flops 5905580032 | bytes 30146560 | tf_op jit(solution)/shard_map/down_proj/pallas_call | solution.py:315
  460.5 3.6 constant_dynamic-slice_fusion
  464.1 4.6 collective-permute-done.10.refs_2_
  469.8 18.5 %fusion.3 = bf16[8,1024,128]{1,2,0:T(8,128)(2,1)} fusion(bf16[8,1024,2048]{2,1,0:T(8,128)(2,1)} %param.10, f32[2048]{0:T(1024)S(1)} %copy-done.19, f32[8,1024]{1,0:T(8,128)S(1)} %copy-done.17, bf16[640,2048]{1,0:T(8,128)(2,1)} %bitcast.42), kind=kOutput, calls=%fused_computation.6 | convolution fusion | flops 4363124736 | bytes 36216832 | tf_op jit(solution)/shard_map/dot_general | solution.py:497
  488.3 2.0 slice_bitcast_fusion.4
  490.3 44.8 %collective-permute-done.3.refs_3_ = bf16[256,2048]{1,0:T(8,128)(2,1)} collective-permute-done((bf16[256,2048]{1,0:T(8,128)(2,1)}, bf16[256,2048]{1,0:T(8,128)(2,1)}, u32[]{:S(2)}, u32[]{:S(2)}) %collective-permute-start.3) | collective-permute-done | bytes 1048608 | tf_op jit(solution)/shard_map/ppermute | solution.py:545
  535.1 3.4 collective-permute-start.5
  538.5 1.6 fusion.10
  540.2 2.6 collective-permute-start.1
  543.2 4.2 fusion.8
  547.4 1.6 slice_bitcast_fusion
  549.0 32.1 %collective-permute-done.4.refs_4_ = bf16[512,2048]{1,0:T(8,128)(2,1)} collective-permute-done((bf16[512,2048]{1,0:T(8,128)(2,1)}, bf16[512,2048]{1,0:T(8,128)(2,1)}, u32[]{:S(2)}, u32[]{:S(2)}) %collective-permute-start.4) | collective-permute-done | bytes 2097184 | tf_op jit(solution)/shard_map/ppermute | solution.py:545
  581.1 3.2 constant_dynamic-slice_fusion.1
  584.2 19.2 %collective-permute-done.refs_0_ = bf16[256,2048]{1,0:T(8,128)(2,1)S(1)} collective-permute-done((bf16[256,2048]{1,0:T(8,128)(2,1)}, bf16[256,2048]{1,0:T(8,128)(2,1)S(1)}, u32[]{:S(2)}, u32[]{:S(2)}) %collective-permute-start) | collective-permute-done | bytes 1048608 | tf_op jit(solution)/shard_map/ppermute | solution.py:545
  603.6 1.4 collective-permute-done.1.refs_1_
  606.0 3.3 collective-permute-start.7
  609.3 18.2 %collective-permute-done.13.refs_5_ = bf16[256,2048]{1,0:T(8,128)(2,1)} collective-permute-done((bf16[256,2048]{1,0:T(8,128)(2,1)}, bf16[256,2048]{1,0:T(8,128)(2,1)}, u32[]{:S(2)}, u32[]{:S(2)}) %collective-permute-start.13) | collective-permute-done | bytes 1048608 | tf_op jit(solution)/shard_map/ppermute | solution.py:545
  628.5 1.3 copy-done
  629.8 1.9 collective-permute-start.12
  631.7 16.3 %relayout.1 = (bf16[2048,1408]{1,0:T(8,128)(2,1)}, bf16[2048,1408]{1,0:T(8,128)(2,1)}, bf16[1408,2048]{1,0:T(8,128)(2,1)}) custom-call(s32[1]{0:T(128)} %bitcast.row_ref, bf16[2,5632,2048]{2,1,0:T(8,128)(2,1)} %all-gather.5.cloned.1.call-done.w_ref.gu_ref, bf16[5632,2048]{1,0:T(8,128)(2,1)} %all-gather.7.cloned.1.call-done.w_ref.d_ref), custom_call_target="tpu_custom_call" | custom-call | flops 1730150400 | bytes 34603008 | tf_op jit(solution)/shard_map/relayout/pallas_call | solution.py:389
  648.0 46.9 %collective-permute-done.7.refs_7_ = bf16[256,2048]{1,0:T(8,128)(2,1)S(1)} collective-permute-done((bf16[256,2048]{1,0:T(8,128)(2,1)}, bf16[256,2048]{1,0:T(8,128)(2,1)S(1)}, u32[]{:S(2)}, u32[]{:S(2)}) %collective-permute-start.7) | collective-permute-done | bytes 1048608 | tf_op jit(solution)/shard_map/ppermute | solution.py:573
  696.9 3.3 collective-permute-start.17
  700.3 3.9 copy.44
  704.2 1.6 copy-done.1
  705.8 1.2 copy-done.5
  707.0 1.2 copy-done.7
  708.2 1.2 copy-done.9
  709.4 1.2 copy-done.11
  710.7 6.1 place_rows.5.y_in
  716.8 7.0 place_rows.6.y_in
  723.8 2.6 place_rows.7.y_in
  726.4 2.2 place_rows.8.y_in
  728.7 2.2 place_rows.9
  (85 shorter events, 13.4 us)
Async XLA Ops:
  7.2 80.1 %all-gather.9.cloned.1.call-start = ((), (), s32[]{:S(2)}) async-start(), calls=%async_computation.2 | async-start | bytes 19464192 | tf_op jit(solution)/shard_map/all_gather | solution.py:517
  9.2 235.2 %all-gather.5.cloned.1.call-start = ((), (), s32[]{:S(2)}) async-start(), calls=%async_computation | async-start | bytes 47579136 | tf_op jit(solution)/shard_map/all_gather | solution.py:518
  10.1 355.9 %all-gather.7.cloned.1.call-start = ((), (), s32[]{:S(2)}) async-start(), calls=%async_computation.1 | async-start | bytes 23789568 | tf_op jit(solution)/shard_map/all_gather | solution.py:519
  10.9 0.7 copy-start.18
  10.9 1.9 copy-start.21
  10.9 3.7 copy-start.20
  13.4 0.7 copy-start.15
  13.4 13.9 %copy-start.13 = (f32[1024,32]{0,1:T(8,128)}, f32[1024,32]{0,1:T(8,128)S(1)}, u32[]{:S(2)}) copy-start(f32[1024,32]{0,1:T(8,128)S(1)} %get-tuple-element.104) | copy-start | bytes 393220
  430.3 15.1 %copy-start.22 = (s32[8]{0:T(128)S(1)}, s32[8]{0:T(128)}, u32[]{:S(2)}) copy-start(s32[8]{0:T(128)} %param.11) | copy-start | bytes 100
  442.6 26.1 %collective-permute-start.10 = (bf16[256,2048]{1,0:T(8,128)(2,1)}, bf16[256,2048]{1,0:T(8,128)(2,1)S(1)}, u32[]{:S(2)}, u32[]{:S(2)}) collective-permute-start(bf16[256,2048]{1,0:T(8,128)(2,1)} %get-tuple-element.58), channel_id=1, source_target_pairs={{0,8},{8,16},{16,24},{24,0},{1,9},{9,17},{17,25},{25,1},{2,10},{10... | collective-permute-start | bytes 3145736 | tf_op jit(solution)/shard_map/ppermute | solution.py:545
  443.1 25.5 %collective-permute-start.11 = (bf16[256,2048]{1,0:T(8,128)(2,1)}, bf16[256,2048]{1,0:T(8,128)(2,1)S(1)}, u32[]{:S(2)}, u32[]{:S(2)}) collective-permute-start(bf16[256,2048]{1,0:T(8,128)(2,1)} %get-tuple-element.58), channel_id=1, source_target_pairs={{0,24},{8,0},{16,8},{24,16},{1,25},{9,1},{17,9},{25,17},{2,26},{10... | collective-permute-start | bytes 3145736 | tf_op jit(solution)/shard_map/ppermute | solution.py:545
  445.4 94.8 %collective-permute-start.8 = (bf16[512,2048]{1,0:T(8,128)(2,1)}, bf16[512,2048]{1,0:T(8,128)(2,1)S(1)}, u32[]{:S(2)}, u32[]{:S(2)}) collective-permute-start(bf16[512,2048]{1,0:T(8,128)(2,1)} %get-tuple-element.53), channel_id=1, source_target_pairs={{0,8},{8,16},{16,24},{24,0},{1,9},{9,17},{17,25},{25,1},{2,10},{10... | collective-permute-start | bytes 6291464 | tf_op jit(solution)/shard_map/ppermute | solution.py:545
  445.4 97.4 %collective-permute-start.9 = (bf16[512,2048]{1,0:T(8,128)(2,1)}, bf16[512,2048]{1,0:T(8,128)(2,1)}, u32[]{:S(2)}, u32[]{:S(2)}) collective-permute-start(bf16[512,2048]{1,0:T(8,128)(2,1)} %get-tuple-element.53), channel_id=1, source_target_pairs={{0,24},{8,0},{16,8},{24,16},{1,25},{9,1},{17,9},{25,17},{2,26},{10... | collective-permute-start | bytes 6291464 | tf_op jit(solution)/shard_map/ppermute | solution.py:545
  448.1 21.7 %copy-start.17 = (f32[8,1024]{1,0:T(8,128)S(1)}, f32[8,1024]{1,0:T(8,128)}, u32[]{:S(2)}) copy-start(f32[8,1024]{1,0:T(8,128)} %add_rsqrt_fusion) | copy-start | bytes 98308
  448.1 21.7 %copy-start.19 = (f32[2048]{0:T(1024)S(1)}, f32[2048]{0:T(1024)}, u32[]{:S(2)}) copy-start(f32[2048]{0:T(1024)} %convert_element_type.31) | copy-start | bytes 24580
  460.4 74.8 %collective-permute-start.3 = (bf16[256,2048]{1,0:T(8,128)(2,1)}, bf16[256,2048]{1,0:T(8,128)(2,1)}, u32[]{:S(2)}, u32[]{:S(2)}) collective-permute-start(bf16[256,2048]{1,0:T(8,128)(2,1)} %get-tuple-element.51), channel_id=1, source_target_pairs={{0,24},{8,0},{16,8},{24,16},{1,25},{9,1},{17,9},{25,17},{2,26},{10... | collective-permute-start | bytes 3145736 | tf_op jit(solution)/shard_map/ppermute | solution.py:545
  468.6 71.5 %collective-permute-start.2 = (bf16[256,2048]{1,0:T(8,128)(2,1)}, bf16[256,2048]{1,0:T(8,128)(2,1)}, u32[]{:S(2)}, u32[]{:S(2)}) collective-permute-start(bf16[256,2048]{1,0:T(8,128)(2,1)} %get-tuple-element.51), channel_id=1, source_target_pairs={{0,8},{8,16},{16,24},{24,0},{1,9},{9,17},{17,25},{25,1},{2,10},{10... | collective-permute-start | bytes 3145736 | tf_op jit(solution)/shard_map/ppermute | solution.py:545
  468.6 1.0 copy-start.2
  469.6 111.5 %collective-permute-start.4 = (bf16[512,2048]{1,0:T(8,128)(2,1)}, bf16[512,2048]{1,0:T(8,128)(2,1)}, u32[]{:S(2)}, u32[]{:S(2)}) collective-permute-start(bf16[512,2048]{1,0:T(8,128)(2,1)} %get-tuple-element.52), channel_id=1, source_target_pairs={{0,8},{8,16},{16,24},{24,0},{1,9},{9,17},{17,25},{25,1},{2,10},{10... | collective-permute-start | bytes 6291464 | tf_op jit(solution)/shard_map/ppermute | solution.py:545
  469.8 68.8 %copy-start.14 = (f32[1024,32]{0,1:T(8,128)S(1)}, f32[1024,32]{0,1:T(8,128)}, u32[]{:S(2)}) copy-start(f32[1024,32]{0,1:T(8,128)} %copy-done.13) | copy-start | bytes 393220
  469.8 68.8 %copy-start.16 = (f32[1024,32]{0,1:T(8,128)S(1)}, f32[1024,32]{0,1:T(8,128)}, u32[]{:S(2)}) copy-start(f32[1024,32]{0,1:T(8,128)} %copy-done.15) | copy-start | bytes 393220
  488.3 59.1 %copy-start.12 = (bf16[8,80,2048]{2,1,0:T(8,128)(2,1)S(1)}, bf16[8,80,2048]{2,1,0:T(8,128)(2,1)}, u32[]{:S(2)}) copy-start(bf16[8,80,2048]{2,1,0:T(8,128)(2,1)} %constant_dynamic-slice_fusion) | copy-start | bytes 7864324
  535.1 93.4 %collective-permute-start.5 = (bf16[512,2048]{1,0:T(8,128)(2,1)}, bf16[512,2048]{1,0:T(8,128)(2,1)S(1)}, u32[]{:S(2)}, u32[]{:S(2)}) collective-permute-start(bf16[512,2048]{1,0:T(8,128)(2,1)} %get-tuple-element.52), channel_id=1, source_target_pairs={{0,24},{8,0},{16,8},{24,16},{1,25},{9,1},{17,9},{25,17},{2,26},{10... | collective-permute-start | bytes 6291464 | tf_op jit(solution)/shard_map/ppermute | solution.py:545
  540.1 63.3 %collective-permute-start = (bf16[256,2048]{1,0:T(8,128)(2,1)}, bf16[256,2048]{1,0:T(8,128)(2,1)S(1)}, u32[]{:S(2)}, u32[]{:S(2)}) collective-permute-start(bf16[256,2048]{1,0:T(8,128)(2,1)} %get-tuple-element.50), channel_id=1, source_target_pairs={{0,8},{8,16},{16,24},{24,0},{1,9},{9,17},{17,25},{25,1},{2,10},{10... | collective-permute-start | bytes 3145736 | tf_op jit(solution)/shard_map/ppermute | solution.py:545
  540.2 64.8 %collective-permute-start.1 = (bf16[256,2048]{1,0:T(8,128)(2,1)}, bf16[256,2048]{1,0:T(8,128)(2,1)S(1)}, u32[]{:S(2)}, u32[]{:S(2)}) collective-permute-start(bf16[256,2048]{1,0:T(8,128)(2,1)} %get-tuple-element.50), channel_id=1, source_target_pairs={{0,24},{8,0},{16,8},{24,16},{1,25},{9,1},{17,9},{25,17},{2,26},{10... | collective-permute-start | bytes 3145736 | tf_op jit(solution)/shard_map/ppermute | solution.py:545
  542.9 84.6 %collective-permute-start.13 = (bf16[256,2048]{1,0:T(8,128)(2,1)}, bf16[256,2048]{1,0:T(8,128)(2,1)}, u32[]{:S(2)}, u32[]{:S(2)}) collective-permute-start(bf16[256,2048]{1,0:T(8,128)(2,1)} %get-tuple-element.66), channel_id=1, source_target_pairs={{0,24},{8,0},{16,8},{24,16},{1,25},{9,1},{17,9},{25,17},{2,26},{10... | collective-permute-start | bytes 3145736 | tf_op jit(solution)/shard_map/ppermute | solution.py:545
  581.1 135.7 %collective-permute-start.14 = (bf16[512,2048]{1,0:T(8,128)(2,1)}, bf16[512,2048]{1,0:T(8,128)(2,1)}, u32[]{:S(2)}, u32[]{:S(2)}) collective-permute-start(bf16[512,2048]{1,0:T(8,128)(2,1)} %collective-permute-done.4.refs_4_), channel_id=1, source_target_pairs={{0,8},{8,16},{16,24},{24,0},{1,9},{9,17},{17,25},{25,1},{2,10},{10... | collective-permute-start | bytes 6291464 | tf_op jit(solution)/shard_map/ppermute | solution.py:571
  603.5 120.4 %collective-permute-start.15 = (bf16[512,2048]{1,0:T(8,128)(2,1)}, bf16[512,2048]{1,0:T(8,128)(2,1)}, u32[]{:S(2)}, u32[]{:S(2)}) collective-permute-start(bf16[512,2048]{1,0:T(8,128)(2,1)} %collective-permute-done.9.refs_1_), channel_id=1, source_target_pairs={{0,24},{8,0},{16,8},{24,16},{1,25},{9,1},{17,9},{25,17},{2,26},{10... | collective-permute-start | bytes 6291464 | tf_op jit(solution)/shard_map/ppermute | solution.py:573
  605.0 1.0 copy-start.6
  606.0 88.9 %collective-permute-start.7 = (bf16[256,2048]{1,0:T(8,128)(2,1)}, bf16[256,2048]{1,0:T(8,128)(2,1)S(1)}, u32[]{:S(2)}, u32[]{:S(2)}) collective-permute-start(bf16[256,2048]{1,0:T(8,128)(2,1)} %collective-permute-done.3.refs_3_), channel_id=1, source_target_pairs={{0,24},{8,0},{16,8},{24,16},{1,25},{9,1},{17,9},{25,17},{2,26},{10... | collective-permute-start | bytes 3145736 | tf_op jit(solution)/shard_map/ppermute | solution.py:573
  627.5 68.5 %collective-permute-start.6 = (bf16[256,2048]{1,0:T(8,128)(2,1)S(1)}, bf16[256,2048]{1,0:T(8,128)(2,1)S(1)}, u32[]{:S(2)}, u32[]{:S(2)}) collective-permute-start(bf16[256,2048]{1,0:T(8,128)(2,1)S(1)} %collective-permute-done.refs_0_), channel_id=1, source_target_pairs={{0,8},{8,16},{16,24},{24,0},{1,9},{9,17},{17,25},{25,1},{2,10},{10... | collective-permute-start | bytes 3145736 | tf_op jit(solution)/shard_map/ppermute | solution.py:571
  627.5 1.0 copy-start.4
  628.5 1.3 copy-start
  629.8 87.0 %collective-permute-start.12 = (bf16[256,2048]{1,0:T(8,128)(2,1)}, bf16[256,2048]{1,0:T(8,128)(2,1)}, u32[]{:S(2)}, u32[]{:S(2)}) collective-permute-start(bf16[256,2048]{1,0:T(8,128)(2,1)} %get-tuple-element.66), channel_id=1, source_target_pairs={{0,8},{8,16},{16,24},{24,0},{1,9},{9,17},{17,25},{25,1},{2,10},{10... | collective-permute-start | bytes 3145736 | tf_op jit(solution)/shard_map/ppermute | solution.py:545
  694.9 1.0 copy-start.8
  696.0 30.5 %collective-permute-start.16 = (bf16[256,2048]{1,0:T(8,128)(2,1)S(1)}, bf16[256,2048]{1,0:T(8,128)(2,1)}, u32[]{:S(2)}, u32[]{:S(2)}) collective-permute-start(bf16[256,2048]{1,0:T(8,128)(2,1)S(1)} %collective-permute-done.10.refs_2_), channel_id=1, source_target_pairs={{0,8},{8,16},{16,24},{24,0},{1,9},{9,17},{17,25},{25,1},{2,10},{10... | collective-permute-start | bytes 3145736 | tf_op jit(solution)/shard_map/ppermute | solution.py:571
  696.0 1.0 copy-start.10
  696.9 31.7 %collective-permute-start.17 = (bf16[256,2048]{1,0:T(8,128)(2,1)}, bf16[256,2048]{1,0:T(8,128)(2,1)}, u32[]{:S(2)}, u32[]{:S(2)}) collective-permute-start(bf16[256,2048]{1,0:T(8,128)(2,1)} %collective-permute-done.13.refs_5_), channel_id=1, source_target_pairs={{0,24},{8,0},{16,8},{24,16},{1,25},{9,1},{17,9},{25,17},{2,26},{10... | collective-permute-start | bytes 3145736 | tf_op jit(solution)/shard_map/ppermute | solution.py:573
  704.2 1.6 copy-start.1
  705.8 1.2 copy-start.5
  707.0 1.2 copy-start.7
  708.2 1.2 copy-start.9
  709.4 1.2 copy-start.11
  710.7 6.2 copy-start.3
Sparse Core Ops, SparseCore 0:
  10.7 76.5 all-gather.8
  89.4 140.7 all-gather.4
  232.2 80.8 all-gather.6

commit v6 on v5

--- a/solution.py
+++ b/solution.py
@@ -19,17 +19,8 @@
 FF_TILE = 512
 OUT_TILE = 512
 NT_DIMS = (((1,), (1,)), ((), ()))
-FIRST_SPLIT = (4, 4, 2)
-LATER_SPLIT = (2, 4, 4)
-
-
-def inv_rms(x_in):
-    x_wide = x_in.astype(jnp.float32)
-    return lax.rsqrt(jnp.mean(x_wide * x_wide, axis=-1, keepdims=True) + NORM_EPS)
-
-
-def scaled(x_in, inv_scale, gain_vec):
-    return (x_in.astype(jnp.float32) * inv_scale * gain_vec.astype(jnp.float32)).astype(jnp.bfloat16)
+MESH = pl.DeviceIdType.MESH
+GATES_PER_PROMPT = 2
 
 
 def rope_tables(seq_len, head_dim):
@@ -404,36 +395,242 @@
     )(row, gu_full, down_full)
 
 
-def qkv_kernel(qkv_block, row_ref, x_ref, gain_ref, w_ref, out_ref, u_scr, w_scr):
+def gather_attn_kernel(ring, kv_rows, x_ref, gain_ref, wq_ref, wo_ref, q_ref, o_ref, kv_ref, q_scr, o_scr, x_scr, u_scr, kv_scr, send_sem, recv_sem, local_sem, x_sem, out_sem, q_sem):
+    n_row, n_col = ring
+    row = lax.axis_index('tpa')
+    col = lax.axis_index('tpb')
+    core = lax.rem(col, 2)
+    chip = col // 2
+    n_chip = n_col // 2
+    far = n_row // 2
+    mate = col + 1 - 2 * core
+
+    def at_row(offset):
+        return lax.rem(row + offset + n_row, n_row)
+
+    def at_col(offset):
+        return 2 * lax.rem(chip + offset + n_chip, n_chip) + core
+
+    def peer(axis, step):
+        return {'tpa': at_row(step)} if axis == 'y' else {'tpb': at_col(step)}
+
+    barrier = pltpu.get_barrier_semaphore()
+    for axis in 'xy':
+        for step in (1, -1):
+            pl.semaphore_signal(barrier, inc=1, device_id=peer(axis, step), device_id_type=MESH)
+    pl.semaphore_signal(barrier, inc=1, device_id={'tpb': mate}, device_id_type=MESH)
+
+    offsets = (0, -1, 1, far)
+    tensors = (('q', q_scr, wq_ref, 'xy'), ('o', o_scr, wo_ref, 'yx'))
+    started = []
+    index_of = {}
+
+    def sem_at(key):
+        return index_of.setdefault(key, len(index_of))
+
+    def slot(order, first, second):
+        dx, dy = (first, second) if order == 'xy' else (second, first)
+        return at_row(dy), at_col(dx)
+
+    def halves(scr):
+        rows = scr.shape[2]
+        split = (rows // 32) * 16
+        return {1: slice(0, split), -1: slice(split, rows), 0: slice(0, rows)}
+
+    def descriptor(scr, where, part, target, key):
+        ref = scr.at[where[0], where[1], halves(scr)[part], :]
+        return pltpu.make_async_remote_copy(src_ref=ref, dst_ref=ref, send_sem=send_sem.at[sem_at(key)], recv_sem=recv_sem.at[sem_at(key)], device_id=target, device_id_type=MESH)
+
+    def send(name, scr, order, first, second, part, axis, step):
+        key = (name, first, second, part, axis, step)
+        target = {'tpb': mate} if axis == 'm' else peer(axis, step)
+        copy = descriptor(scr, slot(order, first, second), part, target, key)
+        copy.start()
+        started.append(copy)
+
+    def receive(scr, order, first, second, part, key):
+        where = slot(order, first, second)
+        descriptor(scr, where, part, {'tpb': mate}, key).wait_recv()
+
+    own_batch, _, seq_len, dim = x_ref.shape
+    rows = x_scr.shape[1]
+    per = seq_len // rows
+    tiles = own_batch * n_row * per
+
+    def fetch_x(tile):
+        slot, where = tile // (n_row * per), lax.rem(tile // per, n_row)
+        return pltpu.make_async_copy(x_ref.at[slot, where, pl.ds(pl.multiple_of(lax.rem(tile, per) * rows, rows), rows), :], x_scr.at[lax.rem(tile, 2)], x_sem.at[lax.rem(tile, 2)])
+
+    def store_kv(tile):
+        return pltpu.make_async_copy(kv_scr.at[lax.rem(tile, 2)], kv_ref.at[tile // per, :, pl.ds(pl.multiple_of(lax.rem(tile, per) * rows, rows), rows)], out_sem.at[lax.rem(tile, 2)])
+
+    own = [pltpu.make_async_copy(ref, scr.at[row, col], local_sem.at[k]) for k, (_, scr, ref, _) in enumerate(tensors)]
+    for copy in own:
+        copy.start()
+    for tile in range(min(2, tiles)):
+        fetch_x(jnp.int32(tile)).start()
+    for copy in own:
+        copy.wait()
+    pl.semaphore_wait(barrier, 5)
+
+    def spread(name, scr, order, first):
+        for step in (1, -1):
+            send(name, scr, order, first, 0, 0, order[1], step)
+        send(name, scr, order, first, 0, 0, 'm', 0)
+
+    for name, scr, _, order in tensors:
+        for step in (1, -1):
+            send(name, scr, order, 0, 0, 0, order[0], step)
+    for name, scr, _, order in tensors:
+        spread(name, scr, order, 0)
+    gain = gain_ref[...].astype(jnp.float32)
+    for step in (1, -1):
+        for name, scr, _, order in tensors:
+            receive(scr, order, -step, 0, 0, (name, 0, 0, 0, order[0], step))
+            send(name, scr, order, -step, 0, step, order[0], step)
+            spread(name, scr, order, -step)
+    for name, scr, _, order in tensors:
+        for step in (1, -1):
+            receive(scr, order, far, 0, step, (name, -step, 0, step, order[0], step))
+        spread(name, scr, order, far)
+
+    def mate_wait(name, scr, order, first, second):
+        dx, dy = (first, second) if order == 'xy' else (second, first)
+        ref = scr.at[at_row(dy), 2 * lax.rem(chip + dx + n_chip, n_chip) + 1 - core]
+        key = sem_at((name, first, second, 0, 'm', 0))
+        pltpu.make_async_remote_copy(src_ref=ref, dst_ref=ref, send_sem=send_sem.at[key], recv_sem=recv_sem.at[key], device_id={'tpb': mate}, device_id_type=MESH).wait_recv()
+
+    cols = q_scr.shape[1] * q_scr.shape[2]
+
+    def kv_tiles(first, last):
+        def body(tile, carry):
+            fetch_x(tile).wait()
+            normalise(x_scr.at[lax.rem(tile, 2)], gain, u_scr, rows)
+
+            @pl.when(tile + 2 < tiles)
+            def _():
+                fetch_x(tile + 2).start()
+
+            @pl.when(tile >= 2)
+            def _():
+                store_kv(tile - 2).wait()
+
+            weight = q_scr[row].reshape(cols, dim)[cols - kv_rows:]
+            kv_scr[lax.rem(tile, 2)] = lax.dot_general(weight, u_scr[...], NT_DIMS, preferred_element_type=jnp.float32).astype(jnp.bfloat16)
+            store_kv(tile).start()
+            return carry
+
+        lax.fori_loop(first, last, body, 0)
+
+    def store_q(offset, at):
+        return pltpu.make_async_copy(q_scr.at[at_row(offset)], q_ref.at[at_row(offset)], q_sem.at[at])
+
+    def second_hop(name, scr, order, first):
+        for step in (1, -1):
+            receive(scr, order, first, -step, 0, (name, first, 0, 0, order[1], step))
+            send(name, scr, order, first, -step, step, order[1], step)
+            send(name, scr, order, first, -step, 0, 'm', 0)
+
+    for first in offsets[:2]:
+        for name, scr, _, order in tensors:
+            second_hop(name, scr, order, first)
+    for first in offsets:
+        mate_wait('q', q_scr, 'xy', first, 0)
+    store_q(0, 0).start()
+    kv_tiles(0, tiles // 4)
+    for first in offsets[2:]:
+        for name, scr, _, order in tensors:
+            second_hop(name, scr, order, first)
+    kv_tiles(tiles // 4, tiles // 2)
+
+    def last_hop(name, scr, order):
+        for first in offsets:
+            for step in (1, -1):
+                receive(scr, order, first, far, step, (name, first, -step, step, order[1], step))
+            send(name, scr, order, first, far, 0, 'm', 0)
+
+    for second in offsets[1:3]:
+        for first in offsets:
+            mate_wait('q', q_scr, 'xy', first, second)
+        store_q(second, offsets.index(second)).start()
+    last_hop('q', q_scr, 'xy')
+    last_hop('o', o_scr, 'yx')
+    kv_tiles(tiles // 2, tiles)
+    for first in offsets:
+        mate_wait('q', q_scr, 'xy', first, far)
+    store_q(far, 3).start()
+    for second in offsets:
+        for first in offsets:
+            mate_wait('o', o_scr, 'yx', first, second)
+    o_out = pltpu.make_async_copy(o_scr, o_ref, local_sem.at[0])
+    o_out.start()
+    for copy in started:
+        copy.wait_send()
+    for tile in range(max(0, tiles - 2), tiles):
+        store_kv(jnp.int32(tile)).wait()
+    for at, offset in enumerate(offsets):
+        store_q(offset, at).wait()
+    o_out.wait()
+
+
+def gather_attn(x_rows, gain, w_qkv_t, w_o, n_row, n_col, kv_rows):
+    own_batch, _, seq_len, dim = x_rows.shape
+    q_rows, o_rows = w_qkv_t.shape[0], w_o.shape[0]
+    rows = min(512, seq_len)
+    tokens = own_batch * n_row * seq_len
+    moves = 2 * (4 + 9 * n_row)
+    anywhere = pl.BlockSpec(memory_space=pl.ANY)
+    return pl.pallas_call(
+        functools.partial(gather_attn_kernel, (n_row, n_col), kv_rows),
+        out_shape=(
+            jax.ShapeDtypeStruct((n_row, n_col, q_rows, dim), jnp.bfloat16),
+            jax.ShapeDtypeStruct((n_row, n_col, o_rows, dim), jnp.bfloat16),
+            jax.ShapeDtypeStruct((own_batch * n_row, kv_rows, seq_len), jnp.bfloat16),
+        ),
+        in_specs=[anywhere, pl.BlockSpec(memory_space=pltpu.VMEM), anywhere, anywhere],
+        out_specs=(anywhere, anywhere, anywhere),
+        scratch_shapes=[
+            pltpu.VMEM((n_row, n_col, q_rows, dim), jnp.bfloat16),
+            pltpu.VMEM((n_row, n_col, o_rows, dim), jnp.bfloat16),
+            pltpu.VMEM((2, rows, dim), jnp.bfloat16),
+            pltpu.VMEM((rows, dim), jnp.bfloat16),
+            pltpu.VMEM((2, kv_rows, rows), jnp.bfloat16),
+            pltpu.SemaphoreType.DMA((moves,)),
+            pltpu.SemaphoreType.DMA((moves,)),
+            pltpu.SemaphoreType.DMA((2,)),
+            pltpu.SemaphoreType.DMA((2,)),
+            pltpu.SemaphoreType.DMA((2,)),
+            pltpu.SemaphoreType.DMA((4,)),
+        ],
+        compiler_params=pltpu.CompilerParams(collective_id=0, has_side_effects=True, vmem_limit_bytes=58 * 1024 * 1024),
+        cost_estimate=pl.CostEstimate(flops=2 * tokens * dim * kv_rows, bytes_accessed=2 * dim * n_row * n_col * (q_rows + o_rows), transcendentals=0),
+        name='gather_attn',
+    )(x_rows, gain[None, :], w_qkv_t, w_o)
+
+
+def qkv_kernel(row_ref, x_ref, gain_ref, w_ref, out_ref, u_scr):
     piece, tile = pl.program_id(0), pl.program_id(1)
-    rows = x_ref.shape[2]
-
-    @pl.when(tile == 0)
-    def _():
-        for block in range(w_ref.shape[0]):
-            w_scr[block * qkv_block:(block + 1) * qkv_block, :] = w_ref[block, :qkv_block, :]
 
     @pl.when(piece == 0)
     def _():
-        normalise(x_ref.at[0, 0], gain_ref[...].astype(jnp.float32), u_scr.at[tile], rows)
-
-    out_ref[0] = lax.dot_general(u_scr[tile], w_scr[...], NT_DIMS, preferred_element_type=jnp.float32).astype(jnp.bfloat16)
-
-
-def qkv_proj(row, x_rows, gain, qkvo, qkv_block, pieces):
+        normalise(x_ref.at[0, 0], gain_ref[...].astype(jnp.float32), u_scr.at[tile], x_ref.shape[2])
+
+    out_ref[0] = lax.dot_general(u_scr[tile], w_ref[...], NT_DIMS, preferred_element_type=jnp.float32).astype(jnp.bfloat16)
+
+
+def qkv_proj(row, x_rows, gain, qkv_t, pieces):
     own_batch, _, seq_len, dim = x_rows.shape
-    blocks = qkvo.shape[0] // pieces
+    cols = qkv_t.shape[0] // pieces
     rows = min(512, seq_len)
     per = seq_len // rows
     tiles = own_batch * per
-    cols = blocks * qkv_block
 
     def x_index(piece, tile, own):
         at = jnp.where(piece == 0, tile, tiles - 1)
         return (at // per, own[0], at % per, 0)
 
     return pl.pallas_call(
-        functools.partial(qkv_kernel, qkv_block),
+        qkv_kernel,
         out_shape=jax.ShapeDtypeStruct((own_batch, seq_len, pieces * cols), jnp.bfloat16),
         grid_spec=pltpu.PrefetchScalarGridSpec(
             num_scalar_prefetch=1,
@@ -441,40 +638,39 @@
             in_specs=[
                 pl.BlockSpec((1, 1, rows, dim), x_index),
                 pl.BlockSpec((1, dim), lambda p, t, _: (0, 0)),
-                pl.BlockSpec((blocks,) + qkvo.shape[1:], lambda p, t, _: (p, 0, 0)),
+                pl.BlockSpec((cols, dim), lambda p, t, _: (p, 0)),
             ],
             out_specs=pl.BlockSpec((1, rows, cols), lambda p, t, _: (t // per, t % per, p)),
-            scratch_shapes=[pltpu.VMEM((tiles, rows, dim), jnp.bfloat16), pltpu.VMEM((cols, dim), jnp.bfloat16)],
+            scratch_shapes=[pltpu.VMEM((tiles, rows, dim), jnp.bfloat16)],
         ),
         compiler_params=pltpu.CompilerParams(dimension_semantics=('arbitrary', 'arbitrary'), vmem_limit_bytes=60 * 1024 * 1024),
         cost_estimate=pl.CostEstimate(flops=2 * own_batch * seq_len * dim * pieces * cols, bytes_accessed=2 * dim * (pieces * cols + 2 * own_batch * seq_len), transcendentals=0),
         name='qkv_proj',
-    )(row, x_rows, gain[None, :], qkvo)
-
-
-def out_kernel(qkv_block, row_ref, a_ref, x_ref, w_ref, h_ref, w_scr, sem):
+    )(row, x_rows, gain[None, :], qkv_t)
+
+
+def out_kernel(row_ref, a_ref, x_ref, w_ref, h_ref, w_scr, sem):
     @pl.when(pl.program_id(0) == 0)
     def _():
-        copy = pltpu.make_async_copy(w_ref.at[:, pl.ds(qkv_block, w_scr.shape[1]), :], w_scr, sem)
+        copy = pltpu.make_async_copy(w_ref, w_scr, sem)
         copy.start()
         copy.wait()
 
     dim = h_ref.shape[2]
-    depth = w_scr.shape[0] * w_scr.shape[1]
     out_tile = min(OUT_TILE, dim)
     for col in range(0, dim, out_tile):
         cols = slice(col, col + out_tile)
-        acc = jnp.dot(a_ref[0], w_scr[:, :, cols].reshape(depth, out_tile), preferred_element_type=jnp.float32)
+        acc = jnp.dot(a_ref[0], w_scr[:, cols], preferred_element_type=jnp.float32)
         h_ref[0, :, cols] = (x_ref[0, 0, :, cols].astype(jnp.float32) + acc).astype(jnp.bfloat16)
 
 
-def out_proj(row, attn, x_rows, qkvo, qkv_block):
+def out_proj(row, attn, x_rows, w_o):
     own_batch, seq_len, depth = attn.shape
     dim = x_rows.shape[3]
-    rows = min(512, seq_len)
+    rows = min(256, seq_len)
     per = seq_len // rows
     return pl.pallas_call(
-        functools.partial(out_kernel, qkv_block),
+        out_kernel,
         out_shape=jax.ShapeDtypeStruct((own_batch, seq_len, dim), jnp.bfloat16),
         grid_spec=pltpu.PrefetchScalarGridSpec(
             num_scalar_prefetch=1,
@@ -485,16 +681,12 @@
                 pl.BlockSpec(memory_space=pl.ANY),
             ],
             out_specs=pl.BlockSpec((1, rows, dim), lambda t, _: (t // per, t % per, 0)),
-            scratch_shapes=[pltpu.VMEM((qkvo.shape[0], qkvo.shape[1] - qkv_block, dim), jnp.bfloat16), pltpu.SemaphoreType.DMA],
+            scratch_shapes=[pltpu.VMEM((depth, dim), jnp.bfloat16), pltpu.SemaphoreType.DMA],
         ),
         compiler_params=pltpu.CompilerParams(dimension_semantics=('arbitrary',), vmem_limit_bytes=56 * 1024 * 1024),
         cost_estimate=pl.CostEstimate(flops=2 * own_batch * seq_len * dim * depth, bytes_accessed=2 * dim * (depth + 3 * own_batch * seq_len), transcendentals=0),
         name='out_proj',
-    )(row, attn, x_rows, qkvo)
-
-
-def matmul_t(lhs, rhs_t):
-    return lax.dot_general(lhs, rhs_t, (((lhs.ndim - 1,), (1,)), ((), ())), preferred_element_type=jnp.float32)
+    )(row, attn, x_rows, w_o)
 
 
 def solution(mesh):
@@ -513,47 +705,48 @@
         qkv_row = w_qkv.shape[1] * n_tpb
         o_row = w_o.shape[0] * n_tpb
 
-        qkv_block = w_qkv.shape[1]
-        qkvo = lax.all_gather(jnp.concatenate([w_qkv.T, w_o], axis=0), both, axis=0, tiled=False)
-        gu_full = lax.all_gather(w_gate_up.T.reshape(2, ff_block, model_dim), both, axis=1, tiled=True)
-        down_full = lax.all_gather(w_down, both, axis=0, tiled=True)
         row_arg = row.astype(jnp.int32)[None]
         cos_tab, sin_tab = rope_tables(seq_len, head_dim)
         x_rows = x_loc.reshape(own_batch, n_tpa, seq_len, model_dim)
-        inv_all = inv_rms(x_loc)
         len_own = lax.dynamic_index_in_dim(len_loc.reshape(own_batch, n_tpa), row, 1, keepdims=False)
 
-        qkv_act = qkv_proj(row_arg, x_rows, g_attn, qkvo, qkv_block, 2)
+        kv_cols = k_buf.shape[2] * head_dim
+        q_full, o_full, kv_new = gather_attn(x_rows, g_attn, w_qkv.T, w_o, n_tpa, n_tpb, 2 * kv_cols)
+        q_full, o_full, kv_new, gu_block, down_block = lax.optimization_barrier((q_full, o_full, kv_new, w_gate_up.T, w_down))
+        gu_full = lax.all_gather(gu_block.reshape(2, ff_block, model_dim), both, axis=1, tiled=True)
+        down_full = lax.all_gather(down_block, both, axis=0, tiled=True)
+        qkv_act = qkv_proj(row_arg, x_rows, g_attn, q_full.reshape(-1, model_dim), 4)
         attn_out = attention(qkv_act, len_own, cos_tab, sin_tab, n_tpa * k_buf.shape[2], head_dim)
-        hidden = out_proj(row_arg, attn_out, x_rows, qkvo, qkv_block)
+        hidden = out_proj(row_arg, attn_out, x_rows, o_full.reshape(-1, model_dim))
 
         y_all = empty((own_batch, n_tpa, seq_len, model_dim), jnp.bfloat16)
 
-        spots = []
-        for slot in range(own_batch):
-            start = 0
-            for share in FIRST_SPLIT if slot == 0 else LATER_SPLIT:
-                spots.append((slot, start, seq_len // share))
-                start += seq_len // share
+        gate_rows = seq_len // GATES_PER_PROMPT
+        gates = [(slot, start) for slot in range(own_batch) for start in range(0, seq_len, gate_rows)]
+        chunks = []
+        for index, (slot, start) in enumerate(gates):
+            parts = 2 if index in (0, len(gates) - 1) else 1
+            for part in range(parts):
+                chunks.append((index, part * gate_rows // parts, gate_rows // parts))
+        spots = [(gates[index][0], gates[index][1] + offset, rows) for index, offset, rows in chunks]
         mids = []
+        for slot, start in gates:
+            mids.append(gate_up(hidden, g_mlp, gu_full, slot, start, gate_rows))
         fars = []
         near = []
-        for slot, start, rows in spots:
-            if start == 0:
-                mids.append(gate_up(hidden, g_mlp, gu_full, slot, 0, seq_len))
-            y_all, part = down_proj(row_arg, hidden, mids[slot], down_full, y_all, slot, start, start, rows)
+        for index, (gate, offset, rows) in enumerate(chunks):
+            slot, start, _ = spots[index]
+            y_all, part = down_proj(row_arg, hidden, mids[gate], down_full, y_all, slot, start, offset, rows)
             near.append((lax.ppermute(part, 'tpa', up_ring), lax.ppermute(part, 'tpa', down_ring)))
 
-        y_all, x_late, qkvo_late, gu_late, down_late = lax.optimization_barrier((y_all, x_loc, qkvo, gu_full, down_full))
-        kv_cols = k_buf.shape[2] * head_dim
+        y_all, kv_late, o_late, q_late, gu_late, down_late = lax.optimization_barrier((y_all, kv_new, o_full, q_full, gu_full, down_full))
         q_cols = qkv_row - 2 * kv_cols
-        own_blocks = lax.dynamic_slice_in_dim(qkvo_late, row * n_tpb, n_tpb, 0)
-        qkv_own = own_blocks[:, :qkv_block].reshape(qkv_row, model_dim)
-        o_rows = own_blocks[:, qkv_block:].reshape(o_row, model_dim)
+        qkv_own = lax.dynamic_index_in_dim(q_late, row, 0, keepdims=False).reshape(qkv_row, model_dim)
+        o_rows = lax.dynamic_index_in_dim(o_late, row, 0, keepdims=False).reshape(o_row, model_dim)
         w_query = qkv_own[:q_cols].T
         w_key = qkv_own[q_cols:q_cols + kv_cols].T
         w_value = qkv_own[q_cols + kv_cols:].T
-        kv_new = matmul_t(scaled(x_late, inv_all, g_attn), qkv_own[q_cols:]).astype(jnp.bfloat16)
+        kv_new = kv_late.transpose(0, 2, 1)
         half_dim = head_dim // 2
         k_first = kv_new[..., :half_dim].astype(jnp.float32)
         k_second = kv_new[..., half_dim:head_dim].astype(jnp.float32)
@@ -563,9 +756,9 @@
         v_cache = jnp.where(valid_pos, kv_new[:, :, None, head_dim:], v_buf)
         w_gate, w_up, down_rows = relayout(row_arg, gu_late, down_late, n_tpa)
         cache_outs = (k_cache, v_cache, w_query, w_key, w_value, o_rows)
-        near[-3], cache_outs = lax.optimization_barrier((near[-3], cache_outs))
+        near[-2], cache_outs = lax.optimization_barrier((near[-2], cache_outs))
         k_cache, v_cache, w_query, w_key, w_value, o_rows = cache_outs
-        near[-2], (w_gate, w_up, down_rows) = lax.optimization_barrier((near[-2], (w_gate, w_up, down_rows)))
+        near[-1], (w_gate, w_up, down_rows) = lax.optimization_barrier((near[-1], (w_gate, w_up, down_rows)))
         for index, ((from_below, from_above), (slot, start, rows)) in enumerate(zip(near, spots)):
             if index % 2 == 0:
                 far = lax.ppermute(from_below, 'tpa', up_ring)
@@ -582,7 +775,7 @@
             for far, (slot, start, rows) in list(zip(fars, spots))[first:last]:
                 yield far, (slot, n_tpa - 2, start, rows)
 
-        n_first = len(FIRST_SPLIT)
+        n_first = len(spots) // 2
         y_all = place(row_arg, y_all, [*near_pieces(0, n_first), *far_pieces(0, 2)])
         y_all = place(row_arg, y_all, [*near_pieces(n_first, len(spots)), *far_pieces(2, n_first)])
         for index in range(n_first, len(spots)):

time: 749 us -> 779 us (1.040)
  Pallas kernels: 404 us -> 498 us
  waiting for transfers between devices: 228 us -> 201 us
  matrix products: 18.5 us -> 0 us
  other arithmetic: 21.5 us -> 3.45 us
    pallas_call x2 -> x3, Pallas kernels: 61.4 us -> 147 us  [the longest x1 82.8 us: gather_attn(): pl.pallas_call(functools.partial(gather_attn_kernel, (n_row, n_col), kv_r...]
    all_gather x3 -> x2, waiting for transfers between devices: 59.3 us -> 0.04 us  [the longest x1 0.02 us: layer_step(): lax.all_gather(gu_block.reshape(2, ff_block, model_dim), both, axis=1, ti...]
    ppermute x6, waiting for transfers between devices: 55.8 us -> 94.7 us  [layer_step(): lax.ppermute(part, 'tpa', up_ring)]
    ppermute x3, waiting for transfers between devices: 46.9 us -> 12.5 us  [layer_step(): far = lax.ppermute(from_above, 'tpa', down_ring)]
    ppermute x3, waiting for transfers between devices: 0.01 us -> 28.5 us  [layer_step(): far = lax.ppermute(from_below, 'tpa', up_ring)]
    dot_general x1 -> x0, matrix products: 18.5 us -> none  [matmul_t(): lax.dot_general(lhs, rhs_t, (((lhs.ndim - 1,), (1,)), ((), ())), preferre...]
    reduce_sum x1 -> x0, other arithmetic: 11.9 us -> none  [inv_rms(): jnp.mean(x_wide * x_wide, axis=-1, keepdims=True) + NORM_EPS]
    pallas_call x2 -> x4, Pallas kernels: 121 us -> 130 us  [gate_up(): pl.pallas_call(functools.partial(gate_up_kernel, slot, start), out_shape=...]
  transfers between devices with their start and end apart: 21 -> 20, of which waited for: 8 -> 7; matrix products, arithmetic and copies ran while one was open for 7% -> 2% of each run, Pallas kernels for 44% -> 42%
where the time goes in v6:
time: 779 us; the launch traced here: 768 us
  Pallas kernels  498 us (64%)
  waiting for transfers between devices  201 us (26%)
  local copies, waits for them, and re-layouts  30.6 us (4%)
  starting transfers between devices  20.8 us (3%)
  between operations  14.8 us (2%)
    pallas_call x4, Pallas kernels, gate_up(): pl.pallas_call(functools.partial(gate_up_kernel, slot, start), out_shape=...  130 us
    pallas_call x1, Pallas kernels, attention(): pl.pallas_call(functools.partial(attention_kernel, head_dim, group_size),...  96.7 us
    ppermute x6, waiting for transfers between devices, layer_step(): lax.ppermute(part, 'tpa', up_ring)  94.7 us
    pallas_call x6, Pallas kernels, down_proj(): pl.pallas_call(functools.partial(down_kernel, slot, start, first), out_sh...  89 us
    pallas_call x1, Pallas kernels, gather_attn(): pl.pallas_call(functools.partial(gather_attn_kernel, (n_row, n_col), kv_r...  82.8 us
    ppermute x6, waiting for transfers between devices, layer_step(): lax.ppermute(part, 'tpa', down_ring)  64.1 us
    pallas_call x1, Pallas kernels, qkv_proj(): pl.pallas_call(qkv_kernel, out_shape=jax.ShapeDtypeStruct((own_batch, seq...  39.5 us
    ppermute x3, waiting for transfers between devices, layer_step(): far = lax.ppermute(from_below, 'tpa', up_ring)  28.5 us
  transfers between devices with their start and end apart: 20, of which 7 were waited for; matrix products, arithmetic and copies ran while one was open for 2% of the time, Pallas kernels for 42%

profile of v6, /device:TPU:97, one launch (start us, length us, event | category | flops | bytes accessed | tf_op | source)
XLA Modules:
  0.0 768.0 jit_solution(10889805075733561511)
XLA Ops:
  7.3 1.3 broadcast_in_dim.17.gain_ref
  8.5 82.8 %gather_attn.1 = (bf16[4,8,80,2048]{3,2,1,0:T(8,128)(2,1)}, bf16[4,8,64,2048]{3,2,1,0:T(8,128)(2,1)}, bf16[8,128,1024]{2,1,0:T(8,128)(2,1)}) custom-call(bf16[2,4,1024,2048]{3,2,1,0:T(8,128)(2,1)} %bitcast.34, bf16[1,2048]{1,0:T(2,128)(2,1)} %broadcast_in_dim.17.gain_ref, bf16[80,2048]{1,0:T(8,128)(2,1)} %bitcast.49, bf16[64,2048]{1,0:T(8,128)(2,1)} %wo_ref.1), custom_call_target="tpu_custom_call" | custom-call | flops 4294967296 | bytes 18874368 | tf_op jit(solution)/shard_map/gather_attn/pallas_call | solution.py:583
  95.5 39.5 %qkv_proj.1.qkv_ref = bf16[2,1024,2560]{2,1,0:T(8,128)(2,1)} custom-call(s32[1]{0:T(128)} %bitcast.row_ref, bf16[2,4,1024,2048]{3,2,1,0:T(8,128)(2,1)} %bitcast.35, bf16[1,2048]{1,0:T(2,128)(2,1)} %broadcast_in_dim.17.gain_ref, bf16[2560,2048]{1,0:T(8,128)(2,1)} %bitcast.47), custom_call_target="tpu_custom_call" | custom-call | flops 21474836480 | bytes 27262976 | tf_op jit(solution)/shard_map/qkv_proj/pallas_call | solution.py:632
  135.0 96.7 %prefill_attention.1.a_ref = bf16[2,1024,2048]{2,1,0:T(8,128)(2,1)} custom-call(s32[2]{0:T(128)S(1)} %dynamic-slice_reduce_fusion.len_ref, bf16[2,1024,2560]{2,1,0:T(8,128)(2,1)} %qkv_proj.1.qkv_ref, f32[1024,128]{1,0:T(8,128)S(1)} %copy.38.cos_ref, f32[1024,128]{1,0:T(8,128)S(1)} %copy.39.sin_ref), custom_call_target="tpu_custom_call" | custom-call | flops 68719476736 | bytes 18874368 | tf_op jit(solution)/shard_map/prefill_attention/pallas_call | solution.py:124
  231.7 25.2 %out_proj.1.h_ref = bf16[2,1024,2048]{2,1,0:T(8,128)(2,1)} custom-call(s32[1]{0:T(128)} %bitcast.row_ref, bf16[2,1024,2048]{2,1,0:T(8,128)(2,1)} %prefill_attention.1.a_ref, bf16[2,4,1024,2048]{3,2,1,0:T(8,128)(2,1)} %bitcast.36, bf16[2048,2048]{1,0:T(8,128)(2,1)} %bitcast.48), custom_call_target="tpu_custom_call" | custom-call | flops 17179869184 | bytes 33554432 | tf_op jit(solution)/shard_map/out_proj/pallas_call | solution.py:672
  257.0 32.7 %gate_up.7.mid_ref = bf16[512,5632]{1,0:T(8,128)(2,1)} custom-call(bf16[2,1024,2048]{2,1,0:T(8,128)(2,1)} %out_proj.1.h_ref, bf16[1,2048]{1,0:T(2,128)(2,1)} %broadcast_in_dim.18.gain_ref, bf16[2,5632,2048]{2,1,0:T(8,128)(2,1)} %all-gather.3.cloned.1.call-done.w_ref.gu_ref), custom_call_target="tpu_custom_call" | custom-call | flops 23622320128 | bytes 54001664 | tf_op jit(solution)/shard_map/gate_up/pallas_call | solution.py:222
  289.7 32.6 %gate_up.6.mid_ref = bf16[512,5632]{1,0:T(8,128)(2,1)} custom-call(bf16[2,1024,2048]{2,1,0:T(8,128)(2,1)} %out_proj.1.h_ref, bf16[1,2048]{1,0:T(2,128)(2,1)} %broadcast_in_dim.18.gain_ref, bf16[2,5632,2048]{2,1,0:T(8,128)(2,1)} %all-gather.3.cloned.1.call-done.w_ref.gu_ref), custom_call_target="tpu_custom_call" | custom-call | flops 23622320128 | bytes 54001664 | tf_op jit(solution)/shard_map/gate_up/pallas_call | solution.py:222
  322.3 32.5 %gate_up.5.mid_ref = bf16[512,5632]{1,0:T(8,128)(2,1)} custom-call(bf16[2,1024,2048]{2,1,0:T(8,128)(2,1)} %out_proj.1.h_ref, bf16[1,2048]{1,0:T(2,128)(2,1)} %broadcast_in_dim.18.gain_ref, bf16[2,5632,2048]{2,1,0:T(8,128)(2,1)} %all-gather.3.cloned.1.call-done.w_ref.gu_ref), custom_call_target="tpu_custom_call" | custom-call | flops 23622320128 | bytes 54001664 | tf_op jit(solution)/shard_map/gate_up/pallas_call | solution.py:222
  354.8 32.5 %gate_up.4.mid_ref = bf16[512,5632]{1,0:T(8,128)(2,1)} custom-call(bf16[2,1024,2048]{2,1,0:T(8,128)(2,1)} %out_proj.1.h_ref, bf16[1,2048]{1,0:T(2,128)(2,1)} %broadcast_in_dim.18.gain_ref, bf16[2,5632,2048]{2,1,0:T(8,128)(2,1)} %all-gather.3.cloned.1.call-done.w_ref.gu_ref), custom_call_target="tpu_custom_call" | custom-call | flops 23622320128 | bytes 54001664 | tf_op jit(solution)/shard_map/gate_up/pallas_call | solution.py:222
  387.3 12.3 %down_proj.6 = (bf16[2,4,1024,2048]{3,2,1,0:T(8,128)(2,1)}, bf16[256,2048]{1,0:T(8,128)(2,1)}) custom-call(s32[1]{0:T(128)} %bitcast.row_ref, bf16[2,1024,2048]{2,1,0:T(8,128)(2,1)} %out_proj.1.h_ref, bf16[512,5632]{1,0:T(8,128)(2,1)} %gate_up.7.mid_ref, ...), custom_call_target="tpu_custom_call", output_to_operand_aliasing={{0}: (4, {})} | custom-call | flops 5905580032 | bytes 30146560 | tf_op jit(solution)/shard_map/down_proj/pallas_call | solution.py:306
  399.5 12.3 %down_proj.7 = (bf16[2,4,1024,2048]{3,2,1,0:T(8,128)(2,1)}, bf16[256,2048]{1,0:T(8,128)(2,1)}) custom-call(s32[1]{0:T(128)} %bitcast.row_ref, bf16[2,1024,2048]{2,1,0:T(8,128)(2,1)} %out_proj.1.h_ref, bf16[512,5632]{1,0:T(8,128)(2,1)} %gate_up.7.mid_ref, ...), custom_call_target="tpu_custom_call", output_to_operand_aliasing={{0}: (4, {})} | custom-call | flops 5905580032 | bytes 30146560 | tf_op jit(solution)/shard_map/down_proj/pallas_call | solution.py:306
  411.8 19.8 %down_proj.8 = (bf16[2,4,1024,2048]{3,2,1,0:T(8,128)(2,1)}, bf16[512,2048]{1,0:T(8,128)(2,1)}) custom-call(s32[1]{0:T(128)} %bitcast.row_ref, bf16[2,1024,2048]{2,1,0:T(8,128)(2,1)} %out_proj.1.h_ref, bf16[512,5632]{1,0:T(8,128)(2,1)} %gate_up.6.mid_ref, ...), custom_call_target="tpu_custom_call", output_to_operand_aliasing={{0}: (4, {})} | custom-call | flops 11811160064 | bytes 37224448 | tf_op jit(solution)/shard_map/down_proj/pallas_call | solution.py:306
  431.6 20.0 %down_proj.9 = (bf16[2,4,1024,2048]{3,2,1,0:T(8,128)(2,1)}, bf16[512,2048]{1,0:T(8,128)(2,1)}) custom-call(s32[1]{0:T(128)} %bitcast.row_ref, bf16[2,1024,2048]{2,1,0:T(8,128)(2,1)} %out_proj.1.h_ref, bf16[512,5632]{1,0:T(8,128)(2,1)} %gate_up.5.mid_ref, ...), custom_call_target="tpu_custom_call", output_to_operand_aliasing={{0}: (4, {})} | custom-call | flops 11811160064 | bytes 37224448 | tf_op jit(solution)/shard_map/down_proj/pallas_call | solution.py:306
  451.6 12.3 %down_proj.10 = (bf16[2,4,1024,2048]{3,2,1,0:T(8,128)(2,1)}, bf16[256,2048]{1,0:T(8,128)(2,1)}) custom-call(s32[1]{0:T(128)} %bitcast.row_ref, bf16[2,1024,2048]{2,1,0:T(8,128)(2,1)} %out_proj.1.h_ref, bf16[512,5632]{1,0:T(8,128)(2,1)} %gate_up.4.mid_ref, ...), custom_call_target="tpu_custom_call", output_to_operand_aliasing={{0}: (4, {})} | custom-call | flops 5905580032 | bytes 30146560 | tf_op jit(solution)/shard_map/down_proj/pallas_call | solution.py:306
  463.9 12.4 %down_proj.11 = (bf16[2,4,1024,2048]{3,2,1,0:T(8,128)(2,1)}, bf16[256,2048]{1,0:T(8,128)(2,1)}) custom-call(s32[1]{0:T(128)} %bitcast.row_ref, bf16[2,1024,2048]{2,1,0:T(8,128)(2,1)} %out_proj.1.h_ref, bf16[512,5632]{1,0:T(8,128)(2,1)} %gate_up.4.mid_ref, ...), custom_call_target="tpu_custom_call", output_to_operand_aliasing={{0}: (4, {})} | custom-call | flops 5905580032 | bytes 30146560 | tf_op jit(solution)/shard_map/down_proj/pallas_call | solution.py:306
  476.3 2.1 collective-permute-start.12
  479.9 1.8 collective-permute-start.11
  482.1 18.8 %collective-permute-done.12.refs_4_ = bf16[256,2048]{1,0:T(8,128)(2,1)S(1)} collective-permute-done((bf16[256,2048]{1,0:T(8,128)(2,1)}, bf16[256,2048]{1,0:T(8,128)(2,1)S(1)}, u32[]{:S(2)}, u32[]{:S(2)}) %collective-permute-start.12) | collective-permute-done | bytes 1048608 | tf_op jit(solution)/shard_map/ppermute | solution.py:740
  502.8 1.6 collective-permute-start.4
  504.4 19.1 %collective-permute-done.10.refs_2_ = bf16[256,2048]{1,0:T(8,128)(2,1)} collective-permute-done((bf16[256,2048]{1,0:T(8,128)(2,1)}, bf16[256,2048]{1,0:T(8,128)(2,1)}, u32[]{:S(2)}, u32[]{:S(2)}) %collective-permute-start.10) | collective-permute-done | bytes 1048608 | tf_op jit(solution)/shard_map/ppermute | solution.py:740
  523.5 1.8 collective-permute-start.9
  526.3 1.3 collective-permute-start.5
  527.6 19.2 %collective-permute-done.3.refs_3_ = bf16[256,2048]{1,0:T(8,128)(2,1)S(1)} collective-permute-done((bf16[256,2048]{1,0:T(8,128)(2,1)}, bf16[256,2048]{1,0:T(8,128)(2,1)S(1)}, u32[]{:S(2)}, u32[]{:S(2)}) %collective-permute-start.3) | collective-permute-done | bytes 1048608 | tf_op jit(solution)/shard_map/ppermute | solution.py:740
  546.7 1.4 collective-permute-start
  549.1 1.3 collective-permute-start.1
  550.5 3.3 constant_dynamic-slice_fusion
  553.8 1.9 constant_dynamic-slice_fusion.1
  556.5 56.7 %collective-permute-done.refs_0_ = bf16[256,2048]{1,0:T(8,128)(2,1)S(1)} collective-permute-done((bf16[256,2048]{1,0:T(8,128)(2,1)}, bf16[256,2048]{1,0:T(8,128)(2,1)S(1)}, u32[]{:S(2)}, u32[]{:S(2)}) %collective-permute-start) | collective-permute-done | bytes 1048608 | tf_op jit(solution)/shard_map/ppermute | solution.py:740
  614.2 45.0 %collective-permute-done.1.refs_1_ = bf16[256,2048]{1,0:T(8,128)(2,1)S(1)} collective-permute-done((bf16[256,2048]{1,0:T(8,128)(2,1)}, bf16[256,2048]{1,0:T(8,128)(2,1)S(1)}, u32[]{:S(2)}, u32[]{:S(2)}) %collective-permute-start.1) | collective-permute-done | bytes 1048608 | tf_op jit(solution)/shard_map/ppermute | solution.py:740
  659.2 1.5 collective-permute-start.7
  660.6 2.7 collective-permute-start.15
  663.7 1.4 copy-done
  665.1 2.4 fusion.4
  667.5 1.5 slice_bitcast_fusion
  669.0 12.5 %collective-permute-done.7.refs_7_ = bf16[256,2048]{1,0:T(8,128)(2,1)S(1)} collective-permute-done((bf16[256,2048]{1,0:T(8,128)(2,1)S(1)}, bf16[256,2048]{1,0:T(8,128)(2,1)S(1)}, u32[]{:S(2)}, u32[]{:S(2)}) %collective-permute-start.7) | collective-permute-done | bytes 1048608 | tf_op jit(solution)/shard_map/ppermute | solution.py:766
  682.5 1.3 collective-permute-start.16
  683.8 16.3 %relayout.1 = (bf16[2048,1408]{1,0:T(8,128)(2,1)}, bf16[2048,1408]{1,0:T(8,128)(2,1)}, bf16[1408,2048]{1,0:T(8,128)(2,1)}) custom-call(s32[1]{0:T(128)} %bitcast.row_ref, bf16[2,5632,2048]{2,1,0:T(8,128)(2,1)} %all-gather.3.cloned.1.call-done.w_ref.gu_ref, bf16[5632,2048]{1,0:T(8,128)(2,1)} %all-gather.5.cloned.1.call-done.w_ref.d_ref), custom_call_target="tpu_custom_call" | custom-call | flops 1730150400 | bytes 34603008 | tf_op jit(solution)/shard_map/relayout/pallas_call | solution.py:380
  700.2 28.5 %collective-permute-done.6.refs_6_ = bf16[256,2048]{1,0:T(8,128)(2,1)S(1)} collective-permute-done((bf16[256,2048]{1,0:T(8,128)(2,1)S(1)}, bf16[256,2048]{1,0:T(8,128)(2,1)S(1)}, u32[]{:S(2)}, u32[]{:S(2)}) %collective-permute-start.6) | collective-permute-done | bytes 1048608 | tf_op jit(solution)/shard_map/ppermute | solution.py:764
  729.9 3.9 copy.44
  733.9 1.6 copy-done.1
  735.5 1.2 copy-done.7
  736.7 1.2 copy-done.9
  737.9 1.2 copy-done.11
  742.8 5.6 place_rows.5.y_in
  748.5 5.3 place_rows.6.y_in
  753.9 2.6 place_rows.7.y_in
  756.5 2.2 place_rows.8.y_in
  758.7 2.2 place_rows.9
  (92 shorter events, 18.1 us)
Async XLA Ops:
  7.2 249.8 %all-gather.3.cloned.1.call-start = ((), (), s32[]{:S(2)}) async-start(), calls=%async_computation | async-start | bytes 47579136 | tf_op jit(solution)/shard_map/all_gather | solution.py:716
  91.4 295.9 %all-gather.5.cloned.1.call-start = ((), (), s32[]{:S(2)}) async-start(), calls=%async_computation.1 | async-start | bytes 23789568 | tf_op jit(solution)/shard_map/all_gather | solution.py:717
  92.2 0.7 copy-start.26
  92.2 2.5 copy-start.25
  93.5 41.5 %copy-start.19 = (f32[1024,32]{0,1:T(8,128)}, f32[1024,32]{0,1:T(8,128)S(1)}, u32[]{:S(2)}) copy-start(f32[1024,32]{0,1:T(8,128)S(1)} %get-tuple-element.122) | copy-start | bytes 393220
  463.8 39.0 %copy-start.28 = (bf16[512,2048]{1,0:T(8,128)(2,1)S(1)}, bf16[512,2048]{1,0:T(8,128)(2,1)}, u32[]{:S(2)}) copy-start(bf16[512,2048]{1,0:T(8,128)(2,1)} %get-tuple-element.69) | copy-start | bytes 6291460
  463.8 86.5 %copy-start.27 = (s32[8]{0:T(128)S(1)}, s32[8]{0:T(128)}, u32[]{:S(2)}) copy-start(s32[8]{0:T(128)} %param.11) | copy-start | bytes 100
  476.3 187.0 %copy-start.18 = (bf16[8,128,1024]{2,1,0:T(8,128)(2,1)S(1)}, bf16[8,128,1024]{2,1,0:T(8,128)(2,1)}, u32[]{:S(2)}) copy-start(bf16[8,128,1024]{2,1,0:T(8,128)(2,1)} %get-tuple-element.72) | copy-start | bytes 6291460
  476.3 187.0 %copy-start.20 = (f32[1024,32]{0,1:T(8,128)S(1)}, f32[1024,32]{0,1:T(8,128)}, u32[]{:S(2)}) copy-start(f32[1024,32]{0,1:T(8,128)} %copy-done.19) | copy-start | bytes 393220
  476.3 187.0 %copy-start.22 = (f32[1024,32]{0,1:T(8,128)S(1)}, f32[1024,32]{0,1:T(8,128)}, u32[]{:S(2)}) copy-start(f32[1024,32]{0,1:T(8,128)} %copy-done.21) | copy-start | bytes 393220
  476.3 24.6 %collective-permute-start.12 = (bf16[256,2048]{1,0:T(8,128)(2,1)}, bf16[256,2048]{1,0:T(8,128)(2,1)S(1)}, u32[]{:S(2)}, u32[]{:S(2)}) collective-permute-start(bf16[256,2048]{1,0:T(8,128)(2,1)} %get-tuple-element.77), channel_id=1, source_target_pairs={{0,8},{8,16},{16,24},{24,0},{1,9},{9,17},{17,25},{25,1},{2,10},{10... | collective-permute-start | bytes 3145736 | tf_op jit(solution)/shard_map/ppermute | solution.py:740
  478.4 24.4 %collective-permute-start.13 = (bf16[256,2048]{1,0:T(8,128)(2,1)}, bf16[256,2048]{1,0:T(8,128)(2,1)S(1)}, u32[]{:S(2)}, u32[]{:S(2)}) collective-permute-start(bf16[256,2048]{1,0:T(8,128)(2,1)} %get-tuple-element.77), channel_id=1, source_target_pairs={{0,24},{8,0},{16,8},{24,16},{1,25},{9,1},{17,9},{25,17},{2,26},{10... | collective-permute-start | bytes 3145736 | tf_op jit(solution)/shard_map/ppermute | solution.py:740
  479.1 44.4 %collective-permute-start.10 = (bf16[256,2048]{1,0:T(8,128)(2,1)}, bf16[256,2048]{1,0:T(8,128)(2,1)}, u32[]{:S(2)}, u32[]{:S(2)}) collective-permute-start(bf16[256,2048]{1,0:T(8,128)(2,1)} %get-tuple-element.71), channel_id=1, source_target_pairs={{0,8},{8,16},{16,24},{24,0},{1,9},{9,17},{17,25},{25,1},{2,10},{10... | collective-permute-start | bytes 3145736 | tf_op jit(solution)/shard_map/ppermute | solution.py:740
  479.9 45.4 %collective-permute-start.11 = (bf16[256,2048]{1,0:T(8,128)(2,1)}, bf16[256,2048]{1,0:T(8,128)(2,1)S(1)}, u32[]{:S(2)}, u32[]{:S(2)}) collective-permute-start(bf16[256,2048]{1,0:T(8,128)(2,1)} %get-tuple-element.71), channel_id=1, source_target_pairs={{0,24},{8,0},{16,8},{24,16},{1,25},{9,1},{17,9},{25,17},{2,26},{10... | collective-permute-start | bytes 3145736 | tf_op jit(solution)/shard_map/ppermute | solution.py:740
  481.8 65.0 %collective-permute-start.3 = (bf16[256,2048]{1,0:T(8,128)(2,1)}, bf16[256,2048]{1,0:T(8,128)(2,1)S(1)}, u32[]{:S(2)}, u32[]{:S(2)}) collective-permute-start(bf16[256,2048]{1,0:T(8,128)(2,1)} %get-tuple-element.68), channel_id=1, source_target_pairs={{0,24},{8,0},{16,8},{24,16},{1,25},{9,1},{17,9},{25,17},{2,26},{10... | collective-permute-start | bytes 3145736 | tf_op jit(solution)/shard_map/ppermute | solution.py:740
  500.9 1.0 copy-start.2
  501.9 46.2 %collective-permute-start.2 = (bf16[256,2048]{1,0:T(8,128)(2,1)}, bf16[256,2048]{1,0:T(8,128)(2,1)S(1)}, u32[]{:S(2)}, u32[]{:S(2)}) collective-permute-start(bf16[256,2048]{1,0:T(8,128)(2,1)} %get-tuple-element.68), channel_id=1, source_target_pairs={{0,8},{8,16},{16,24},{24,0},{1,9},{9,17},{17,25},{25,1},{2,10},{10... | collective-permute-start | bytes 3145736 | tf_op jit(solution)/shard_map/ppermute | solution.py:740
  502.8 157.8 %collective-permute-start.4 = (bf16[512,2048]{1,0:T(8,128)(2,1)S(1)}, bf16[512,2048]{1,0:T(8,128)(2,1)}, u32[]{:S(2)}, u32[]{:S(2)}) collective-permute-start(bf16[512,2048]{1,0:T(8,128)(2,1)S(1)} %copy-done.28), channel_id=1, source_target_pairs={{0,8},{8,16},{16,24},{24,0},{1,9},{9,17},{17,25},{25,1},{2,10},{10... | collective-permute-start | bytes 6291464 | tf_op jit(solution)/shard_map/ppermute | solution.py:740
  523.5 137.1 %collective-permute-start.9 = (bf16[512,2048]{1,0:T(8,128)(2,1)}, bf16[512,2048]{1,0:T(8,128)(2,1)S(1)}, u32[]{:S(2)}, u32[]{:S(2)}) collective-permute-start(bf16[512,2048]{1,0:T(8,128)(2,1)} %get-tuple-element.70), channel_id=1, source_target_pairs={{0,24},{8,0},{16,8},{24,16},{1,25},{9,1},{17,9},{25,17},{2,26},{10... | collective-permute-start | bytes 6291464 | tf_op jit(solution)/shard_map/ppermute | solution.py:740
  525.3 1.0 copy-start.4
  526.3 137.4 %collective-permute-start.5 = (bf16[512,2048]{1,0:T(8,128)(2,1)S(1)}, bf16[512,2048]{1,0:T(8,128)(2,1)S(1)}, u32[]{:S(2)}, u32[]{:S(2)}) collective-permute-start(bf16[512,2048]{1,0:T(8,128)(2,1)S(1)} %copy-done.28), channel_id=1, source_target_pairs={{0,24},{8,0},{16,8},{24,16},{1,25},{9,1},{17,9},{25,17},{2,26},{10... | collective-permute-start | bytes 6291464 | tf_op jit(solution)/shard_map/ppermute | solution.py:740
  546.7 117.0 %copy-start.6 = (bf16[256,2048]{1,0:T(8,128)(2,1)}, bf16[256,2048]{1,0:T(8,128)(2,1)S(1)}, u32[]{:S(2)}) copy-start(bf16[256,2048]{1,0:T(8,128)(2,1)S(1)} %collective-permute-done.3.refs_3_) | copy-start | bytes 3145732
  546.7 66.6 %collective-permute-start = (bf16[256,2048]{1,0:T(8,128)(2,1)}, bf16[256,2048]{1,0:T(8,128)(2,1)S(1)}, u32[]{:S(2)}, u32[]{:S(2)}) collective-permute-start(bf16[256,2048]{1,0:T(8,128)(2,1)} %get-tuple-element.67), channel_id=1, source_target_pairs={{0,8},{8,16},{16,24},{24,0},{1,9},{9,17},{17,25},{25,1},{2,10},{10... | collective-permute-start | bytes 3145736 | tf_op jit(solution)/shard_map/ppermute | solution.py:740
  548.1 1.0 copy-start.8
  549.1 110.1 %collective-permute-start.1 = (bf16[256,2048]{1,0:T(8,128)(2,1)}, bf16[256,2048]{1,0:T(8,128)(2,1)S(1)}, u32[]{:S(2)}, u32[]{:S(2)}) collective-permute-start(bf16[256,2048]{1,0:T(8,128)(2,1)} %get-tuple-element.67), channel_id=1, source_target_pairs={{0,24},{8,0},{16,8},{24,16},{1,25},{9,1},{17,9},{25,17},{2,26},{10... | collective-permute-start | bytes 3145736 | tf_op jit(solution)/shard_map/ppermute | solution.py:740
  550.5 114.6 %copy-start.23 = (bf16[8,1024,1,64]{1,3,2,0:T(8,128)(2,1)S(1)}, bf16[8,1024,1,64]{1,3,2,0:T(8,128)(2,1)}, u32[]{:S(2)}) copy-start(bf16[8,1024,1,64]{1,3,2,0:T(8,128)(2,1)} %param.13) | copy-start | bytes 3145732
  550.5 114.6 %copy-start.24 = (bf16[8,1024,1,64]{1,3,2,0:T(8,128)(2,1)S(1)}, bf16[8,1024,1,64]{1,3,2,0:T(8,128)(2,1)}, u32[]{:S(2)}) copy-start(bf16[8,1024,1,64]{1,3,2,0:T(8,128)(2,1)} %param.12) | copy-start | bytes 3145732
  613.3 55.7 %copy-start.10 = (bf16[256,2048]{1,0:T(8,128)(2,1)}, bf16[256,2048]{1,0:T(8,128)(2,1)S(1)}, u32[]{:S(2)}) copy-start(bf16[256,2048]{1,0:T(8,128)(2,1)S(1)} %collective-permute-done.refs_0_) | copy-start | bytes 3145732
  613.3 135.2 %collective-permute-start.8 = (bf16[512,2048]{1,0:T(8,128)(2,1)}, bf16[512,2048]{1,0:T(8,128)(2,1)}, u32[]{:S(2)}, u32[]{:S(2)}) collective-permute-start(bf16[512,2048]{1,0:T(8,128)(2,1)} %get-tuple-element.70), channel_id=1, source_target_pairs={{0,8},{8,16},{16,24},{24,0},{1,9},{9,17},{17,25},{25,1},{2,10},{10... | collective-permute-start | bytes 6291464 | tf_op jit(solution)/shard_map/ppermute | solution.py:740
  659.2 9.9 %copy-start.12 = (bf16[256,2048]{1,0:T(8,128)(2,1)}, bf16[256,2048]{1,0:T(8,128)(2,1)S(1)}, u32[]{:S(2)}) copy-start(bf16[256,2048]{1,0:T(8,128)(2,1)S(1)} %collective-permute-done.1.refs_1_) | copy-start | bytes 3145732
  659.2 22.4 %collective-permute-start.7 = (bf16[256,2048]{1,0:T(8,128)(2,1)S(1)}, bf16[256,2048]{1,0:T(8,128)(2,1)S(1)}, u32[]{:S(2)}, u32[]{:S(2)}) collective-permute-start(bf16[256,2048]{1,0:T(8,128)(2,1)S(1)} %collective-permute-done.3.refs_3_), channel_id=1, source_target_pairs={{0,24},{8,0},{16,8},{24,16},{1,25},{9,1},{17,9},{25,17},{2,26},{10... | collective-permute-start | bytes 3145736 | tf_op jit(solution)/shard_map/ppermute | solution.py:766
  660.6 87.8 %collective-permute-start.14 = (bf16[512,2048]{1,0:T(8,128)(2,1)}, bf16[512,2048]{1,0:T(8,128)(2,1)}, u32[]{:S(2)}, u32[]{:S(2)}) collective-permute-start(bf16[512,2048]{1,0:T(8,128)(2,1)} %collective-permute-done.4.refs_4_), channel_id=1, source_target_pairs={{0,8},{8,16},{16,24},{24,0},{1,9},{9,17},{17,25},{25,1},{2,10},{10... | collective-permute-start | bytes 6291464 | tf_op jit(solution)/shard_map/ppermute | solution.py:764
  660.6 93.2 %collective-permute-start.15 = (bf16[512,2048]{1,0:T(8,128)(2,1)S(1)}, bf16[512,2048]{1,0:T(8,128)(2,1)}, u32[]{:S(2)}, u32[]{:S(2)}) collective-permute-start(bf16[512,2048]{1,0:T(8,128)(2,1)S(1)} %collective-permute-done.9.refs_1_), channel_id=1, source_target_pairs={{0,24},{8,0},{16,8},{24,16},{1,25},{9,1},{17,9},{25,17},{2,26},{10... | collective-permute-start | bytes 6291464 | tf_op jit(solution)/shard_map/ppermute | solution.py:766
  663.7 1.4 copy-start
  665.1 63.6 %collective-permute-start.6 = (bf16[256,2048]{1,0:T(8,128)(2,1)S(1)}, bf16[256,2048]{1,0:T(8,128)(2,1)S(1)}, u32[]{:S(2)}, u32[]{:S(2)}) collective-permute-start(bf16[256,2048]{1,0:T(8,128)(2,1)S(1)} %collective-permute-done.refs_0_), channel_id=1, source_target_pairs={{0,8},{8,16},{16,24},{24,0},{1,9},{9,17},{17,25},{25,1},{2,10},{10... | collective-permute-start | bytes 3145736 | tf_op jit(solution)/shard_map/ppermute | solution.py:764
  681.6 1.0 copy-start.14
  682.5 73.9 %collective-permute-start.16 = (bf16[256,2048]{1,0:T(8,128)(2,1)}, bf16[256,2048]{1,0:T(8,128)(2,1)}, u32[]{:S(2)}, u32[]{:S(2)}) collective-permute-start(bf16[256,2048]{1,0:T(8,128)(2,1)} %collective-permute-done.10.refs_2_), channel_id=1, source_target_pairs={{0,8},{8,16},{16,24},{24,0},{1,9},{9,17},{17,25},{25,1},{2,10},{10... | collective-permute-start | bytes 3145736 | tf_op jit(solution)/shard_map/ppermute | solution.py:764
  728.7 1.0 copy-start.16
  729.7 29.0 %collective-permute-start.17 = (bf16[256,2048]{1,0:T(8,128)(2,1)S(1)}, bf16[256,2048]{1,0:T(8,128)(2,1)}, u32[]{:S(2)}, u32[]{:S(2)}) collective-permute-start(bf16[256,2048]{1,0:T(8,128)(2,1)S(1)} %collective-permute-done.13.refs_5_), channel_id=1, source_target_pairs={{0,24},{8,0},{16,8},{24,16},{1,25},{9,1},{17,9},{25,17},{2,26},{10... | collective-permute-start | bytes 3145736 | tf_op jit(solution)/shard_map/ppermute | solution.py:766
  733.9 1.6 copy-start.1
  735.5 1.2 copy-start.7
  736.7 1.2 copy-start.9
  737.9 1.2 copy-start.11
  739.1 1.2 copy-start.13
  740.4 1.2 copy-start.15
  741.6 1.2 copy-start.17
  742.8 5.7 copy-start.3
  742.8 5.7 copy-start.5
  (1 other events, 0.6 us)
Sparse Core Ops, SparseCore 0:
  91.5 144.3 all-gather.2
  238.0 80.8 all-gather.4

commit v7 on v6

--- a/solution.py
+++ b/solution.py
@@ -20,7 +20,7 @@
 OUT_TILE = 512
 NT_DIMS = (((1,), (1,)), ((), ()))
 MESH = pl.DeviceIdType.MESH
-GATES_PER_PROMPT = 2
+GATE_TILE = 512
 
 
 def rope_tables(seq_len, head_dim):
@@ -50,8 +50,10 @@
         return vec * cos_ref[rows, :] + jnp.where(first_half, ahead, behind) * sin_ref[rows, :]
 
     q_cols = group_size * head_dim
-    q_top = jnp.zeros((Q_TILE, 1), jnp.float32)
-    k_top = jnp.zeros((Q_TILE, 1), jnp.float32)
+    same_head = lax.broadcasted_iota(jnp.int32, (pair, pair), 0) // head_dim == lax.broadcasted_iota(jnp.int32, (pair, pair), 1) // head_dim
+    head_sum = jnp.where(same_head, 1.0, 0.0).astype(jnp.bfloat16)
+    q_top = jnp.zeros((Q_TILE, pair), jnp.float32)
+    k_top = jnp.zeros((Q_TILE, pair), jnp.float32)
     for start in range(0, seq_len, Q_TILE):
         rows = pl.ds(start, Q_TILE)
         kv = qkv_ref[0, rows, q_cols:q_cols + pair].astype(jnp.float32)
@@ -62,54 +64,62 @@
         kr_scr[rows, :] = jnp.where(low_lane, bias * one_low, pltpu.roll(k_rot, head_dim, 1)).astype(jnp.bfloat16)
         vl_scr[rows, :] = jnp.where(low_lane, pltpu.roll(kv, head_dim, 1), 0.0).astype(jnp.bfloat16)
         vr_scr[rows, :] = jnp.where(low_lane, 0.0, kv).astype(jnp.bfloat16)
-        k_top = jnp.maximum(k_top, jnp.sum(jnp.where(low_lane, k_rot * k_rot, 0.0), axis=1, keepdims=True))
+        squares = jnp.where(low_lane, k_rot * k_rot, 0.0).astype(jnp.bfloat16)
+        k_top = jnp.maximum(k_top, jnp.dot(squares, head_sum, preferred_element_type=jnp.float32))
         for col in range(0, q_cols, pair):
             query = qkv_ref[0, rows, col:col + pair].astype(jnp.float32)
-            q_top = jnp.maximum(q_top, jnp.sum(query * query, axis=1, keepdims=True))
+            squares = (query * query).astype(jnp.bfloat16)
+            q_top = jnp.maximum(q_top, jnp.dot(squares, head_sum, preferred_element_type=jnp.float32))
     small = jnp.max(q_top) * jnp.max(k_top) < head_dim * SCORE_LIMIT ** 2
 
-    def attend(keep_top, unroll):
-        for start in range(0, seq_len, Q_TILE):
-            rows = pl.ds(start, Q_TILE)
-            keys = start + Q_TILE
-            causal = lax.broadcasted_iota(jnp.int32, (Q_TILE, Q_TILE), 1) <= lax.broadcasted_iota(jnp.int32, (Q_TILE, Q_TILE), 0)
-
-            def weights(query, k_scr):
-                scores = lax.dot_general(query, k_scr[:keys, :], NT_DIMS, preferred_element_type=jnp.float32)
-                parts = [scores[:, block:block + Q_TILE] for block in range(0, keys, Q_TILE)]
-                parts[-1] = jnp.where(causal, parts[-1], MASK_VALUE)
-                if keep_top:
-                    top = parts[0]
-                    for part in parts[1:]:
-                        top = jnp.maximum(top, part)
-                    top = jnp.max(top, axis=1, keepdims=True)
-                    parts = [part - top for part in parts]
-                parts = [jnp.exp(part) for part in parts]
-                total = parts[0]
+    def attend(start, keys, keep_top, unroll):
+        rows = pl.ds(start, Q_TILE)
+        row_id = start + lax.broadcasted_iota(jnp.int32, (Q_TILE, Q_TILE), 0)
+        col_id = lax.broadcasted_iota(jnp.int32, (Q_TILE, Q_TILE), 1)
+
+        def weights(query, k_scr):
+            scores = lax.dot_general(query, k_scr[:keys, :], NT_DIMS, preferred_element_type=jnp.float32)
+            parts = [scores[:, block:block + Q_TILE] for block in range(0, keys, Q_TILE)]
+            if keep_top:
+                parts = [jnp.where(block * Q_TILE + col_id <= row_id, part, MASK_VALUE) for block, part in enumerate(parts)]
+                top = parts[0]
                 for part in parts[1:]:
-                    total = total + part
-                scale = 1.0 / jnp.sum(total, axis=1, keepdims=True)
-                return jnp.concatenate([(part * scale).astype(jnp.bfloat16) for part in parts], axis=1)
-
-            def head_pair(index, carry):
-                cols = pl.ds(pl.multiple_of(index * pair, pair), pair)
-                query = rope(qkv_ref[0, rows, cols].astype(jnp.float32), rows).astype(jnp.bfloat16).astype(jnp.float32) * head_dim ** -0.5
-                left = weights(jnp.where(low_lane, query, one_high).astype(jnp.bfloat16), kl_scr)
-                right = weights(jnp.where(low_lane, one_low, query).astype(jnp.bfloat16), kr_scr)
-                acc = jnp.dot(left, vl_scr[:keys, :], preferred_element_type=jnp.float32)
-                acc = acc + jnp.dot(right, vr_scr[:keys, :], preferred_element_type=jnp.float32)
-                out_ref[0, rows, cols] = acc.astype(jnp.bfloat16)
-                return carry
-
-            lax.fori_loop(0, group_size // 2, head_pair, 0, unroll=unroll)
+                    top = jnp.maximum(top, part)
+                top = jnp.max(top, axis=1, keepdims=True)
+                parts = [part - top for part in parts]
+            else:
+                parts[-1] = jnp.where(start + col_id <= row_id, parts[-1], MASK_VALUE)
+            parts = [jnp.exp(part) for part in parts]
+            total = parts[0]
+            for part in parts[1:]:
+                total = total + part
+            scale = 1.0 / jnp.sum(total, axis=1, keepdims=True)
+            return jnp.concatenate([(part * scale).astype(jnp.bfloat16) for part in parts], axis=1)
+
+        def head_pair(index, carry):
+            cols = pl.ds(pl.multiple_of(index * pair, pair), pair)
+            query = rope(qkv_ref[0, rows, cols].astype(jnp.float32), rows).astype(jnp.bfloat16).astype(jnp.float32) * head_dim ** -0.5
+            left = weights(jnp.where(low_lane, query, one_high).astype(jnp.bfloat16), kl_scr)
+            right = weights(jnp.where(low_lane, one_low, query).astype(jnp.bfloat16), kr_scr)
+            acc = jnp.dot(left, vl_scr[:keys, :], preferred_element_type=jnp.float32)
+            acc = acc + jnp.dot(right, vr_scr[:keys, :], preferred_element_type=jnp.float32)
+            out_ref[0, rows, cols] = acc.astype(jnp.bfloat16)
+            return carry
+
+        lax.fori_loop(0, group_size // 2, head_pair, 0, unroll=unroll)
 
     @pl.when(small)
     def _():
-        attend(False, 2)
+        for start in range(0, seq_len, Q_TILE):
+            attend(start, start + Q_TILE, False, 2)
 
     @pl.when(jnp.logical_not(small))
     def _():
-        attend(True, 1)
+        def tile(index, carry):
+            attend(pl.multiple_of(index * Q_TILE, Q_TILE), seq_len, True, 1)
+            return carry
+
+        lax.fori_loop(0, seq_len // Q_TILE, tile, 0)
 
 
 def attention(qkv_act, lengths, cos_tab, sin_tab, kv_heads, head_dim):
@@ -174,10 +184,16 @@
     h_copy.wait()
     normalise(h_scr, gain_ref[...].astype(jnp.float32), u_scr, rows)
 
-    def finish(step):
-        gate = act_scr[0].astype(jnp.float32)
-        up = act_scr[1].astype(jnp.float32)
-        mid_scr[lax.rem(step, 2)] = (jax.nn.silu(gate) * up).astype(jnp.bfloat16)
+    part_rows = min(GATE_TILE, rows)
+    parts = rows // part_rows
+
+    def span(part):
+        return pl.ds(pl.multiple_of(part * part_rows, part_rows), part_rows)
+
+    def finish(step, part):
+        gate = act_scr[0, span(part), :].astype(jnp.float32)
+        up = act_scr[1, span(part), :].astype(jnp.float32)
+        mid_scr[lax.rem(step, 2), span(part), :] = (jax.nn.silu(gate) * up).astype(jnp.bfloat16)
 
     def body(step, carry):
         @pl.when(step + depth - 1 < steps)
@@ -190,11 +206,17 @@
 
         w_copy(step).wait()
         index = lax.rem(step, depth)
-        gate = lax.dot_general(u_scr[...], w_buf[index, 0], NT_DIMS, preferred_element_type=jnp.float32)
-        up = lax.dot_general(u_scr[...], w_buf[index, 1], NT_DIMS, preferred_element_type=jnp.float32)
-        finish(step + 1)
-        act_scr[0] = gate.astype(jnp.bfloat16)
-        act_scr[1] = up.astype(jnp.bfloat16)
+
+        def rows_body(part, carry):
+            normed = u_scr[span(part), :]
+            gate = lax.dot_general(normed, w_buf[index, 0], NT_DIMS, preferred_element_type=jnp.float32)
+            up = lax.dot_general(normed, w_buf[index, 1], NT_DIMS, preferred_element_type=jnp.float32)
+            finish(step + 1, part)
+            act_scr[0, span(part), :] = gate.astype(jnp.bfloat16)
+            act_scr[1, span(part), :] = up.astype(jnp.bfloat16)
+            return carry
+
+        lax.fori_loop(0, parts, rows_body, 0)
 
         @pl.when(step >= 1)
         def _():
@@ -202,11 +224,15 @@
 
         return carry
 
-    act_scr[...] = jnp.zeros_like(act_scr)
     lax.fori_loop(0, steps, body, 0)
     if steps >= 3:
         out_copy(steps - 3).wait()
-    finish(steps - 1)
+
+    def last_rows(part, carry):
+        finish(steps - 1, part)
+        return carry
+
+    lax.fori_loop(0, parts, last_rows, 0)
     out_copy(steps - 1).start()
     if steps >= 2:
         out_copy(steps - 2).wait()
@@ -541,7 +567,7 @@
     for first in offsets[2:]:
         for name, scr, _, order in tensors:
             second_hop(name, scr, order, first)
-    kv_tiles(tiles // 4, tiles // 2)
+    kv_tiles(tiles // 4, 13 * tiles // 16)
 
     def last_hop(name, scr, order):
         for first in offsets:
@@ -555,7 +581,7 @@
         store_q(second, offsets.index(second)).start()
     last_hop('q', q_scr, 'xy')
     last_hop('o', o_scr, 'yx')
-    kv_tiles(tiles // 2, tiles)
+    kv_tiles(13 * tiles // 16, tiles)
     for first in offsets:
         mate_wait('q', q_scr, 'xy', first, far)
     store_q(far, 3).start()
@@ -715,23 +741,23 @@
         q_full, o_full, kv_new, gu_block, down_block = lax.optimization_barrier((q_full, o_full, kv_new, w_gate_up.T, w_down))
         gu_full = lax.all_gather(gu_block.reshape(2, ff_block, model_dim), both, axis=1, tiled=True)
         down_full = lax.all_gather(down_block, both, axis=0, tiled=True)
-        qkv_act = qkv_proj(row_arg, x_rows, g_attn, q_full.reshape(-1, model_dim), 4)
+        qkv_act = qkv_proj(row_arg, x_rows, g_attn, q_full.reshape(-1, model_dim), 2)
         attn_out = attention(qkv_act, len_own, cos_tab, sin_tab, n_tpa * k_buf.shape[2], head_dim)
         hidden = out_proj(row_arg, attn_out, x_rows, o_full.reshape(-1, model_dim))
 
         y_all = empty((own_batch, n_tpa, seq_len, model_dim), jnp.bfloat16)
 
-        gate_rows = seq_len // GATES_PER_PROMPT
-        gates = [(slot, start) for slot in range(own_batch) for start in range(0, seq_len, gate_rows)]
+        half = seq_len // 2
+        gates = [(0, 0, seq_len, (half // 2, half // 2, half)), (1, 0, half, (half,)), (1, half, half, (half // 2, half // 2))]
         chunks = []
-        for index, (slot, start) in enumerate(gates):
-            parts = 2 if index in (0, len(gates) - 1) else 1
-            for part in range(parts):
-                chunks.append((index, part * gate_rows // parts, gate_rows // parts))
-        spots = [(gates[index][0], gates[index][1] + offset, rows) for index, offset, rows in chunks]
+        spots = []
         mids = []
-        for slot, start in gates:
+        for index, (slot, start, gate_rows, parts) in enumerate(gates):
             mids.append(gate_up(hidden, g_mlp, gu_full, slot, start, gate_rows))
+            for part, rows in enumerate(parts):
+                offset = sum(parts[:part])
+                chunks.append((index, offset, rows))
+                spots.append((slot, start + offset, rows))
         fars = []
         near = []
         for index, (gate, offset, rows) in enumerate(chunks):

time: 779 us -> 756 us (0.970)
  Pallas kernels: 498 us -> 479 us
    pallas_call x4 -> x3, Pallas kernels: 130 us -> 127 us  [gate_up(): pl.pallas_call(functools.partial(gate_up_kernel, slot, start), out_shape=...]
where the time goes in v7:
time: 756 us; the launch traced here: 747 us
  Pallas kernels  479 us (63%)
  waiting for transfers between devices  201 us (27%)
  local copies, waits for them, and re-layouts  30.6 us (4%)
  starting transfers between devices  18.3 us (2%)
  between operations  14.5 us (2%)
    pallas_call x3, Pallas kernels, gate_up(): pl.pallas_call(functools.partial(gate_up_kernel, slot, start), out_shape=...  127 us
    ppermute x6, waiting for transfers between devices, layer_step(): lax.ppermute(part, 'tpa', up_ring)  96 us
    pallas_call x1, Pallas kernels, attention(): pl.pallas_call(functools.partial(attention_kernel, head_dim, group_size),...  93.3 us
    pallas_call x6, Pallas kernels, down_proj(): pl.pallas_call(functools.partial(down_kernel, slot, start, first), out_sh...  88.7 us
    pallas_call x1, Pallas kernels, gather_attn(): pl.pallas_call(functools.partial(gather_attn_kernel, (n_row, n_col), kv_r...  77.1 us
    ppermute x6, waiting for transfers between devices, layer_step(): lax.ppermute(part, 'tpa', down_ring)  64.3 us
    pallas_call x1, Pallas kernels, qkv_proj(): pl.pallas_call(qkv_kernel, out_shape=jax.ShapeDtypeStruct((own_batch, seq...  33.4 us
    ppermute x3, waiting for transfers between devices, layer_step(): far = lax.ppermute(from_below, 'tpa', up_ring)  29.3 us
  transfers between devices with their start and end apart: 20, of which 7 were waited for; matrix products, arithmetic and copies ran while one was open for 2% of the time, Pallas kernels for 42%

profile of v7, /device:TPU:97, one launch (start us, length us, event | category | flops | bytes accessed | tf_op | source)
XLA Modules:
  0.0 747.2 jit_solution(5337739588012710078)
XLA Ops:
  7.3 1.3 broadcast_in_dim.17.gain_ref
  8.5 77.1 %gather_attn.1 = (bf16[4,8,80,2048]{3,2,1,0:T(8,128)(2,1)}, bf16[4,8,64,2048]{3,2,1,0:T(8,128)(2,1)}, bf16[8,128,1024]{2,1,0:T(8,128)(2,1)}) custom-call(bf16[2,4,1024,2048]{3,2,1,0:T(8,128)(2,1)} %bitcast.34, bf16[1,2048]{1,0:T(2,128)(2,1)} %broadcast_in_dim.17.gain_ref, bf16[80,2048]{1,0:T(8,128)(2,1)} %bitcast.49, bf16[64,2048]{1,0:T(8,128)(2,1)} %wo_ref.1), custom_call_target="tpu_custom_call" | custom-call | flops 4294967296 | bytes 18874368 | tf_op jit(solution)/shard_map/gather_attn/pallas_call | solution.py:609
  89.9 33.4 %qkv_proj.1.qkv_ref = bf16[2,1024,2560]{2,1,0:T(8,128)(2,1)} custom-call(s32[1]{0:T(128)} %bitcast.row_ref, bf16[2,4,1024,2048]{3,2,1,0:T(8,128)(2,1)} %bitcast.35, bf16[1,2048]{1,0:T(2,128)(2,1)} %broadcast_in_dim.17.gain_ref, bf16[2560,2048]{1,0:T(8,128)(2,1)} %bitcast.47), custom_call_target="tpu_custom_call" | custom-call | flops 21474836480 | bytes 27262976 | tf_op jit(solution)/shard_map/qkv_proj/pallas_call | solution.py:658
  123.2 93.3 %prefill_attention.1.a_ref = bf16[2,1024,2048]{2,1,0:T(8,128)(2,1)} custom-call(s32[2]{0:T(128)S(1)} %dynamic-slice_reduce_fusion.len_ref, bf16[2,1024,2560]{2,1,0:T(8,128)(2,1)} %qkv_proj.1.qkv_ref, f32[1024,128]{1,0:T(8,128)S(1)} %copy.38.cos_ref, f32[1024,128]{1,0:T(8,128)S(1)} %copy.39.sin_ref), custom_call_target="tpu_custom_call" | custom-call | flops 68719476736 | bytes 18874368 | tf_op jit(solution)/shard_map/prefill_attention/pallas_call | solution.py:134
  216.5 25.5 %out_proj.1.h_ref = bf16[2,1024,2048]{2,1,0:T(8,128)(2,1)} custom-call(s32[1]{0:T(128)} %bitcast.row_ref, bf16[2,1024,2048]{2,1,0:T(8,128)(2,1)} %prefill_attention.1.a_ref, bf16[2,4,1024,2048]{3,2,1,0:T(8,128)(2,1)} %bitcast.36, bf16[2048,2048]{1,0:T(8,128)(2,1)} %bitcast.48), custom_call_target="tpu_custom_call" | custom-call | flops 17179869184 | bytes 33554432 | tf_op jit(solution)/shard_map/out_proj/pallas_call | solution.py:698
  242.1 32.7 %gate_up.4.mid_ref = bf16[512,5632]{1,0:T(8,128)(2,1)} custom-call(bf16[2,1024,2048]{2,1,0:T(8,128)(2,1)} %out_proj.1.h_ref, bf16[1,2048]{1,0:T(2,128)(2,1)} %broadcast_in_dim.18.gain_ref, bf16[2,5632,2048]{2,1,0:T(8,128)(2,1)} %all-gather.3.cloned.1.call-done.w_ref.gu_ref), custom_call_target="tpu_custom_call" | custom-call | flops 23622320128 | bytes 54001664 | tf_op jit(solution)/shard_map/gate_up/pallas_call | solution.py:248
  274.7 32.8 %gate_up.3.mid_ref = bf16[512,5632]{1,0:T(8,128)(2,1)} custom-call(bf16[2,1024,2048]{2,1,0:T(8,128)(2,1)} %out_proj.1.h_ref, bf16[1,2048]{1,0:T(2,128)(2,1)} %broadcast_in_dim.18.gain_ref, bf16[2,5632,2048]{2,1,0:T(8,128)(2,1)} %all-gather.3.cloned.1.call-done.w_ref.gu_ref), custom_call_target="tpu_custom_call" | custom-call | flops 23622320128 | bytes 54001664 | tf_op jit(solution)/shard_map/gate_up/pallas_call | solution.py:248
  307.6 61.2 %gate_up.5.mid_ref = bf16[1024,5632]{1,0:T(8,128)(2,1)} custom-call(bf16[2,1024,2048]{2,1,0:T(8,128)(2,1)} %out_proj.1.h_ref, bf16[1,2048]{1,0:T(2,128)(2,1)} %broadcast_in_dim.18.gain_ref, bf16[2,5632,2048]{2,1,0:T(8,128)(2,1)} %all-gather.3.cloned.1.call-done.w_ref.gu_ref), custom_call_target="tpu_custom_call" | custom-call | flops 47244640256 | bytes 61865984 | tf_op jit(solution)/shard_map/gate_up/pallas_call | solution.py:248
  368.8 12.3 %down_proj.6 = (bf16[2,4,1024,2048]{3,2,1,0:T(8,128)(2,1)}, bf16[256,2048]{1,0:T(8,128)(2,1)}) custom-call(s32[1]{0:T(128)} %bitcast.row_ref, bf16[2,1024,2048]{2,1,0:T(8,128)(2,1)} %out_proj.1.h_ref, bf16[1024,5632]{1,0:T(8,128)(2,1)} %gate_up.5.mid_ref, ...), custom_call_target="tpu_custom_call", output_to_operand_aliasing={{0}: (4, {})} | custom-call | flops 5905580032 | bytes 30146560 | tf_op jit(solution)/shard_map/down_proj/pallas_call | solution.py:332
  381.1 12.3 %down_proj.7 = (bf16[2,4,1024,2048]{3,2,1,0:T(8,128)(2,1)}, bf16[256,2048]{1,0:T(8,128)(2,1)}) custom-call(s32[1]{0:T(128)} %bitcast.row_ref, bf16[2,1024,2048]{2,1,0:T(8,128)(2,1)} %out_proj.1.h_ref, bf16[1024,5632]{1,0:T(8,128)(2,1)} %gate_up.5.mid_ref, ...), custom_call_target="tpu_custom_call", output_to_operand_aliasing={{0}: (4, {})} | custom-call | flops 5905580032 | bytes 30146560 | tf_op jit(solution)/shard_map/down_proj/pallas_call | solution.py:332
  393.3 19.8 %down_proj.8 = (bf16[2,4,1024,2048]{3,2,1,0:T(8,128)(2,1)}, bf16[512,2048]{1,0:T(8,128)(2,1)}) custom-call(s32[1]{0:T(128)} %bitcast.row_ref, bf16[2,1024,2048]{2,1,0:T(8,128)(2,1)} %out_proj.1.h_ref, bf16[1024,5632]{1,0:T(8,128)(2,1)} %gate_up.5.mid_ref, ...), custom_call_target="tpu_custom_call", output_to_operand_aliasing={{0}: (4, {})} | custom-call | flops 11811160064 | bytes 37224448 | tf_op jit(solution)/shard_map/down_proj/pallas_call | solution.py:332
  413.1 19.8 %down_proj.9 = (bf16[2,4,1024,2048]{3,2,1,0:T(8,128)(2,1)}, bf16[512,2048]{1,0:T(8,128)(2,1)}) custom-call(s32[1]{0:T(128)} %bitcast.row_ref, bf16[2,1024,2048]{2,1,0:T(8,128)(2,1)} %out_proj.1.h_ref, bf16[512,5632]{1,0:T(8,128)(2,1)} %gate_up.4.mid_ref, ...), custom_call_target="tpu_custom_call", output_to_operand_aliasing={{0}: (4, {})} | custom-call | flops 11811160064 | bytes 37224448 | tf_op jit(solution)/shard_map/down_proj/pallas_call | solution.py:332
  432.9 12.3 %down_proj.10 = (bf16[2,4,1024,2048]{3,2,1,0:T(8,128)(2,1)}, bf16[256,2048]{1,0:T(8,128)(2,1)}) custom-call(s32[1]{0:T(128)} %bitcast.row_ref, bf16[2,1024,2048]{2,1,0:T(8,128)(2,1)} %out_proj.1.h_ref, bf16[512,5632]{1,0:T(8,128)(2,1)} %gate_up.3.mid_ref, ...), custom_call_target="tpu_custom_call", output_to_operand_aliasing={{0}: (4, {})} | custom-call | flops 5905580032 | bytes 30146560 | tf_op jit(solution)/shard_map/down_proj/pallas_call | solution.py:332
  445.2 12.4 %down_proj.11 = (bf16[2,4,1024,2048]{3,2,1,0:T(8,128)(2,1)}, bf16[256,2048]{1,0:T(8,128)(2,1)}) custom-call(s32[1]{0:T(128)} %bitcast.row_ref, bf16[2,1024,2048]{2,1,0:T(8,128)(2,1)} %out_proj.1.h_ref, bf16[512,5632]{1,0:T(8,128)(2,1)} %gate_up.3.mid_ref, ...), custom_call_target="tpu_custom_call", output_to_operand_aliasing={{0}: (4, {})} | custom-call | flops 5905580032 | bytes 30146560 | tf_op jit(solution)/shard_map/down_proj/pallas_call | solution.py:332
  457.6 1.4 collective-permute-start.12
  459.0 1.4 collective-permute-start.13
  460.7 2.4 collective-permute-start.11
  463.1 18.3 %collective-permute-done.12.refs_4_ = bf16[256,2048]{1,0:T(8,128)(2,1)S(1)} collective-permute-done((bf16[256,2048]{1,0:T(8,128)(2,1)}, bf16[256,2048]{1,0:T(8,128)(2,1)S(1)}, u32[]{:S(2)}, u32[]{:S(2)}) %collective-permute-start.12) | collective-permute-done | bytes 1048608 | tf_op jit(solution)/shard_map/ppermute | solution.py:766
  482.4 1.5 collective-permute-start.4
  483.9 20.1 %collective-permute-done.10.refs_2_ = bf16[256,2048]{1,0:T(8,128)(2,1)} collective-permute-done((bf16[256,2048]{1,0:T(8,128)(2,1)}, bf16[256,2048]{1,0:T(8,128)(2,1)}, u32[]{:S(2)}, u32[]{:S(2)}) %collective-permute-start.10) | collective-permute-done | bytes 1048608 | tf_op jit(solution)/shard_map/ppermute | solution.py:766
  505.2 2.1 collective-permute-start.5
  507.3 19.1 %collective-permute-done.3.refs_3_ = bf16[256,2048]{1,0:T(8,128)(2,1)S(1)} collective-permute-done((bf16[256,2048]{1,0:T(8,128)(2,1)}, bf16[256,2048]{1,0:T(8,128)(2,1)S(1)}, u32[]{:S(2)}, u32[]{:S(2)}) %collective-permute-start.3) | collective-permute-done | bytes 1048608 | tf_op jit(solution)/shard_map/ppermute | solution.py:766
  528.6 1.5 collective-permute-start.1
  530.2 3.3 constant_dynamic-slice_fusion
  533.5 1.9 constant_dynamic-slice_fusion.1
  536.2 57.5 %collective-permute-done.refs_0_ = bf16[256,2048]{1,0:T(8,128)(2,1)S(1)} collective-permute-done((bf16[256,2048]{1,0:T(8,128)(2,1)}, bf16[256,2048]{1,0:T(8,128)(2,1)S(1)}, u32[]{:S(2)}, u32[]{:S(2)}) %collective-permute-start) | collective-permute-done | bytes 1048608 | tf_op jit(solution)/shard_map/ppermute | solution.py:766
  593.8 45.1 %collective-permute-done.1.refs_1_ = bf16[256,2048]{1,0:T(8,128)(2,1)S(1)} collective-permute-done((bf16[256,2048]{1,0:T(8,128)(2,1)}, bf16[256,2048]{1,0:T(8,128)(2,1)S(1)}, u32[]{:S(2)}, u32[]{:S(2)}) %collective-permute-start.1) | collective-permute-done | bytes 1048608 | tf_op jit(solution)/shard_map/ppermute | solution.py:766
  638.9 2.2 collective-permute-start.7
  641.1 2.7 collective-permute-start.15
  644.2 1.3 copy-done
  645.5 2.4 fusion.4
  648.0 1.5 slice_bitcast_fusion
  649.4 11.2 %collective-permute-done.7.refs_7_ = bf16[256,2048]{1,0:T(8,128)(2,1)S(1)} collective-permute-done((bf16[256,2048]{1,0:T(8,128)(2,1)S(1)}, bf16[256,2048]{1,0:T(8,128)(2,1)S(1)}, u32[]{:S(2)}, u32[]{:S(2)}) %collective-permute-start.7) | collective-permute-done | bytes 1048608 | tf_op jit(solution)/shard_map/ppermute | solution.py:792
  662.7 16.3 %relayout.1 = (bf16[2048,1408]{1,0:T(8,128)(2,1)}, bf16[2048,1408]{1,0:T(8,128)(2,1)}, bf16[1408,2048]{1,0:T(8,128)(2,1)}) custom-call(s32[1]{0:T(128)} %bitcast.row_ref, bf16[2,5632,2048]{2,1,0:T(8,128)(2,1)} %all-gather.3.cloned.1.call-done.w_ref.gu_ref, bf16[5632,2048]{1,0:T(8,128)(2,1)} %all-gather.5.cloned.1.call-done.w_ref.d_ref), custom_call_target="tpu_custom_call" | custom-call | flops 1730150400 | bytes 34603008 | tf_op jit(solution)/shard_map/relayout/pallas_call | solution.py:406
  679.1 29.3 %collective-permute-done.6.refs_6_ = bf16[256,2048]{1,0:T(8,128)(2,1)S(1)} collective-permute-done((bf16[256,2048]{1,0:T(8,128)(2,1)S(1)}, bf16[256,2048]{1,0:T(8,128)(2,1)S(1)}, u32[]{:S(2)}, u32[]{:S(2)}) %collective-permute-start.6) | collective-permute-done | bytes 1048608 | tf_op jit(solution)/shard_map/ppermute | solution.py:790
  709.3 3.9 copy.44
  713.3 1.6 copy-done.1
  714.8 1.2 copy-done.7
  716.1 1.2 copy-done.9
  717.3 1.2 copy-done.11
  718.5 1.2 copy-done.13
  719.7 1.2 copy-done.15
  721.0 1.2 copy-done.17
  722.2 5.6 place_rows.5.y_in
  727.9 5.3 place_rows.6.y_in
  733.3 2.6 place_rows.7.y_in
  735.8 2.2 place_rows.8.y_in
  738.1 2.2 place_rows.9
  (91 shorter events, 13.2 us)
Async XLA Ops:
  7.2 234.9 %all-gather.3.cloned.1.call-start = ((), (), s32[]{:S(2)}) async-start(), calls=%async_computation | async-start | bytes 47579136 | tf_op jit(solution)/shard_map/all_gather | solution.py:742
  85.7 283.0 %all-gather.5.cloned.1.call-start = ((), (), s32[]{:S(2)}) async-start(), calls=%async_computation.1 | async-start | bytes 23789568 | tf_op jit(solution)/shard_map/all_gather | solution.py:743
  86.6 0.7 copy-start.26
  86.6 2.5 copy-start.25
  87.9 35.3 %copy-start.19 = (f32[1024,32]{0,1:T(8,128)}, f32[1024,32]{0,1:T(8,128)S(1)}, u32[]{:S(2)}) copy-start(f32[1024,32]{0,1:T(8,128)S(1)} %get-tuple-element.122) | copy-start | bytes 393220
  445.2 37.2 %copy-start.28 = (bf16[512,2048]{1,0:T(8,128)(2,1)S(1)}, bf16[512,2048]{1,0:T(8,128)(2,1)}, u32[]{:S(2)}) copy-start(bf16[512,2048]{1,0:T(8,128)(2,1)} %get-tuple-element.69) | copy-start | bytes 6291460
  445.2 84.9 %copy-start.27 = (s32[8]{0:T(128)S(1)}, s32[8]{0:T(128)}, u32[]{:S(2)}) copy-start(s32[8]{0:T(128)} %param.11) | copy-start | bytes 100
  457.6 186.2 %copy-start.18 = (bf16[8,128,1024]{2,1,0:T(8,128)(2,1)S(1)}, bf16[8,128,1024]{2,1,0:T(8,128)(2,1)}, u32[]{:S(2)}) copy-start(bf16[8,128,1024]{2,1,0:T(8,128)(2,1)} %get-tuple-element.72) | copy-start | bytes 6291460
  457.6 186.2 %copy-start.20 = (f32[1024,32]{0,1:T(8,128)S(1)}, f32[1024,32]{0,1:T(8,128)}, u32[]{:S(2)}) copy-start(f32[1024,32]{0,1:T(8,128)} %copy-done.19) | copy-start | bytes 393220
  457.6 186.2 %copy-start.22 = (f32[1024,32]{0,1:T(8,128)S(1)}, f32[1024,32]{0,1:T(8,128)}, u32[]{:S(2)}) copy-start(f32[1024,32]{0,1:T(8,128)} %copy-done.21) | copy-start | bytes 393220
  457.6 23.8 %collective-permute-start.12 = (bf16[256,2048]{1,0:T(8,128)(2,1)}, bf16[256,2048]{1,0:T(8,128)(2,1)S(1)}, u32[]{:S(2)}, u32[]{:S(2)}) collective-permute-start(bf16[256,2048]{1,0:T(8,128)(2,1)} %get-tuple-element.77), channel_id=1, source_target_pairs={{0,8},{8,16},{16,24},{24,0},{1,9},{9,17},{17,25},{25,1},{2,10},{10... | collective-permute-start | bytes 3145736 | tf_op jit(solution)/shard_map/ppermute | solution.py:766
  459.0 23.4 %collective-permute-start.13 = (bf16[256,2048]{1,0:T(8,128)(2,1)}, bf16[256,2048]{1,0:T(8,128)(2,1)S(1)}, u32[]{:S(2)}, u32[]{:S(2)}) collective-permute-start(bf16[256,2048]{1,0:T(8,128)(2,1)} %get-tuple-element.77), channel_id=1, source_target_pairs={{0,24},{8,0},{16,8},{24,16},{1,25},{9,1},{17,9},{25,17},{2,26},{10... | collective-permute-start | bytes 3145736 | tf_op jit(solution)/shard_map/ppermute | solution.py:766
  460.4 43.6 %collective-permute-start.10 = (bf16[256,2048]{1,0:T(8,128)(2,1)}, bf16[256,2048]{1,0:T(8,128)(2,1)}, u32[]{:S(2)}, u32[]{:S(2)}) collective-permute-start(bf16[256,2048]{1,0:T(8,128)(2,1)} %get-tuple-element.71), channel_id=1, source_target_pairs={{0,8},{8,16},{16,24},{24,0},{1,9},{9,17},{17,25},{25,1},{2,10},{10... | collective-permute-start | bytes 3145736 | tf_op jit(solution)/shard_map/ppermute | solution.py:766
  460.7 43.6 %collective-permute-start.11 = (bf16[256,2048]{1,0:T(8,128)(2,1)}, bf16[256,2048]{1,0:T(8,128)(2,1)S(1)}, u32[]{:S(2)}, u32[]{:S(2)}) collective-permute-start(bf16[256,2048]{1,0:T(8,128)(2,1)} %get-tuple-element.71), channel_id=1, source_target_pairs={{0,24},{8,0},{16,8},{24,16},{1,25},{9,1},{17,9},{25,17},{2,26},{10... | collective-permute-start | bytes 3145736 | tf_op jit(solution)/shard_map/ppermute | solution.py:766
  463.1 63.4 %collective-permute-start.3 = (bf16[256,2048]{1,0:T(8,128)(2,1)}, bf16[256,2048]{1,0:T(8,128)(2,1)S(1)}, u32[]{:S(2)}, u32[]{:S(2)}) collective-permute-start(bf16[256,2048]{1,0:T(8,128)(2,1)} %get-tuple-element.68), channel_id=1, source_target_pairs={{0,24},{8,0},{16,8},{24,16},{1,25},{9,1},{17,9},{25,17},{2,26},{10... | collective-permute-start | bytes 3145736 | tf_op jit(solution)/shard_map/ppermute | solution.py:766
  481.4 1.0 copy-start.2
  482.4 45.2 %collective-permute-start.2 = (bf16[256,2048]{1,0:T(8,128)(2,1)}, bf16[256,2048]{1,0:T(8,128)(2,1)S(1)}, u32[]{:S(2)}, u32[]{:S(2)}) collective-permute-start(bf16[256,2048]{1,0:T(8,128)(2,1)} %get-tuple-element.68), channel_id=1, source_target_pairs={{0,8},{8,16},{16,24},{24,0},{1,9},{9,17},{17,25},{25,1},{2,10},{10... | collective-permute-start | bytes 3145736 | tf_op jit(solution)/shard_map/ppermute | solution.py:766
  482.4 158.7 %collective-permute-start.4 = (bf16[512,2048]{1,0:T(8,128)(2,1)S(1)}, bf16[512,2048]{1,0:T(8,128)(2,1)}, u32[]{:S(2)}, u32[]{:S(2)}) collective-permute-start(bf16[512,2048]{1,0:T(8,128)(2,1)S(1)} %copy-done.28), channel_id=1, source_target_pairs={{0,8},{8,16},{16,24},{24,0},{1,9},{9,17},{17,25},{25,1},{2,10},{10... | collective-permute-start | bytes 6291464 | tf_op jit(solution)/shard_map/ppermute | solution.py:766
  504.0 137.1 %collective-permute-start.9 = (bf16[512,2048]{1,0:T(8,128)(2,1)}, bf16[512,2048]{1,0:T(8,128)(2,1)S(1)}, u32[]{:S(2)}, u32[]{:S(2)}) collective-permute-start(bf16[512,2048]{1,0:T(8,128)(2,1)} %get-tuple-element.70), channel_id=1, source_target_pairs={{0,24},{8,0},{16,8},{24,16},{1,25},{9,1},{17,9},{25,17},{2,26},{10... | collective-permute-start | bytes 6291464 | tf_op jit(solution)/shard_map/ppermute | solution.py:766
  504.2 1.0 copy-start.4
  505.2 138.9 %collective-permute-start.5 = (bf16[512,2048]{1,0:T(8,128)(2,1)S(1)}, bf16[512,2048]{1,0:T(8,128)(2,1)S(1)}, u32[]{:S(2)}, u32[]{:S(2)}) collective-permute-start(bf16[512,2048]{1,0:T(8,128)(2,1)S(1)} %copy-done.28), channel_id=1, source_target_pairs={{0,24},{8,0},{16,8},{24,16},{1,25},{9,1},{17,9},{25,17},{2,26},{10... | collective-permute-start | bytes 6291464 | tf_op jit(solution)/shard_map/ppermute | solution.py:766
  526.4 117.7 %copy-start.6 = (bf16[256,2048]{1,0:T(8,128)(2,1)}, bf16[256,2048]{1,0:T(8,128)(2,1)S(1)}, u32[]{:S(2)}) copy-start(bf16[256,2048]{1,0:T(8,128)(2,1)S(1)} %collective-permute-done.3.refs_3_) | copy-start | bytes 3145732
  526.4 67.3 %collective-permute-start = (bf16[256,2048]{1,0:T(8,128)(2,1)}, bf16[256,2048]{1,0:T(8,128)(2,1)S(1)}, u32[]{:S(2)}, u32[]{:S(2)}) collective-permute-start(bf16[256,2048]{1,0:T(8,128)(2,1)} %get-tuple-element.67), channel_id=1, source_target_pairs={{0,8},{8,16},{16,24},{24,0},{1,9},{9,17},{17,25},{25,1},{2,10},{10... | collective-permute-start | bytes 3145736 | tf_op jit(solution)/shard_map/ppermute | solution.py:766
  527.6 1.0 copy-start.8
  528.6 110.3 %collective-permute-start.1 = (bf16[256,2048]{1,0:T(8,128)(2,1)}, bf16[256,2048]{1,0:T(8,128)(2,1)S(1)}, u32[]{:S(2)}, u32[]{:S(2)}) collective-permute-start(bf16[256,2048]{1,0:T(8,128)(2,1)} %get-tuple-element.67), channel_id=1, source_target_pairs={{0,24},{8,0},{16,8},{24,16},{1,25},{9,1},{17,9},{25,17},{2,26},{10... | collective-permute-start | bytes 3145736 | tf_op jit(solution)/shard_map/ppermute | solution.py:766
  530.2 115.3 %copy-start.23 = (bf16[8,1024,1,64]{1,3,2,0:T(8,128)(2,1)S(1)}, bf16[8,1024,1,64]{1,3,2,0:T(8,128)(2,1)}, u32[]{:S(2)}) copy-start(bf16[8,1024,1,64]{1,3,2,0:T(8,128)(2,1)} %param.13) | copy-start | bytes 3145732
  530.2 115.3 %copy-start.24 = (bf16[8,1024,1,64]{1,3,2,0:T(8,128)(2,1)S(1)}, bf16[8,1024,1,64]{1,3,2,0:T(8,128)(2,1)}, u32[]{:S(2)}) copy-start(bf16[8,1024,1,64]{1,3,2,0:T(8,128)(2,1)} %param.12) | copy-start | bytes 3145732
  593.8 55.6 %copy-start.10 = (bf16[256,2048]{1,0:T(8,128)(2,1)}, bf16[256,2048]{1,0:T(8,128)(2,1)S(1)}, u32[]{:S(2)}) copy-start(bf16[256,2048]{1,0:T(8,128)(2,1)S(1)} %collective-permute-done.refs_0_) | copy-start | bytes 3145732
  593.8 134.1 %collective-permute-start.8 = (bf16[512,2048]{1,0:T(8,128)(2,1)}, bf16[512,2048]{1,0:T(8,128)(2,1)}, u32[]{:S(2)}, u32[]{:S(2)}) collective-permute-start(bf16[512,2048]{1,0:T(8,128)(2,1)} %get-tuple-element.70), channel_id=1, source_target_pairs={{0,8},{8,16},{16,24},{24,0},{1,9},{9,17},{17,25},{25,1},{2,10},{10... | collective-permute-start | bytes 6291464 | tf_op jit(solution)/shard_map/ppermute | solution.py:766
  638.9 10.5 %copy-start.12 = (bf16[256,2048]{1,0:T(8,128)(2,1)}, bf16[256,2048]{1,0:T(8,128)(2,1)S(1)}, u32[]{:S(2)}) copy-start(bf16[256,2048]{1,0:T(8,128)(2,1)S(1)} %collective-permute-done.1.refs_1_) | copy-start | bytes 3145732
  638.9 21.7 %collective-permute-start.7 = (bf16[256,2048]{1,0:T(8,128)(2,1)S(1)}, bf16[256,2048]{1,0:T(8,128)(2,1)S(1)}, u32[]{:S(2)}, u32[]{:S(2)}) collective-permute-start(bf16[256,2048]{1,0:T(8,128)(2,1)S(1)} %collective-permute-done.3.refs_3_), channel_id=1, source_target_pairs={{0,24},{8,0},{16,8},{24,16},{1,25},{9,1},{17,9},{25,17},{2,26},{10... | collective-permute-start | bytes 3145736 | tf_op jit(solution)/shard_map/ppermute | solution.py:792
  641.1 86.8 %collective-permute-start.14 = (bf16[512,2048]{1,0:T(8,128)(2,1)}, bf16[512,2048]{1,0:T(8,128)(2,1)}, u32[]{:S(2)}, u32[]{:S(2)}) collective-permute-start(bf16[512,2048]{1,0:T(8,128)(2,1)} %collective-permute-done.4.refs_4_), channel_id=1, source_target_pairs={{0,8},{8,16},{16,24},{24,0},{1,9},{9,17},{17,25},{25,1},{2,10},{10... | collective-permute-start | bytes 6291464 | tf_op jit(solution)/shard_map/ppermute | solution.py:790
  641.1 92.1 %collective-permute-start.15 = (bf16[512,2048]{1,0:T(8,128)(2,1)S(1)}, bf16[512,2048]{1,0:T(8,128)(2,1)}, u32[]{:S(2)}, u32[]{:S(2)}) collective-permute-start(bf16[512,2048]{1,0:T(8,128)(2,1)S(1)} %collective-permute-done.9.refs_1_), channel_id=1, source_target_pairs={{0,24},{8,0},{16,8},{24,16},{1,25},{9,1},{17,9},{25,17},{2,26},{10... | collective-permute-start | bytes 6291464 | tf_op jit(solution)/shard_map/ppermute | solution.py:792
  644.2 1.3 copy-start
  645.5 62.8 %collective-permute-start.6 = (bf16[256,2048]{1,0:T(8,128)(2,1)S(1)}, bf16[256,2048]{1,0:T(8,128)(2,1)S(1)}, u32[]{:S(2)}, u32[]{:S(2)}) collective-permute-start(bf16[256,2048]{1,0:T(8,128)(2,1)S(1)} %collective-permute-done.refs_0_), channel_id=1, source_target_pairs={{0,8},{8,16},{16,24},{24,0},{1,9},{9,17},{17,25},{25,1},{2,10},{10... | collective-permute-start | bytes 3145736 | tf_op jit(solution)/shard_map/ppermute | solution.py:790
  660.6 1.0 copy-start.14
  661.6 74.3 %collective-permute-start.16 = (bf16[256,2048]{1,0:T(8,128)(2,1)}, bf16[256,2048]{1,0:T(8,128)(2,1)}, u32[]{:S(2)}, u32[]{:S(2)}) collective-permute-start(bf16[256,2048]{1,0:T(8,128)(2,1)} %collective-permute-done.10.refs_2_), channel_id=1, source_target_pairs={{0,8},{8,16},{16,24},{24,0},{1,9},{9,17},{17,25},{25,1},{2,10},{10... | collective-permute-start | bytes 3145736 | tf_op jit(solution)/shard_map/ppermute | solution.py:790
  708.3 1.0 copy-start.16
  709.3 28.7 %collective-permute-start.17 = (bf16[256,2048]{1,0:T(8,128)(2,1)S(1)}, bf16[256,2048]{1,0:T(8,128)(2,1)}, u32[]{:S(2)}, u32[]{:S(2)}) collective-permute-start(bf16[256,2048]{1,0:T(8,128)(2,1)S(1)} %collective-permute-done.13.refs_5_), channel_id=1, source_target_pairs={{0,24},{8,0},{16,8},{24,16},{1,25},{9,1},{17,9},{25,17},{2,26},{10... | collective-permute-start | bytes 3145736 | tf_op jit(solution)/shard_map/ppermute | solution.py:792
  713.3 1.6 copy-start.1
  714.8 1.2 copy-start.7
  716.1 1.2 copy-start.9
  717.3 1.2 copy-start.11
  718.5 1.2 copy-start.13
  719.7 1.2 copy-start.15
  721.0 1.2 copy-start.17
  722.2 5.7 copy-start.3
  722.2 5.7 copy-start.5
  (1 other events, 0.7 us)
Sparse Core Ops, SparseCore 0:
  85.9 144.7 all-gather.2
  232.7 81.0 all-gather.4
